TPU v7x, 256 devices: a whole 4x4x8 slice. The times are simulated.
256 devices in a mesh: section: 8 (over y, core), gx: 8 (over z), gy: 4 (over x).
Axes of the slice: x: 4, y: 4, z: 8, core: 2. Of those that a mesh axis runs over, the one named last changes fastest.
Arguments:
- load_index: int32 [8], P('section'), may hold values from 0 to 63
- load_table: float32 [64, 3], replicated, may hold values from -4 to 4
- toughness: float32 [8, 128, 64, 128], P('section', 'gx', 'gy'), may hold values from 0.3 to 3
- clamp_mask: int32 [128, 64, 128], P('gx', 'gy'), may hold values 0 or 1
- load_mask: int32 [128, 64, 128], P('gx', 'gy'), may hold values 0 or 1
- crack_mask: int32 [128, 64, 128], P('gx', 'gy'), may hold values 0 or 1
Outputs:
- displacement: float32 [8, 3, 128, 64, 128], P('section', None, 'gx', 'gy')
- damage: float32 [8, 128, 64, 128], P('section', 'gx', 'gy')
- section_residuals: float32 [8, 8], P('section')
All inputs are finite; a program needn't handle non-finite values. No bound on the sum of `clamp_mask` or of `load_mask` or of `crack_mask` on one device may be relied on, other than what follows from the above.
Results may differ from a plain program's by a relative error of at most 0.0003.
Values sent between devices are 32-bit elements; how exact they have to be, the bound alone decides.
No kernel may reach another device: no remote copies, remote signals or barrier semaphores. Data moves between devices by JAX's collectives and lax.ppermute only.
A program may use at most 64 MiB of HBM per device.

v0:
```python
import jax
import jax.numpy as jnp
from jax import lax
from jax.sharding import PartitionSpec as P

lame_lambda = 1.0
shear_modulus = 1.0
relax_weight = 0.6
stiff_floor = 0.001
eigen_guard = 1e-08
neighbour_offsets = ((1, 0, 0), (-1, 0, 0), (0, 1, 0), (0, -1, 0), (0, 0, 1), (0, 0, -1))


def padded_2(block, sides, width):
    for axis, dim in sides:
        count = lax.axis_size(axis)
        forward = [(i, i + 1) for i in range(count - 1)]
        backward = [(target, source) for source, target in forward]
        low = lax.ppermute(
            lax.slice_in_dim(block, block.shape[dim] - width, None, axis=dim), axis, forward
        )
        high = lax.ppermute(lax.slice_in_dim(block, 0, width, axis=dim), axis, backward)
        block = jnp.concatenate([low, block, high], axis=dim)
    return block


def laid_out(blocks, dim):
    shape = list(blocks.shape[1:])
    shape[dim] *= blocks.shape[0]
    return jnp.moveaxis(blocks, 0, dim).reshape(shape)


def copy_for_each(x, axis):
    length = lax.axis_size(axis)
    return lax.all_to_all(jnp.broadcast_to(x[None], (length, *x.shape)), axis, 0, 0, tiled=True)


def gather_directly(x, axis, dim):
    return laid_out(copy_for_each(x, axis), dim)


def taken_together(x, axis):
    everything = copy_for_each(x, axis)
    return jnp.sum(everything, axis=0)


def unit_offset(axis_index, sign):
    return tuple((sign if other == axis_index else 0 for other in range(3)))


def shifted(padded, offset):
    span_first = padded.shape[-3] - 2
    span_second = padded.shape[-2] - 2
    span_third = padded.shape[-1] - 2
    return padded[
        ...,
        1 + offset[0] : 1 + offset[0] + span_first,
        1 + offset[1] : 1 + offset[1] + span_second,
        1 + offset[2] : 1 + offset[2] + span_third,
    ]


def component(field, index):
    return field[..., index, :, :, :]


def elastic_parts(moved_pad, damage_pad):
    stiff_pad = jnp.square(1.0 - damage_pad) + stiff_floor
    centre = shifted(stiff_pad, (0, 0, 0))
    current = shifted(moved_pad, (0, 0, 0))
    laplace = jnp.zeros_like(current)
    weights = jnp.zeros_like(centre)
    for offset in neighbour_offsets:
        face = 0.5 * (centre + shifted(stiff_pad, offset))
        weights = weights + face
        laplace = laplace + jnp.expand_dims(face, -4) * (shifted(moved_pad, offset) - current)
    divergence = jnp.zeros_like(centre)
    pairs = []
    for axis_index in range(3):
        forward = unit_offset(axis_index, 1)
        backward = unit_offset(axis_index, -1)
        part = component(moved_pad, axis_index)
        divergence = divergence + 0.5 * (shifted(part, forward) - shifted(part, backward))
        pairs.append(shifted(stiff_pad, forward) + shifted(stiff_pad, backward))
    flow = centre * divergence
    diagonal = shear_modulus * jnp.expand_dims(weights, -4) + 0.25 * (
        lame_lambda + shear_modulus
    ) * jnp.stack(pairs, axis=-4)
    return (current, laplace, flow, diagonal)


def flow_gradient(flow_pad):
    parts = [
        0.5
        * (
            shifted(flow_pad, unit_offset(axis_index, 1))
            - shifted(flow_pad, unit_offset(axis_index, -1))
        )
        for axis_index in range(3)
    ]
    return jnp.stack(parts, axis=-4)


def spectral_energy(strain_xx, strain_yy, strain_zz, strain_xy, strain_xz, strain_yz):
    middle_value = (strain_xx + strain_yy + strain_zz) / 3.0
    dev_xx = strain_xx - middle_value
    dev_yy = strain_yy - middle_value
    dev_zz = strain_zz - middle_value
    shear_sum = jnp.square(strain_xy) + jnp.square(strain_xz) + jnp.square(strain_yz)
    spread = jnp.square(dev_xx) + jnp.square(dev_yy) + jnp.square(dev_zz) + 2.0 * shear_sum
    radius = jnp.sqrt(spread / 6.0)
    guarded = spread / 6.0 + eigen_guard
    determinant = (
        dev_xx * (dev_yy * dev_zz - jnp.square(strain_yz))
        - strain_xy * (strain_xy * dev_zz - strain_yz * strain_xz)
        + strain_xz * (strain_xy * strain_yz - dev_yy * strain_xz)
    )
    ratio = jnp.clip(determinant / (2.0 * guarded * jnp.sqrt(guarded)), -1.0, 1.0)
    angle = jnp.arccos(ratio) / 3.0
    largest = middle_value + 2.0 * radius * jnp.cos(angle)
    smallest = middle_value + 2.0 * radius * jnp.cos(angle + 2.0 * jnp.pi / 3.0)
    between = 3.0 * middle_value - largest - smallest
    positive = (
        jnp.square(jax.nn.relu(largest))
        + jnp.square(jax.nn.relu(between))
        + jnp.square(jax.nn.relu(smallest))
    )
    return (
        0.5 * lame_lambda * jnp.square(jax.nn.relu(3.0 * middle_value)) + shear_modulus * positive
    )


def damage_update(moved_pad, damage_pad, toughness_cell, crack_cell):
    grads = [
        [
            0.5
            * (
                shifted(component(moved_pad, first), unit_offset(second, 1))
                - shifted(component(moved_pad, first), unit_offset(second, -1))
            )
            for second in range(3)
        ]
        for first in range(3)
    ]
    energy = spectral_energy(
        grads[0][0],
        grads[1][1],
        grads[2][2],
        0.5 * (grads[0][1] + grads[1][0]),
        0.5 * (grads[0][2] + grads[2][0]),
        0.5 * (grads[1][2] + grads[2][1]),
    )
    beside_all = jnp.zeros_like(energy)
    for offset in neighbour_offsets:
        beside_all = beside_all + shifted(damage_pad, offset)
    updated = (2.0 * energy + toughness_cell * beside_all) / (
        toughness_cell + 2.0 * energy + 6.0 * toughness_cell
    )
    return jnp.where(crack_cell > 0.5, 1.0, updated)


def pad_depth(field):
    return jnp.pad(field, [(0, 0)] * (field.ndim - 1) + [(1, 1)])


def cropped(field, margin):
    return field[..., margin : field.shape[-3] - margin, margin : field.shape[-2] - margin, :]


def on_device(load_index, load_table, toughness, clamp_mask, load_mask, crack_mask):
    sections = lax.axis_size("section")
    clamp = clamp_mask.astype(jnp.float32)
    load = load_mask.astype(jnp.float32)
    crack = crack_mask.astype(jnp.float32)
    fixed = jnp.maximum(clamp, load)
    free = 1.0 - fixed
    cells = float(clamp.size * lax.axis_size("gx") * lax.axis_size("gy"))
    picker = (
        load_index[:, None] == jnp.arange(load_table.shape[0], dtype=jnp.int32)[None, :]
    ).astype(jnp.float32)
    load_vectors = jnp.dot(
        picker, load_table, precision=lax.Precision.HIGHEST, preferred_element_type=jnp.float32
    )
    columns = jnp.arange(sections, dtype=jnp.int32)
    rims = padded_2(jnp.stack([clamp, load, jnp.ones_like(clamp)]), (("gx", 1), ("gy", 2)), 2)
    inside_wide = rims[2]
    rims_near = cropped(rims, 1)
    fixed_near = jnp.maximum(jnp.maximum(rims_near[0], rims_near[1]), 1.0 - rims_near[2])
    load_near = rims_near[1]

    def sweep(state, vectors, field):
        padded = pad_depth(padded_2(state, (("gx", 2), ("gy", 3)), 3))
        current, laplace, flow, diagonal = elastic_parts(padded[:, :3], padded[:, 3])
        flow = flow * inside_wide
        gradient = flow_gradient(pad_depth(flow))
        residual = shear_modulus * cropped(laplace, 1) + (lame_lambda + shear_modulus) * gradient
        relaxed = cropped(current, 1) + relax_weight * residual / cropped(diagonal, 1)
        prescribed = load_near[None, None] * vectors[:, :, None, None, None]
        moved_wide = jnp.where(fixed_near[None, None] > 0.5, prescribed, relaxed)
        new_damage = damage_update(pad_depth(moved_wide), cropped(padded[:, 3], 2), field, crack)
        new_moved = cropped(moved_wide, 1)
        residual_inner = cropped(residual, 1)
        squares = jnp.sum(free[None, None] * jnp.square(residual_inner), axis=(1, 2, 3, 4))
        return (jnp.concatenate([new_moved, new_damage[:, None]], axis=1), squares)

    start_moved = load[None, None] * load_vectors[:, :, None, None, None]
    start_state = jnp.concatenate(
        [start_moved, jnp.broadcast_to(crack, (load_vectors.shape[0], 1) + crack.shape)], axis=1
    )
    start_table = jnp.zeros((load_vectors.shape[0], sections), jnp.float32)
    gathered = gather_directly(toughness, "section", 0)
    home = lax.axis_index("section")

    def advance_home(round_index, carry):
        state, table = carry
        column = (home + round_index) % sections
        field = lax.dynamic_index_in_dim(gathered, column, 0, keepdims=False)
        state, squares = sweep(state, load_vectors, field)
        table = table + (columns == column).astype(jnp.float32)[None, :] * squares[:, None]
        return (state, table)

    final_state, table = lax.fori_loop(0, sections, advance_home, (start_state, start_table))
    table = jnp.sqrt(taken_together(table, ("gx", "gy")) / (3.0 * cells))
    return (final_state[:, :3], final_state[:, 3], table)


def solution(mesh):
    in_specs = (
        P("section"),
        P(),
        P("section", "gx", "gy", None),
        P("gx", "gy", None),
        P("gx", "gy", None),
        P("gx", "gy", None),
    )
    out_specs = (
        P("section", None, "gx", "gy", None),
        P("section", "gx", "gy", None),
        P("section", None),
    )
    return jax.shard_map(
        on_device, mesh=mesh, in_specs=in_specs, out_specs=out_specs, check_vma=False
    )
```

profile of v0, /device:TPU:2, one launch (start us, length us, event | category | flops | bytes accessed | tf_op | source)
XLA Modules:
  0.0 272.7 jit_solution(12507520927510009659)
XLA Ops:
  2.6 3.8 %collective-permute-start.4 = (f32[3,2,16,128]{3,2,1,0:T(8,128)S(1)}, f32[3,2,16,128]{3,2,1,0:T(8,128)S(1)}, u32[]{:S(2)}, u32[]{:S(2)}) collective-permute-start(f32[3,2,16,128]{3,2,1,0:T(8,128)S(1)} %get-tuple-element.433), channel_id=1, source_target_pairs={{0,4},{4,8},{8,12},{12,16},{16,20},{20,24},{24,28},{1,5},{5,9},{9,... | collective-permute-start | bytes 147464 | tf_op jit(solution)/shard_map/ppermute | solution.py:19
  8.8 4.6 %all-to-all-start = ((f32[8,1,16,16,128]{4,3,2,1,0:T(8,128)}), f32[8,1,16,16,128]{4,3,2,1,0:T(8,128)S(1)}, u32[]{:S(2)}, u32[]{:S(2)}) async-start(f32[8,1,16,16,128]{4,3,2,1,0:T(8,128)} %broadcast_in_dim.113), calls=%async_computation | async-start | bytes 2097152 | tf_op jit(solution)/shard_map/all_to_all | solution.py:35
  14.5 3.4 %collective-permute-start.6 = (f32[3,20,2,128]{3,2,1,0:T(2,128)S(1)}, f32[3,20,2,128]{3,2,1,0:T(2,128)S(1)}, u32[]{:S(2)}, u32[]{:S(2)}) collective-permute-start(f32[3,20,2,128]{3,2,1,0:T(2,128)S(1)} %get-tuple-element.431), channel_id=1, source_target_pairs={{0,1},{1,2},{2,3},{4,5},{5,6},{6,7},{8,9},{9,10},{10,11},{12,13},{... | collective-permute-start | bytes 184328 | tf_op jit(solution)/shard_map/ppermute | solution.py:19
  17.9 2.4 collective-permute-start.7
  20.8 3.2 %collective-permute-done.7 = f32[3,20,2,128]{3,2,1,0:T(2,128)S(1)} collective-permute-done((f32[3,20,2,128]{3,2,1,0:T(2,128)S(1)}, f32[3,20,2,128]{3,2,1,0:T(2,128)S(1)}, u32[]{:S(2)}, u32[]{:S(2)}) %collective-permute-start.7) | collective-permute-done | bytes 61472 | tf_op jit(solution)/shard_map/ppermute | solution.py:22
  24.2 5.1 %all-to-all-done = f32[8,1,16,16,128]{4,3,2,1,0:T(8,128)S(1)} async-done(((f32[8,1,16,16,128]{4,3,2,1,0:T(8,128)}), f32[8,1,16,16,128]{4,3,2,1,0:T(8,128)S(1)}, u32[]{:S(2)}, u32[]{:S(2)}) %all-to-all-start) | async-done | bytes 1048608 | tf_op jit(solution)/shard_map/all_to_all | solution.py:35
  29.4 225.6 %while.19 = (s32[]{:T(128)}, f32[1,4,16,16,128]{4,3,2,1,0:T(8,128)S(1)}, f32[1,8]{1,0:T(1,128)S(1)}, f32[18,18,128]{2,1,0:T(8,128)S(1)}, f32[1,18,18,128]{3,2,1,...) while((s32[]{:T(128)}, ...), condition=%wide.region_2.3_spmd.clone, body=%wide.region_0.2_spmd.clone.sunk | while | flops 9979785 | bytes 42991660 | solution.py:222
  29.4 4.6 %collective-permute-start = (f32[1,4,3,16,128]{4,3,2,1,0:T(8,128)S(1)}, f32[1,4,3,16,128]{4,3,2,1,0:T(8,128)S(1)}, u32[]{:S(2)}, u32[]{:S(2)}) collective-permute-start(f32[1,4,3,16,128]{4,3,2,1,0:T(8,128)S(1)} %get-tuple-element.540), channel_id=1, source_target_pairs={{0,4},{4,8},{8,12},{12,16},{16,20},{20,24},{24,28},{1,5},{5,9},{9,... | collective-permute-start | bytes 294920 | tf_op jit(solution)/shard_map/while/body/eval_jaxpr/ppermute | solution.py:19
  36.2 4.3 %collective-permute-done.1 = f32[1,4,3,16,128]{4,3,2,1,0:T(8,128)S(1)} collective-permute-done((f32[1,4,3,16,128]{4,3,2,1,0:T(8,128)S(1)}, f32[1,4,3,16,128]{4,3,2,1,0:T(8,128)S(1)}, u32[]{:S(2)}, u32[]{:S(2)}) %collective-permute-start.1) | collective-permute-done | bytes 98336 | tf_op jit(solution)/shard_map/while/body/eval_jaxpr/ppermute | solution.py:22
  40.5 2.4 collective-permute-start.2
  43.0 3.4 %collective-permute-start.3 = (f32[1,4,22,3,128]{4,3,2,1,0:T(4,128)S(1)}, f32[1,4,22,3,128]{4,3,2,1,0:T(4,128)S(1)}, u32[]{:S(2)}, u32[]{:S(2)}) collective-permute-start(f32[1,4,22,3,128]{4,3,2,1,0:T(4,128)S(1)} %get-tuple-element.543), channel_id=1, source_target_pairs={{0,1},{1,2},{2,3},{4,5},{5,6},{6,7},{8,9},{9,10},{10,11},{12,13},{... | collective-permute-start | bytes 405512 | tf_op jit(solution)/shard_map/while/body/eval_jaxpr/ppermute | solution.py:19
  47.9 2.5 collective-permute-done.3
  55.1 2.1 fusion.92
  58.6 4.8 %collective-permute-start = (f32[1,4,3,16,128]{4,3,2,1,0:T(8,128)S(1)}, f32[1,4,3,16,128]{4,3,2,1,0:T(8,128)S(1)}, u32[]{:S(2)}, u32[]{:S(2)}) collective-permute-start(f32[1,4,3,16,128]{4,3,2,1,0:T(8,128)S(1)} %get-tuple-element.540), channel_id=1, source_target_pairs={{0,4},{4,8},{8,12},{12,16},{16,20},{20,24},{24,28},{1,5},{5,9},{9,... | collective-permute-start | bytes 294920 | tf_op jit(solution)/shard_map/while/body/eval_jaxpr/ppermute | solution.py:19
  65.7 5.5 %collective-permute-done.1 = f32[1,4,3,16,128]{4,3,2,1,0:T(8,128)S(1)} collective-permute-done((f32[1,4,3,16,128]{4,3,2,1,0:T(8,128)S(1)}, f32[1,4,3,16,128]{4,3,2,1,0:T(8,128)S(1)}, u32[]{:S(2)}, u32[]{:S(2)}) %collective-permute-start.1) | collective-permute-done | bytes 98336 | tf_op jit(solution)/shard_map/while/body/eval_jaxpr/ppermute | solution.py:22
  73.2 3.9 %collective-permute-start.3 = (f32[1,4,22,3,128]{4,3,2,1,0:T(4,128)S(1)}, f32[1,4,22,3,128]{4,3,2,1,0:T(4,128)S(1)}, u32[]{:S(2)}, u32[]{:S(2)}) collective-permute-start(f32[1,4,22,3,128]{4,3,2,1,0:T(4,128)S(1)} %get-tuple-element.543), channel_id=1, source_target_pairs={{0,1},{1,2},{2,3},{4,5},{5,6},{6,7},{8,9},{9,10},{10,11},{12,13},{... | collective-permute-start | bytes 405512 | tf_op jit(solution)/shard_map/while/body/eval_jaxpr/ppermute | solution.py:19
  78.6 1.9 collective-permute-done.3
  85.2 2.1 fusion.92
  88.7 5.1 %collective-permute-start = (f32[1,4,3,16,128]{4,3,2,1,0:T(8,128)S(1)}, f32[1,4,3,16,128]{4,3,2,1,0:T(8,128)S(1)}, u32[]{:S(2)}, u32[]{:S(2)}) collective-permute-start(f32[1,4,3,16,128]{4,3,2,1,0:T(8,128)S(1)} %get-tuple-element.540), channel_id=1, source_target_pairs={{0,4},{4,8},{8,12},{12,16},{16,20},{20,24},{24,28},{1,5},{5,9},{9,... | collective-permute-start | bytes 294920 | tf_op jit(solution)/shard_map/while/body/eval_jaxpr/ppermute | solution.py:19
  96.1 4.3 %collective-permute-done.1 = f32[1,4,3,16,128]{4,3,2,1,0:T(8,128)S(1)} collective-permute-done((f32[1,4,3,16,128]{4,3,2,1,0:T(8,128)S(1)}, f32[1,4,3,16,128]{4,3,2,1,0:T(8,128)S(1)}, u32[]{:S(2)}, u32[]{:S(2)}) %collective-permute-start.1) | collective-permute-done | bytes 98336 | tf_op jit(solution)/shard_map/while/body/eval_jaxpr/ppermute | solution.py:22
  102.4 3.9 %collective-permute-start.3 = (f32[1,4,22,3,128]{4,3,2,1,0:T(4,128)S(1)}, f32[1,4,22,3,128]{4,3,2,1,0:T(4,128)S(1)}, u32[]{:S(2)}, u32[]{:S(2)}) collective-permute-start(f32[1,4,22,3,128]{4,3,2,1,0:T(4,128)S(1)} %get-tuple-element.543), channel_id=1, source_target_pairs={{0,1},{1,2},{2,3},{4,5},{5,6},{6,7},{8,9},{9,10},{10,11},{12,13},{... | collective-permute-start | bytes 405512 | tf_op jit(solution)/shard_map/while/body/eval_jaxpr/ppermute | solution.py:19
  107.9 1.9 collective-permute-done.3
  114.5 2.1 fusion.92
  118.0 3.9 %collective-permute-start = (f32[1,4,3,16,128]{4,3,2,1,0:T(8,128)S(1)}, f32[1,4,3,16,128]{4,3,2,1,0:T(8,128)S(1)}, u32[]{:S(2)}, u32[]{:S(2)}) collective-permute-start(f32[1,4,3,16,128]{4,3,2,1,0:T(8,128)S(1)} %get-tuple-element.540), channel_id=1, source_target_pairs={{0,4},{4,8},{8,12},{12,16},{16,20},{20,24},{24,28},{1,5},{5,9},{9,... | collective-permute-start | bytes 294920 | tf_op jit(solution)/shard_map/while/body/eval_jaxpr/ppermute | solution.py:19
  124.1 4.3 %collective-permute-done.1 = f32[1,4,3,16,128]{4,3,2,1,0:T(8,128)S(1)} collective-permute-done((f32[1,4,3,16,128]{4,3,2,1,0:T(8,128)S(1)}, f32[1,4,3,16,128]{4,3,2,1,0:T(8,128)S(1)}, u32[]{:S(2)}, u32[]{:S(2)}) %collective-permute-start.1) | collective-permute-done | bytes 98336 | tf_op jit(solution)/shard_map/while/body/eval_jaxpr/ppermute | solution.py:22
  130.4 3.9 %collective-permute-start.3 = (f32[1,4,22,3,128]{4,3,2,1,0:T(4,128)S(1)}, f32[1,4,22,3,128]{4,3,2,1,0:T(4,128)S(1)}, u32[]{:S(2)}, u32[]{:S(2)}) collective-permute-start(f32[1,4,22,3,128]{4,3,2,1,0:T(4,128)S(1)} %get-tuple-element.543), channel_id=1, source_target_pairs={{0,1},{1,2},{2,3},{4,5},{5,6},{6,7},{8,9},{9,10},{10,11},{12,13},{... | collective-permute-start | bytes 405512 | tf_op jit(solution)/shard_map/while/body/eval_jaxpr/ppermute | solution.py:19
  135.9 1.9 collective-permute-done.3
  142.5 2.1 fusion.92
  146.0 3.1 %collective-permute-start = (f32[1,4,3,16,128]{4,3,2,1,0:T(8,128)S(1)}, f32[1,4,3,16,128]{4,3,2,1,0:T(8,128)S(1)}, u32[]{:S(2)}, u32[]{:S(2)}) collective-permute-start(f32[1,4,3,16,128]{4,3,2,1,0:T(8,128)S(1)} %get-tuple-element.540), channel_id=1, source_target_pairs={{0,4},{4,8},{8,12},{12,16},{16,20},{20,24},{24,28},{1,5},{5,9},{9,... | collective-permute-start | bytes 294920 | tf_op jit(solution)/shard_map/while/body/eval_jaxpr/ppermute | solution.py:19
  151.4 4.3 %collective-permute-done.1 = f32[1,4,3,16,128]{4,3,2,1,0:T(8,128)S(1)} collective-permute-done((f32[1,4,3,16,128]{4,3,2,1,0:T(8,128)S(1)}, f32[1,4,3,16,128]{4,3,2,1,0:T(8,128)S(1)}, u32[]{:S(2)}, u32[]{:S(2)}) %collective-permute-start.1) | collective-permute-done | bytes 98336 | tf_op jit(solution)/shard_map/while/body/eval_jaxpr/ppermute | solution.py:22
  157.7 3.9 %collective-permute-start.3 = (f32[1,4,22,3,128]{4,3,2,1,0:T(4,128)S(1)}, f32[1,4,22,3,128]{4,3,2,1,0:T(4,128)S(1)}, u32[]{:S(2)}, u32[]{:S(2)}) collective-permute-start(f32[1,4,22,3,128]{4,3,2,1,0:T(4,128)S(1)} %get-tuple-element.543), channel_id=1, source_target_pairs={{0,1},{1,2},{2,3},{4,5},{5,6},{6,7},{8,9},{9,10},{10,11},{12,13},{... | collective-permute-start | bytes 405512 | tf_op jit(solution)/shard_map/while/body/eval_jaxpr/ppermute | solution.py:19
  169.7 2.1 fusion.92
  173.2 3.1 %collective-permute-start = (f32[1,4,3,16,128]{4,3,2,1,0:T(8,128)S(1)}, f32[1,4,3,16,128]{4,3,2,1,0:T(8,128)S(1)}, u32[]{:S(2)}, u32[]{:S(2)}) collective-permute-start(f32[1,4,3,16,128]{4,3,2,1,0:T(8,128)S(1)} %get-tuple-element.540), channel_id=1, source_target_pairs={{0,4},{4,8},{8,12},{12,16},{16,20},{20,24},{24,28},{1,5},{5,9},{9,... | collective-permute-start | bytes 294920 | tf_op jit(solution)/shard_map/while/body/eval_jaxpr/ppermute | solution.py:19
  178.6 4.3 %collective-permute-done.1 = f32[1,4,3,16,128]{4,3,2,1,0:T(8,128)S(1)} collective-permute-done((f32[1,4,3,16,128]{4,3,2,1,0:T(8,128)S(1)}, f32[1,4,3,16,128]{4,3,2,1,0:T(8,128)S(1)}, u32[]{:S(2)}, u32[]{:S(2)}) %collective-permute-start.1) | collective-permute-done | bytes 98336 | tf_op jit(solution)/shard_map/while/body/eval_jaxpr/ppermute | solution.py:22
  184.9 3.9 %collective-permute-start.3 = (f32[1,4,22,3,128]{4,3,2,1,0:T(4,128)S(1)}, f32[1,4,22,3,128]{4,3,2,1,0:T(4,128)S(1)}, u32[]{:S(2)}, u32[]{:S(2)}) collective-permute-start(f32[1,4,22,3,128]{4,3,2,1,0:T(4,128)S(1)} %get-tuple-element.543), channel_id=1, source_target_pairs={{0,1},{1,2},{2,3},{4,5},{5,6},{6,7},{8,9},{9,10},{10,11},{12,13},{... | collective-permute-start | bytes 405512 | tf_op jit(solution)/shard_map/while/body/eval_jaxpr/ppermute | solution.py:19
  190.4 1.9 collective-permute-done.3
  197.0 2.1 fusion.92
  200.5 3.1 %collective-permute-start = (f32[1,4,3,16,128]{4,3,2,1,0:T(8,128)S(1)}, f32[1,4,3,16,128]{4,3,2,1,0:T(8,128)S(1)}, u32[]{:S(2)}, u32[]{:S(2)}) collective-permute-start(f32[1,4,3,16,128]{4,3,2,1,0:T(8,128)S(1)} %get-tuple-element.540), channel_id=1, source_target_pairs={{0,4},{4,8},{8,12},{12,16},{16,20},{20,24},{24,28},{1,5},{5,9},{9,... | collective-permute-start | bytes 294920 | tf_op jit(solution)/shard_map/while/body/eval_jaxpr/ppermute | solution.py:19
  205.8 4.3 %collective-permute-done.1 = f32[1,4,3,16,128]{4,3,2,1,0:T(8,128)S(1)} collective-permute-done((f32[1,4,3,16,128]{4,3,2,1,0:T(8,128)S(1)}, f32[1,4,3,16,128]{4,3,2,1,0:T(8,128)S(1)}, u32[]{:S(2)}, u32[]{:S(2)}) %collective-permute-start.1) | collective-permute-done | bytes 98336 | tf_op jit(solution)/shard_map/while/body/eval_jaxpr/ppermute | solution.py:22
  212.1 3.9 %collective-permute-start.3 = (f32[1,4,22,3,128]{4,3,2,1,0:T(4,128)S(1)}, f32[1,4,22,3,128]{4,3,2,1,0:T(4,128)S(1)}, u32[]{:S(2)}, u32[]{:S(2)}) collective-permute-start(f32[1,4,22,3,128]{4,3,2,1,0:T(4,128)S(1)} %get-tuple-element.543), channel_id=1, source_target_pairs={{0,1},{1,2},{2,3},{4,5},{5,6},{6,7},{8,9},{9,10},{10,11},{12,13},{... | collective-permute-start | bytes 405512 | tf_op jit(solution)/shard_map/while/body/eval_jaxpr/ppermute | solution.py:19
  224.2 2.1 fusion.92
  227.7 3.1 %collective-permute-start = (f32[1,4,3,16,128]{4,3,2,1,0:T(8,128)S(1)}, f32[1,4,3,16,128]{4,3,2,1,0:T(8,128)S(1)}, u32[]{:S(2)}, u32[]{:S(2)}) collective-permute-start(f32[1,4,3,16,128]{4,3,2,1,0:T(8,128)S(1)} %get-tuple-element.540), channel_id=1, source_target_pairs={{0,4},{4,8},{8,12},{12,16},{16,20},{20,24},{24,28},{1,5},{5,9},{9,... | collective-permute-start | bytes 294920 | tf_op jit(solution)/shard_map/while/body/eval_jaxpr/ppermute | solution.py:19
  233.1 4.3 %collective-permute-done.1 = f32[1,4,3,16,128]{4,3,2,1,0:T(8,128)S(1)} collective-permute-done((f32[1,4,3,16,128]{4,3,2,1,0:T(8,128)S(1)}, f32[1,4,3,16,128]{4,3,2,1,0:T(8,128)S(1)}, u32[]{:S(2)}, u32[]{:S(2)}) %collective-permute-start.1) | collective-permute-done | bytes 98336 | tf_op jit(solution)/shard_map/while/body/eval_jaxpr/ppermute | solution.py:22
  239.4 3.9 %collective-permute-start.3 = (f32[1,4,22,3,128]{4,3,2,1,0:T(4,128)S(1)}, f32[1,4,22,3,128]{4,3,2,1,0:T(4,128)S(1)}, u32[]{:S(2)}, u32[]{:S(2)}) collective-permute-start(f32[1,4,22,3,128]{4,3,2,1,0:T(4,128)S(1)} %get-tuple-element.543), channel_id=1, source_target_pairs={{0,1},{1,2},{2,3},{4,5},{5,6},{6,7},{8,9},{9,10},{10,11},{12,13},{... | collective-permute-start | bytes 405512 | tf_op jit(solution)/shard_map/while/body/eval_jaxpr/ppermute | solution.py:19
  244.8 1.9 collective-permute-done.3
  251.5 2.1 fusion.92
  255.5 8.0 %all-to-all-start.1 = ((f32[32,1,8]{2,1,0:T(1,128)}), f32[32,1,8]{2,1,0:T(1,128)S(1)}, u32[]{:S(2)}, u32[]{:S(2)}) async-start(f32[32,1,8]{2,1,0:T(1,128)} %broadcast_in_dim.115), calls=%async_computation.1 | async-start | bytes 32768 | tf_op jit(solution)/shard_map/all_to_all | solution.py:35
  265.0 7.1 %all-to-all-done.1 = f32[32,1,8]{2,1,0:T(1,128)S(1)} async-done(((f32[32,1,8]{2,1,0:T(1,128)}), f32[32,1,8]{2,1,0:T(1,128)S(1)}, u32[]{:S(2)}, u32[]{:S(2)}) %all-to-all-start.1) | async-done | bytes 1056 | tf_op jit(solution)/shard_map/all_to_all | solution.py:35
  (275 shorter events, 103.5 us)
Async XLA Ops:
  0.6 13.5 %copy-start = (f32[64,3]{0,1:T(4,128)S(1)}, f32[64,3]{0,1:T(4,128)}, u32[]{:S(2)}) copy-start(f32[64,3]{0,1:T(4,128)} %param.9) | copy-start | bytes 2308
  0.6 7.1 %copy-start.3 = (f32[1,16,16,128]{3,2,1,0:T(8,128)S(1)}, f32[1,16,16,128]{3,2,1,0:T(8,128)}, u32[]{:S(2)}) copy-start(f32[1,16,16,128]{3,2,1,0:T(8,128)} %param.10) | copy-start | bytes 393220
  2.6 11.8 %collective-permute-start.4 = (f32[3,2,16,128]{3,2,1,0:T(8,128)S(1)}, f32[3,2,16,128]{3,2,1,0:T(8,128)S(1)}, u32[]{:S(2)}, u32[]{:S(2)}) collective-permute-start(f32[3,2,16,128]{3,2,1,0:T(8,128)S(1)} %get-tuple-element.433), channel_id=1, source_target_pairs={{0,4},{4,8},{8,12},{12,16},{16,20},{20,24},{24,28},{1,5},{5,9},{9,... | collective-permute-start | bytes 147464 | tf_op jit(solution)/shard_map/ppermute | solution.py:19
  6.4 8.0 %collective-permute-start.5 = (f32[3,2,16,128]{3,2,1,0:T(8,128)S(1)}, f32[3,2,16,128]{3,2,1,0:T(8,128)S(1)}, u32[]{:S(2)}, u32[]{:S(2)}) collective-permute-start(f32[3,2,16,128]{3,2,1,0:T(8,128)S(1)} %get-tuple-element.434), channel_id=1, source_target_pairs={{4,0},{8,4},{12,8},{16,12},{20,16},{24,20},{28,24},{5,1},{9,5},{13... | collective-permute-start | bytes 147464 | tf_op jit(solution)/shard_map/ppermute | solution.py:22
  8.8 5.5 %copy-start.1 = (s32[16,16,128]{2,1,0:T(8,128)S(1)}, s32[16,16,128]{2,1,0:T(8,128)}, u32[]{:S(2)}) copy-start(s32[16,16,128]{2,1,0:T(8,128)} %param.12) | copy-start | bytes 393220
  8.8 5.5 %copy-start.2 = (s32[16,16,128]{2,1,0:T(8,128)S(1)}, s32[16,16,128]{2,1,0:T(8,128)}, u32[]{:S(2)}) copy-start(s32[16,16,128]{2,1,0:T(8,128)} %param.11) | copy-start | bytes 393220
  8.8 5.6 %copy-start.4 = (s32[16,16,128]{2,1,0:T(8,128)S(1)}, s32[16,16,128]{2,1,0:T(8,128)}, u32[]{:S(2)}) copy-start(s32[16,16,128]{2,1,0:T(8,128)} %param.13) | copy-start | bytes 393220
  8.8 20.5 %all-to-all-start = ((f32[8,1,16,16,128]{4,3,2,1,0:T(8,128)}), f32[8,1,16,16,128]{4,3,2,1,0:T(8,128)S(1)}, u32[]{:S(2)}, u32[]{:S(2)}) async-start(f32[8,1,16,16,128]{4,3,2,1,0:T(8,128)} %broadcast_in_dim.113), calls=%async_computation | async-start | bytes 2097152 | tf_op jit(solution)/shard_map/all_to_all | solution.py:35
  14.5 6.3 %collective-permute-start.6 = (f32[3,20,2,128]{3,2,1,0:T(2,128)S(1)}, f32[3,20,2,128]{3,2,1,0:T(2,128)S(1)}, u32[]{:S(2)}, u32[]{:S(2)}) collective-permute-start(f32[3,20,2,128]{3,2,1,0:T(2,128)S(1)} %get-tuple-element.431), channel_id=1, source_target_pairs={{0,1},{1,2},{2,3},{4,5},{5,6},{6,7},{8,9},{9,10},{10,11},{12,13},{... | collective-permute-start | bytes 184328 | tf_op jit(solution)/shard_map/ppermute | solution.py:19
  17.9 6.1 %collective-permute-start.7 = (f32[3,20,2,128]{3,2,1,0:T(2,128)S(1)}, f32[3,20,2,128]{3,2,1,0:T(2,128)S(1)}, u32[]{:S(2)}, u32[]{:S(2)}) collective-permute-start(f32[3,20,2,128]{3,2,1,0:T(2,128)S(1)} %get-tuple-element.432), channel_id=1, source_target_pairs={{1,0},{2,1},{3,2},{5,4},{6,5},{7,6},{9,8},{10,9},{11,10},{13,12},{... | collective-permute-start | bytes 184328 | tf_op jit(solution)/shard_map/ppermute | solution.py:22
  29.4 6.8 %collective-permute-start = (f32[1,4,3,16,128]{4,3,2,1,0:T(8,128)S(1)}, f32[1,4,3,16,128]{4,3,2,1,0:T(8,128)S(1)}, u32[]{:S(2)}, u32[]{:S(2)}) collective-permute-start(f32[1,4,3,16,128]{4,3,2,1,0:T(8,128)S(1)} %get-tuple-element.540), channel_id=1, source_target_pairs={{0,4},{4,8},{8,12},{12,16},{16,20},{20,24},{24,28},{1,5},{5,9},{9,... | collective-permute-start | bytes 294920 | tf_op jit(solution)/shard_map/while/body/eval_jaxpr/ppermute | solution.py:19
  33.9 6.5 %collective-permute-start.1 = (f32[1,4,3,16,128]{4,3,2,1,0:T(8,128)S(1)}, f32[1,4,3,16,128]{4,3,2,1,0:T(8,128)S(1)}, u32[]{:S(2)}, u32[]{:S(2)}) collective-permute-start(f32[1,4,3,16,128]{4,3,2,1,0:T(8,128)S(1)} %get-tuple-element.541), channel_id=1, source_target_pairs={{4,0},{8,4},{12,8},{16,12},{20,16},{24,20},{28,24},{5,1},{9,5},{13... | collective-permute-start | bytes 294920 | tf_op jit(solution)/shard_map/while/body/eval_jaxpr/ppermute | solution.py:22
  40.5 7.4 %collective-permute-start.2 = (f32[1,4,22,3,128]{4,3,2,1,0:T(4,128)S(1)}, f32[1,4,22,3,128]{4,3,2,1,0:T(4,128)S(1)}, u32[]{:S(2)}, u32[]{:S(2)}) collective-permute-start(f32[1,4,22,3,128]{4,3,2,1,0:T(4,128)S(1)} %get-tuple-element.542), channel_id=1, source_target_pairs={{1,0},{2,1},{3,2},{5,4},{6,5},{7,6},{9,8},{10,9},{11,10},{13,12},{... | collective-permute-start | bytes 405512 | tf_op jit(solution)/shard_map/while/body/eval_jaxpr/ppermute | solution.py:22
  43.0 7.4 %collective-permute-start.3 = (f32[1,4,22,3,128]{4,3,2,1,0:T(4,128)S(1)}, f32[1,4,22,3,128]{4,3,2,1,0:T(4,128)S(1)}, u32[]{:S(2)}, u32[]{:S(2)}) collective-permute-start(f32[1,4,22,3,128]{4,3,2,1,0:T(4,128)S(1)} %get-tuple-element.543), channel_id=1, source_target_pairs={{0,1},{1,2},{2,3},{4,5},{5,6},{6,7},{8,9},{9,10},{10,11},{12,13},{... | collective-permute-start | bytes 405512 | tf_op jit(solution)/shard_map/while/body/eval_jaxpr/ppermute | solution.py:19
  58.6 7.0 %collective-permute-start = (f32[1,4,3,16,128]{4,3,2,1,0:T(8,128)S(1)}, f32[1,4,3,16,128]{4,3,2,1,0:T(8,128)S(1)}, u32[]{:S(2)}, u32[]{:S(2)}) collective-permute-start(f32[1,4,3,16,128]{4,3,2,1,0:T(8,128)S(1)} %get-tuple-element.540), channel_id=1, source_target_pairs={{0,4},{4,8},{8,12},{12,16},{16,20},{20,24},{24,28},{1,5},{5,9},{9,... | collective-permute-start | bytes 294920 | tf_op jit(solution)/shard_map/while/body/eval_jaxpr/ppermute | solution.py:19
  63.4 7.7 %collective-permute-start.1 = (f32[1,4,3,16,128]{4,3,2,1,0:T(8,128)S(1)}, f32[1,4,3,16,128]{4,3,2,1,0:T(8,128)S(1)}, u32[]{:S(2)}, u32[]{:S(2)}) collective-permute-start(f32[1,4,3,16,128]{4,3,2,1,0:T(8,128)S(1)} %get-tuple-element.541), channel_id=1, source_target_pairs={{4,0},{8,4},{12,8},{16,12},{20,16},{24,20},{28,24},{5,1},{9,5},{13... | collective-permute-start | bytes 294920 | tf_op jit(solution)/shard_map/while/body/eval_jaxpr/ppermute | solution.py:22
  71.2 7.4 %collective-permute-start.2 = (f32[1,4,22,3,128]{4,3,2,1,0:T(4,128)S(1)}, f32[1,4,22,3,128]{4,3,2,1,0:T(4,128)S(1)}, u32[]{:S(2)}, u32[]{:S(2)}) collective-permute-start(f32[1,4,22,3,128]{4,3,2,1,0:T(4,128)S(1)} %get-tuple-element.542), channel_id=1, source_target_pairs={{1,0},{2,1},{3,2},{5,4},{6,5},{7,6},{9,8},{10,9},{11,10},{13,12},{... | collective-permute-start | bytes 405512 | tf_op jit(solution)/shard_map/while/body/eval_jaxpr/ppermute | solution.py:22
  73.2 7.4 %collective-permute-start.3 = (f32[1,4,22,3,128]{4,3,2,1,0:T(4,128)S(1)}, f32[1,4,22,3,128]{4,3,2,1,0:T(4,128)S(1)}, u32[]{:S(2)}, u32[]{:S(2)}) collective-permute-start(f32[1,4,22,3,128]{4,3,2,1,0:T(4,128)S(1)} %get-tuple-element.543), channel_id=1, source_target_pairs={{0,1},{1,2},{2,3},{4,5},{5,6},{6,7},{8,9},{9,10},{10,11},{12,13},{... | collective-permute-start | bytes 405512 | tf_op jit(solution)/shard_map/while/body/eval_jaxpr/ppermute | solution.py:19
  88.7 7.3 %collective-permute-start = (f32[1,4,3,16,128]{4,3,2,1,0:T(8,128)S(1)}, f32[1,4,3,16,128]{4,3,2,1,0:T(8,128)S(1)}, u32[]{:S(2)}, u32[]{:S(2)}) collective-permute-start(f32[1,4,3,16,128]{4,3,2,1,0:T(8,128)S(1)} %get-tuple-element.540), channel_id=1, source_target_pairs={{0,4},{4,8},{8,12},{12,16},{16,20},{20,24},{24,28},{1,5},{5,9},{9,... | collective-permute-start | bytes 294920 | tf_op jit(solution)/shard_map/while/body/eval_jaxpr/ppermute | solution.py:19
  93.9 6.5 %collective-permute-start.1 = (f32[1,4,3,16,128]{4,3,2,1,0:T(8,128)S(1)}, f32[1,4,3,16,128]{4,3,2,1,0:T(8,128)S(1)}, u32[]{:S(2)}, u32[]{:S(2)}) collective-permute-start(f32[1,4,3,16,128]{4,3,2,1,0:T(8,128)S(1)} %get-tuple-element.541), channel_id=1, source_target_pairs={{4,0},{8,4},{12,8},{16,12},{20,16},{24,20},{28,24},{5,1},{9,5},{13... | collective-permute-start | bytes 294920 | tf_op jit(solution)/shard_map/while/body/eval_jaxpr/ppermute | solution.py:22
  100.5 7.4 %collective-permute-start.2 = (f32[1,4,22,3,128]{4,3,2,1,0:T(4,128)S(1)}, f32[1,4,22,3,128]{4,3,2,1,0:T(4,128)S(1)}, u32[]{:S(2)}, u32[]{:S(2)}) collective-permute-start(f32[1,4,22,3,128]{4,3,2,1,0:T(4,128)S(1)} %get-tuple-element.542), channel_id=1, source_target_pairs={{1,0},{2,1},{3,2},{5,4},{6,5},{7,6},{9,8},{10,9},{11,10},{13,12},{... | collective-permute-start | bytes 405512 | tf_op jit(solution)/shard_map/while/body/eval_jaxpr/ppermute | solution.py:22
  102.4 7.4 %collective-permute-start.3 = (f32[1,4,22,3,128]{4,3,2,1,0:T(4,128)S(1)}, f32[1,4,22,3,128]{4,3,2,1,0:T(4,128)S(1)}, u32[]{:S(2)}, u32[]{:S(2)}) collective-permute-start(f32[1,4,22,3,128]{4,3,2,1,0:T(4,128)S(1)} %get-tuple-element.543), channel_id=1, source_target_pairs={{0,1},{1,2},{2,3},{4,5},{5,6},{6,7},{8,9},{9,10},{10,11},{12,13},{... | collective-permute-start | bytes 405512 | tf_op jit(solution)/shard_map/while/body/eval_jaxpr/ppermute | solution.py:19
  118.0 6.1 %collective-permute-start = (f32[1,4,3,16,128]{4,3,2,1,0:T(8,128)S(1)}, f32[1,4,3,16,128]{4,3,2,1,0:T(8,128)S(1)}, u32[]{:S(2)}, u32[]{:S(2)}) collective-permute-start(f32[1,4,3,16,128]{4,3,2,1,0:T(8,128)S(1)} %get-tuple-element.540), channel_id=1, source_target_pairs={{0,4},{4,8},{8,12},{12,16},{16,20},{20,24},{24,28},{1,5},{5,9},{9,... | collective-permute-start | bytes 294920 | tf_op jit(solution)/shard_map/while/body/eval_jaxpr/ppermute | solution.py:19
  121.9 6.5 %collective-permute-start.1 = (f32[1,4,3,16,128]{4,3,2,1,0:T(8,128)S(1)}, f32[1,4,3,16,128]{4,3,2,1,0:T(8,128)S(1)}, u32[]{:S(2)}, u32[]{:S(2)}) collective-permute-start(f32[1,4,3,16,128]{4,3,2,1,0:T(8,128)S(1)} %get-tuple-element.541), channel_id=1, source_target_pairs={{4,0},{8,4},{12,8},{16,12},{20,16},{24,20},{28,24},{5,1},{9,5},{13... | collective-permute-start | bytes 294920 | tf_op jit(solution)/shard_map/while/body/eval_jaxpr/ppermute | solution.py:22
  128.5 7.4 %collective-permute-start.2 = (f32[1,4,22,3,128]{4,3,2,1,0:T(4,128)S(1)}, f32[1,4,22,3,128]{4,3,2,1,0:T(4,128)S(1)}, u32[]{:S(2)}, u32[]{:S(2)}) collective-permute-start(f32[1,4,22,3,128]{4,3,2,1,0:T(4,128)S(1)} %get-tuple-element.542), channel_id=1, source_target_pairs={{1,0},{2,1},{3,2},{5,4},{6,5},{7,6},{9,8},{10,9},{11,10},{13,12},{... | collective-permute-start | bytes 405512 | tf_op jit(solution)/shard_map/while/body/eval_jaxpr/ppermute | solution.py:22
  130.4 7.4 %collective-permute-start.3 = (f32[1,4,22,3,128]{4,3,2,1,0:T(4,128)S(1)}, f32[1,4,22,3,128]{4,3,2,1,0:T(4,128)S(1)}, u32[]{:S(2)}, u32[]{:S(2)}) collective-permute-start(f32[1,4,22,3,128]{4,3,2,1,0:T(4,128)S(1)} %get-tuple-element.543), channel_id=1, source_target_pairs={{0,1},{1,2},{2,3},{4,5},{5,6},{6,7},{8,9},{9,10},{10,11},{12,13},{... | collective-permute-start | bytes 405512 | tf_op jit(solution)/shard_map/while/body/eval_jaxpr/ppermute | solution.py:19
  146.0 5.3 %collective-permute-start = (f32[1,4,3,16,128]{4,3,2,1,0:T(8,128)S(1)}, f32[1,4,3,16,128]{4,3,2,1,0:T(8,128)S(1)}, u32[]{:S(2)}, u32[]{:S(2)}) collective-permute-start(f32[1,4,3,16,128]{4,3,2,1,0:T(8,128)S(1)} %get-tuple-element.540), channel_id=1, source_target_pairs={{0,4},{4,8},{8,12},{12,16},{16,20},{20,24},{24,28},{1,5},{5,9},{9,... | collective-permute-start | bytes 294920 | tf_op jit(solution)/shard_map/while/body/eval_jaxpr/ppermute | solution.py:19
  149.1 6.5 %collective-permute-start.1 = (f32[1,4,3,16,128]{4,3,2,1,0:T(8,128)S(1)}, f32[1,4,3,16,128]{4,3,2,1,0:T(8,128)S(1)}, u32[]{:S(2)}, u32[]{:S(2)}) collective-permute-start(f32[1,4,3,16,128]{4,3,2,1,0:T(8,128)S(1)} %get-tuple-element.541), channel_id=1, source_target_pairs={{4,0},{8,4},{12,8},{16,12},{20,16},{24,20},{28,24},{5,1},{9,5},{13... | collective-permute-start | bytes 294920 | tf_op jit(solution)/shard_map/while/body/eval_jaxpr/ppermute | solution.py:22
  155.7 7.4 %collective-permute-start.2 = (f32[1,4,22,3,128]{4,3,2,1,0:T(4,128)S(1)}, f32[1,4,22,3,128]{4,3,2,1,0:T(4,128)S(1)}, u32[]{:S(2)}, u32[]{:S(2)}) collective-permute-start(f32[1,4,22,3,128]{4,3,2,1,0:T(4,128)S(1)} %get-tuple-element.542), channel_id=1, source_target_pairs={{1,0},{2,1},{3,2},{5,4},{6,5},{7,6},{9,8},{10,9},{11,10},{13,12},{... | collective-permute-start | bytes 405512 | tf_op jit(solution)/shard_map/while/body/eval_jaxpr/ppermute | solution.py:22
  157.7 7.4 %collective-permute-start.3 = (f32[1,4,22,3,128]{4,3,2,1,0:T(4,128)S(1)}, f32[1,4,22,3,128]{4,3,2,1,0:T(4,128)S(1)}, u32[]{:S(2)}, u32[]{:S(2)}) collective-permute-start(f32[1,4,22,3,128]{4,3,2,1,0:T(4,128)S(1)} %get-tuple-element.543), channel_id=1, source_target_pairs={{0,1},{1,2},{2,3},{4,5},{5,6},{6,7},{8,9},{9,10},{10,11},{12,13},{... | collective-permute-start | bytes 405512 | tf_op jit(solution)/shard_map/while/body/eval_jaxpr/ppermute | solution.py:19
  173.2 5.3 %collective-permute-start = (f32[1,4,3,16,128]{4,3,2,1,0:T(8,128)S(1)}, f32[1,4,3,16,128]{4,3,2,1,0:T(8,128)S(1)}, u32[]{:S(2)}, u32[]{:S(2)}) collective-permute-start(f32[1,4,3,16,128]{4,3,2,1,0:T(8,128)S(1)} %get-tuple-element.540), channel_id=1, source_target_pairs={{0,4},{4,8},{8,12},{12,16},{16,20},{20,24},{24,28},{1,5},{5,9},{9,... | collective-permute-start | bytes 294920 | tf_op jit(solution)/shard_map/while/body/eval_jaxpr/ppermute | solution.py:19
  176.4 6.5 %collective-permute-start.1 = (f32[1,4,3,16,128]{4,3,2,1,0:T(8,128)S(1)}, f32[1,4,3,16,128]{4,3,2,1,0:T(8,128)S(1)}, u32[]{:S(2)}, u32[]{:S(2)}) collective-permute-start(f32[1,4,3,16,128]{4,3,2,1,0:T(8,128)S(1)} %get-tuple-element.541), channel_id=1, source_target_pairs={{4,0},{8,4},{12,8},{16,12},{20,16},{24,20},{28,24},{5,1},{9,5},{13... | collective-permute-start | bytes 294920 | tf_op jit(solution)/shard_map/while/body/eval_jaxpr/ppermute | solution.py:22
  183.0 7.4 %collective-permute-start.2 = (f32[1,4,22,3,128]{4,3,2,1,0:T(4,128)S(1)}, f32[1,4,22,3,128]{4,3,2,1,0:T(4,128)S(1)}, u32[]{:S(2)}, u32[]{:S(2)}) collective-permute-start(f32[1,4,22,3,128]{4,3,2,1,0:T(4,128)S(1)} %get-tuple-element.542), channel_id=1, source_target_pairs={{1,0},{2,1},{3,2},{5,4},{6,5},{7,6},{9,8},{10,9},{11,10},{13,12},{... | collective-permute-start | bytes 405512 | tf_op jit(solution)/shard_map/while/body/eval_jaxpr/ppermute | solution.py:22
  184.9 7.4 %collective-permute-start.3 = (f32[1,4,22,3,128]{4,3,2,1,0:T(4,128)S(1)}, f32[1,4,22,3,128]{4,3,2,1,0:T(4,128)S(1)}, u32[]{:S(2)}, u32[]{:S(2)}) collective-permute-start(f32[1,4,22,3,128]{4,3,2,1,0:T(4,128)S(1)} %get-tuple-element.543), channel_id=1, source_target_pairs={{0,1},{1,2},{2,3},{4,5},{5,6},{6,7},{8,9},{9,10},{10,11},{12,13},{... | collective-permute-start | bytes 405512 | tf_op jit(solution)/shard_map/while/body/eval_jaxpr/ppermute | solution.py:19
  200.5 5.3 %collective-permute-start = (f32[1,4,3,16,128]{4,3,2,1,0:T(8,128)S(1)}, f32[1,4,3,16,128]{4,3,2,1,0:T(8,128)S(1)}, u32[]{:S(2)}, u32[]{:S(2)}) collective-permute-start(f32[1,4,3,16,128]{4,3,2,1,0:T(8,128)S(1)} %get-tuple-element.540), channel_id=1, source_target_pairs={{0,4},{4,8},{8,12},{12,16},{16,20},{20,24},{24,28},{1,5},{5,9},{9,... | collective-permute-start | bytes 294920 | tf_op jit(solution)/shard_map/while/body/eval_jaxpr/ppermute | solution.py:19
  203.6 6.5 %collective-permute-start.1 = (f32[1,4,3,16,128]{4,3,2,1,0:T(8,128)S(1)}, f32[1,4,3,16,128]{4,3,2,1,0:T(8,128)S(1)}, u32[]{:S(2)}, u32[]{:S(2)}) collective-permute-start(f32[1,4,3,16,128]{4,3,2,1,0:T(8,128)S(1)} %get-tuple-element.541), channel_id=1, source_target_pairs={{4,0},{8,4},{12,8},{16,12},{20,16},{24,20},{28,24},{5,1},{9,5},{13... | collective-permute-start | bytes 294920 | tf_op jit(solution)/shard_map/while/body/eval_jaxpr/ppermute | solution.py:22
  210.2 7.4 %collective-permute-start.2 = (f32[1,4,22,3,128]{4,3,2,1,0:T(4,128)S(1)}, f32[1,4,22,3,128]{4,3,2,1,0:T(4,128)S(1)}, u32[]{:S(2)}, u32[]{:S(2)}) collective-permute-start(f32[1,4,22,3,128]{4,3,2,1,0:T(4,128)S(1)} %get-tuple-element.542), channel_id=1, source_target_pairs={{1,0},{2,1},{3,2},{5,4},{6,5},{7,6},{9,8},{10,9},{11,10},{13,12},{... | collective-permute-start | bytes 405512 | tf_op jit(solution)/shard_map/while/body/eval_jaxpr/ppermute | solution.py:22
  212.1 7.4 %collective-permute-start.3 = (f32[1,4,22,3,128]{4,3,2,1,0:T(4,128)S(1)}, f32[1,4,22,3,128]{4,3,2,1,0:T(4,128)S(1)}, u32[]{:S(2)}, u32[]{:S(2)}) collective-permute-start(f32[1,4,22,3,128]{4,3,2,1,0:T(4,128)S(1)} %get-tuple-element.543), channel_id=1, source_target_pairs={{0,1},{1,2},{2,3},{4,5},{5,6},{6,7},{8,9},{9,10},{10,11},{12,13},{... | collective-permute-start | bytes 405512 | tf_op jit(solution)/shard_map/while/body/eval_jaxpr/ppermute | solution.py:19
  227.7 5.3 %collective-permute-start = (f32[1,4,3,16,128]{4,3,2,1,0:T(8,128)S(1)}, f32[1,4,3,16,128]{4,3,2,1,0:T(8,128)S(1)}, u32[]{:S(2)}, u32[]{:S(2)}) collective-permute-start(f32[1,4,3,16,128]{4,3,2,1,0:T(8,128)S(1)} %get-tuple-element.540), channel_id=1, source_target_pairs={{0,4},{4,8},{8,12},{12,16},{16,20},{20,24},{24,28},{1,5},{5,9},{9,... | collective-permute-start | bytes 294920 | tf_op jit(solution)/shard_map/while/body/eval_jaxpr/ppermute | solution.py:19
  230.8 6.5 %collective-permute-start.1 = (f32[1,4,3,16,128]{4,3,2,1,0:T(8,128)S(1)}, f32[1,4,3,16,128]{4,3,2,1,0:T(8,128)S(1)}, u32[]{:S(2)}, u32[]{:S(2)}) collective-permute-start(f32[1,4,3,16,128]{4,3,2,1,0:T(8,128)S(1)} %get-tuple-element.541), channel_id=1, source_target_pairs={{4,0},{8,4},{12,8},{16,12},{20,16},{24,20},{28,24},{5,1},{9,5},{13... | collective-permute-start | bytes 294920 | tf_op jit(solution)/shard_map/while/body/eval_jaxpr/ppermute | solution.py:22
  237.4 7.4 %collective-permute-start.2 = (f32[1,4,22,3,128]{4,3,2,1,0:T(4,128)S(1)}, f32[1,4,22,3,128]{4,3,2,1,0:T(4,128)S(1)}, u32[]{:S(2)}, u32[]{:S(2)}) collective-permute-start(f32[1,4,22,3,128]{4,3,2,1,0:T(4,128)S(1)} %get-tuple-element.542), channel_id=1, source_target_pairs={{1,0},{2,1},{3,2},{5,4},{6,5},{7,6},{9,8},{10,9},{11,10},{13,12},{... | collective-permute-start | bytes 405512 | tf_op jit(solution)/shard_map/while/body/eval_jaxpr/ppermute | solution.py:22
  239.4 7.4 %collective-permute-start.3 = (f32[1,4,22,3,128]{4,3,2,1,0:T(4,128)S(1)}, f32[1,4,22,3,128]{4,3,2,1,0:T(4,128)S(1)}, u32[]{:S(2)}, u32[]{:S(2)}) collective-permute-start(f32[1,4,22,3,128]{4,3,2,1,0:T(4,128)S(1)} %get-tuple-element.543), channel_id=1, source_target_pairs={{0,1},{1,2},{2,3},{4,5},{5,6},{6,7},{8,9},{9,10},{10,11},{12,13},{... | collective-permute-start | bytes 405512 | tf_op jit(solution)/shard_map/while/body/eval_jaxpr/ppermute | solution.py:19
  255.5 16.6 %all-to-all-start.1 = ((f32[32,1,8]{2,1,0:T(1,128)}), f32[32,1,8]{2,1,0:T(1,128)S(1)}, u32[]{:S(2)}, u32[]{:S(2)}) async-start(f32[32,1,8]{2,1,0:T(1,128)} %broadcast_in_dim.115), calls=%async_computation.1 | async-start | bytes 32768 | tf_op jit(solution)/shard_map/all_to_all | solution.py:35
where the time goes:
time: 274 us; the launch traced here: 273 us
  starting transfers between devices  112 us (41%)
  waiting for transfers between devices  86 us (31%)
  other arithmetic  57.8 us (21%)
  local copies, waits for them, and re-layouts  13.9 us (5%)
    ppermute x18, starting transfers between devices, padded_2(): lax.ppermute(lax.slice_in_dim(block, block.shape[dim] - width, None, axis...  69.1 us
    ppermute x18, waiting for transfers between devices, padded_2(): lax.ppermute(lax.slice_in_dim(block, 0, width, axis=dim), axis, backward)  50.5 us
    ppermute x18, starting transfers between devices, padded_2(): lax.ppermute(lax.slice_in_dim(block, 0, width, axis=dim), axis, backward)  30 us
    ppermute x18, waiting for transfers between devices, padded_2(): lax.ppermute(lax.slice_in_dim(block, block.shape[dim] - width, None, axis...  23.3 us
    broadcast_in_dim x8, other arithmetic, sweep(): return (jnp.concatenate([new_moved, new_damage[:, None]], axis=1), squares)  16.5 us
    all_to_all x2, starting transfers between devices, copy_for_each(): lax.all_to_all(jnp.broadcast_to(x[None], (length, *x.shape)), axis, 0, 0,...  12.6 us
    all_to_all x2, waiting for transfers between devices, copy_for_each(): lax.all_to_all(jnp.broadcast_to(x[None], (length, *x.shape)), axis, 0, 0,...  12.2 us
    mul x16, other arithmetic, elastic_parts(): jnp.expand_dims(face, -4) * (shifted(moved_pad, offset) - current)  8.87 us
  transfers between devices with their start and end apart: 38, of which 36 were waited for; matrix products, arithmetic and copies ran while one was open for 1% of the time, Pallas kernels for 0%

commit v1 on v0

v1 whole, which is shorter than its diff:
```python
import functools

import jax
import jax.numpy as jnp
from jax import lax
from jax.experimental import pallas as pl
from jax.experimental.pallas import tpu as pltpu
from jax.sharding import PartitionSpec as P

GROUPS = (4, 4)
B = 16
HALO = 2 * max(GROUPS) + 1
YP = B + 2 * HALO
ROWS = -(-(YP * YP + 16) // 8) * 8
H_OUT = 0.5 * (1.0 + 0.001)

COS_THIRD = (
    1.000000008260009, -0.22222426779181312, -0.06576120509434145, -0.035390736331322045,
    -0.012547845736683551, -0.050373368401680454, 0.05848138776830297, -0.07087101496233855,
)
SIN_THIRD = (
    1.1547005306829978, 0.1069186220087089, 0.04565984619644209, 0.027903402002033718,
    0.00953945386696008, 0.04580735112208377, -0.054824704413705544, 0.06541734748383539,
)

ROUNDS = sum(GROUPS)
PLACES = [(g, j) for g, k in enumerate(GROUPS) for j in range(k)]
T_HALO = [2 * (GROUPS[g] - 1 - j) for g, j in PLACES]
T_MAX = max(T_HALO)
VMEM = pl.BlockSpec(memory_space=pltpu.VMEM)
SMEM = pl.BlockSpec(memory_space=pltpu.SMEM)
f32 = jnp.float32


def rows_of(h):
    side = B + 2 * h
    return side * side if h == 0 else -(-(side * side + 8) // 8) * 8


def mask_widths():
    k = GROUPS[0]
    return (2 * k - 1, 2 * k + 1, 2 * k, T_MAX)


def state_widths(k):
    return (2 * k + 1,) * 3 + (2 * k,)


def tri(h):
    return h * (h - 1) // 2


def slab_rows(widths):
    return B * sum(widths)


def corner_rows(widths):
    return -(-sum(2 * tri(h) for h in widths) // 8) * 8


def pieces(n):
    return [(s, min(8, n - s)) for s in range(0, n, 8)]


def pack_slabs(readers, widths, outs):
    xhi, xlo, yhi, ylo = outs
    off = 0
    for read, w in zip(readers, widths):
        for l in range(w):
            for s, n in pieces(B):
                xhi[pl.ds(off + l * B + s, n), :] = read(B - w + l, s, n)
                xlo[pl.ds(off + l * B + s, n), :] = read(l, s, n)
        for x in range(B):
            for s, n in pieces(w):
                yhi[pl.ds(off + x * w + s, n), :] = read(x, B - w + s, n)
                ylo[pl.ds(off + x * w + s, n), :] = read(x, s, n)
        off += B * w


def corner_kernel(widths, xlo, xhi, yhi, ylo):
    off = o = 0
    for h in widths:
        for slab, layer in ((xlo, lambda a: h - a), (xhi, lambda a: a - 1)):
            for a in range(1, h):
                n = h - a
                base = off + layer(a) * B
                yhi[pl.ds(o, n), :] = slab[pl.ds(base + B - n, n), :]
                ylo[pl.ds(o, n), :] = slab[pl.ds(base, n), :]
                o += n
        off += B * h


def unpack(own, slabs, corners, widths, edges, stores, reach=None):
    xlo, xhi, ylo, yhi = slabs
    clo, chi = corners
    exlo, exhi, eylo, eyhi = edges
    off = o = 0
    for f, h in enumerate(widths):
        put = stores[f]
        for x in range(B):
            for s, n in pieces(B):
                put(x, s, own[f](x, s, n), None)
        for l in range(h):
            for s, n in pieces(B):
                put(l - h, s, xlo[pl.ds(off + l * B + s, n), :], exlo)
                put(B + l, s, xhi[pl.ds(off + l * B + s, n), :], exhi)
        for x in range(B):
            for s, n in pieces(h):
                put(x, s - h, ylo[pl.ds(off + x * h + s, n), :], eylo)
                put(x, B + s, yhi[pl.ds(off + x * h + s, n), :], eyhi)
        for side, edge in ((0, exlo), (1, exhi)):
            for a in range(1, h):
                n = h - a
                x = -a if side == 0 else B + a - 1
                put(x, -n, clo[pl.ds(o, n), :], jnp.logical_or(edge, eylo))
                put(x, B, chi[pl.ds(o, n), :], jnp.logical_or(edge, eyhi))
                o += n
        off += B * h


def edges_of(place):
    gx, gy = place[0], place[1]
    return gx == 0, gx == place[2] - 1, gy == 0, gy == place[3] - 1


def first_pack_kernel(clamp, load, crack, tough, *outs):
    def own(ref):
        return lambda x, y, n: ref[x, pl.ds(y, n), :].astype(f32)

    def fixed(x, y, n):
        return jnp.maximum(clamp[x, pl.ds(y, n), :], load[x, pl.ds(y, n), :]).astype(f32)

    readers = (fixed, own(load), own(crack), lambda x, y, n: tough[0, x, pl.ds(y, n), :])
    pack_slabs(readers, mask_widths(), outs)


def row(x, y):
    return (x + HALO) * YP + y + HALO


def load_vector(place, table):
    return [table[place[4], i] for i in range(3)]


def first_kernel(
    sides, place, table, clamp, load, crack, tough, xlo, xhi, ylo, yhi, clo, chi,
    state, fix, ld, cr, own_free, *tough_outs,
):
    w = load_vector(place, table)
    edges = edges_of(place)

    def own(ref):
        return lambda x, y, n: ref[x, pl.ds(y, n), :].astype(f32)

    def fixed(x, y, n):
        return jnp.maximum(clamp[x, pl.ds(y, n), :], load[x, pl.ds(y, n), :]).astype(f32)

    def choose(outside, value, other):
        return value if outside is None else jnp.where(outside, other, value)

    def put_fixed(x, y, v, outside):
        fix[pl.ds(row(x, y), v.shape[0]), :] = choose(outside, v, 1.0)
        if outside is None:
            own_free[pl.ds(row(x, y), v.shape[0]), :] = 1.0 - v

    def put_load(x, y, v, outside):
        v = choose(outside, v, 0.0)
        at = pl.ds(row(x, y), v.shape[0])
        ld[at, :] = v
        for i in range(3):
            state[i, at, :] = v * w[i]

    def put_crack(x, y, v, outside):
        at = pl.ds(row(x, y), v.shape[0])
        cr[at, :] = choose(outside, v, -1.0)
        state[3, at, :] = choose(outside, v, 0.0)

    def put_tough(x, y, v, outside):
        n = v.shape[0]
        for ref, h in zip(tough_outs, sides):
            lo, hi = max(y, -h), min(y + n, B + h)
            if -h <= x < B + h and lo < hi:
                at = (x + h) * (B + 2 * h) + lo + h
                ref[pl.ds(at, hi - lo), :] = v[lo - y : hi - y]

    own_free[...] = jnp.zeros_like(own_free)
    unpack(
        (fixed, own(load), own(crack), lambda x, y, n: tough[0, x, pl.ds(y, n), :]),
        (xlo, xhi, ylo, yhi), (clo, chi), mask_widths(), edges,
        (put_fixed, put_load, put_crack, put_tough),
    )


def horner(coefs, w):
    acc = w * coefs[-1] + coefs[-2]
    for c in coefs[-3::-1]:
        acc = acc * w + c
    return acc


def sweep(src, dst, half, flow, fix, ld, cr, own_free, tough, w, left):
    lane = lax.broadcasted_iota(jnp.int32, (8, 128), 1)
    first, last = lane == 0, lane == 127

    def up(v, outside=0.0):
        return jnp.where(last, outside, pltpu.roll(v, 127, 1))

    def down(v, outside=0.0):
        return jnp.where(first, outside, pltpu.roll(v, 1, 1))

    def over(h, body, carry=0):
        def one(i, c):
            for t in range(-(-(B + 2 * h) // 8)):
                c = body(i, (i - h + HALO) * YP + HALO - h + 8 * t, t, c)
            return c

        return lax.fori_loop(0, B + 2 * h, one, carry)

    def pass_flow(i, r, t, c):
        at = pl.ds(r, 8)
        keep = 1.0 - src[3, at, :]
        h = keep * keep * 0.5 + 0.0005
        z = src[2, at, :]
        div = (
            (src[0, pl.ds(r + YP, 8), :] - src[0, pl.ds(r - YP, 8), :])
            + (src[1, pl.ds(r + 1, 8), :] - src[1, pl.ds(r - 1, 8), :])
            + (up(z) - down(z))
        )
        half[at, :] = h
        flow[at, :] = jnp.where(cr[at, :] < -0.5, 0.0, h * div)
        return c

    def pass_moved(i, r, t, acc):
        at = pl.ds(r, 8)
        around = [pl.ds(r + d, 8) for d in (YP, -YP, 1, -1)]
        h0 = half[at, :]
        hn = [half[a, :] for a in around] + [up(h0, H_OUT), down(h0, H_OUT)]
        pairs = [hn[0] + hn[1], hn[2] + hn[3], hn[4] + hn[5]]
        weight = 6.0 * h0 + (pairs[0] + pairs[1] + pairs[2])
        faces = [h0 + n for n in hn]
        f0 = flow[at, :]
        slope = [
            flow[around[0], :] - flow[around[1], :],
            flow[around[2], :] - flow[around[3], :],
            up(f0) - down(f0),
        ]
        is_fixed = fix[at, :] > 0.5
        load = ld[at, :]
        squares = None
        for c in range(3):
            u0 = src[c, at, :]
            un = [src[c, a, :] for a in around] + [up(u0), down(u0)]
            res = slope[c] - weight * u0
            for f, n in zip(faces, un):
                res = res + f * n
            relaxed = u0 + (res * 0.6) / (weight + pairs[c])
            dst[c, at, :] = jnp.where(is_fixed, load * w[c], relaxed)
            squares = res * res if squares is None else squares + res * res
        return acc + jnp.where(own_free[at, :] > 0.5, squares, 0.0)

    def pass_damage(i, r, t, c):
        at = pl.ds(r, 8)
        g = []
        for k in range(3):
            v = dst[k, at, :]
            g.append(
                (
                    dst[k, pl.ds(r + YP, 8), :] - dst[k, pl.ds(r - YP, 8), :],
                    dst[k, pl.ds(r + 1, 8), :] - dst[k, pl.ds(r - 1, 8), :],
                    up(v) - down(v),
                )
            )
        total = g[0][0] + g[1][1] + g[2][2]
        third = total * (1.0 / 3.0)
        dx, dy, dz = g[0][0] - third, g[1][1] - third, g[2][2] - third
        xy, xz, yz = g[0][1] + g[1][0], g[0][2] + g[2][0], g[1][2] + g[2][1]
        xy2, xz2, yz2 = xy * xy, xz * xz, yz * yz
        spread = (dx * dx + dy * dy + dz * dz) + 0.5 * (xy2 + xz2 + yz2)
        det = dx * dy * dz + 0.25 * (xy * xz * yz - (dx * yz2 + dy * xz2 + dz * xy2))
        s6 = spread * (1.0 / 24.0)
        inv = lax.rsqrt(s6 + 1e-08)
        ratio = (det * 0.0625) * (inv * inv * inv)
        radius = s6 * lax.rsqrt(jnp.maximum(s6, 1e-37))
        wq = jnp.maximum(0.5 - 0.5 * jnp.abs(ratio), 0.0)
        cos = horner(COS_THIRD, wq)
        sin = (wq * lax.rsqrt(jnp.maximum(wq, 1e-37))) * horner(SIN_THIRD, wq)
        signed = jnp.where(ratio < 0.0, -radius, radius)
        a, b = signed * cos, signed * sin
        mean = total * (1.0 / 6.0)
        l1, rest = mean + 2.0 * a, mean - a
        p1, p2, p3 = jnp.maximum(l1, 0.0), jnp.maximum(rest + b, 0.0), jnp.maximum(rest - b, 0.0)
        trace = jnp.maximum(total, 0.0)
        psi2 = 0.25 * (trace * trace) + 2.0 * (p1 * p1 + p2 * p2 + p3 * p3)
        d0 = src[3, at, :]
        beside = (
            (src[3, pl.ds(r + YP, 8), :] + src[3, pl.ds(r - YP, 8), :])
            + (src[3, pl.ds(r + 1, 8), :] + src[3, pl.ds(r - 1, 8), :])
            + (up(d0) + down(d0))
        )
        gc = tough[pl.ds(i * (B + 2 * hd) + 8 * t, 8), :]
        new = (psi2 + gc * beside) / (psi2 + 7.0 * gc)
        kind = cr[at, :]
        dst[3, at, :] = jnp.where(kind > 0.5, 1.0, jnp.where(kind < -0.5, 0.0, new))
        return c

    hd = 2 * left
    over(hd + 2, pass_flow)
    acc = over(hd + 1, pass_moved, jnp.zeros((8, 128), f32))
    over(hd, pass_damage)
    return acc


def add_sum(sums, acc, r):
    lane = lax.broadcasted_iota(jnp.int32, (1, 128), 1)
    return jnp.where(lane % ROUNDS == r, jnp.sum(acc), sums)


def group_kernel(group, *refs):
    k = GROUPS[group]
    final = group == len(GROUPS) - 1
    refs = list(refs)

    def take(n):
        out = refs[:n]
        del refs[:n]
        return out

    place, table, fix, ld, cr, own_free = take(6)
    tough = take(k)
    w = load_vector(place, table)
    if group == 0:
        (src,) = take(1)
        sums = jnp.zeros((1, 128), f32)
    else:
        state, xlo, xhi, ylo, yhi, clo, chi, sums_in = take(8)
        sums = sums_in[...]
    if final:
        moved_out, damage_out, sums_out = take(3)
    else:
        (state_out,) = take(1)
        slab_outs = take(4)
        (sums_out,) = take(1)
    half, flow, *bufs = refs
    if group > 0:
        src = bufs[2]

        def own(f):
            return lambda x, y, n: state[f, x, pl.ds(y, n), :]

        def put(f):
            def one(x, y, v, outside):
                v = v if outside is None else jnp.where(outside, 0.0, v)
                src[f, pl.ds(row(x, y), v.shape[0]), :] = v

            return one

        unpack(
            [own(f) for f in range(4)], (xlo, xhi, ylo, yhi), (clo, chi), state_widths(k),
            edges_of(place), [put(f) for f in range(4)],
        )
    start = sum(GROUPS[:group])
    for j in range(k):
        dst = bufs[j % 2]
        acc = sweep(src, dst, half, flow, fix, ld, cr, own_free, tough[j], w, k - 1 - j)
        sums = add_sum(sums, acc, start + j)
        src = dst
    if final:
        for x in range(B):
            for s, n in pieces(B):
                at = pl.ds(row(x, s), n)
                for c in range(3):
                    moved_out[0, c, x, pl.ds(s, n), :] = src[c, at, :]
                damage_out[0, x, pl.ds(s, n), :] = src[3, at, :]
        sums_out[...] = jnp.broadcast_to(sums, sums_out.shape)
    else:
        for f in range(4):
            for x in range(B):
                for s, n in pieces(B):
                    state_out[f, x, pl.ds(s, n), :] = src[f, pl.ds(row(x, s), n), :]
        readers = [
            (lambda x, y, n, f=f: src[f, pl.ds(row(x, y), n), :]) for f in range(4)
        ]
        pack_slabs(readers, state_widths(GROUPS[group + 1]), slab_outs)
        sums_out[...] = sums


def table_kernel(scale, place, parts, out):
    total = jnp.sum(parts[...], axis=0, keepdims=True)
    root = jnp.sqrt(total * scale)
    out[...] = pltpu.roll(jnp.broadcast_to(root, (8, 128)), place[5], 1)[:1, :ROUNDS]


def call(kernel, name, outs, ins, scratch=(), smem=0, us=1.0):
    single = isinstance(outs, tuple)
    shapes = [outs] if single else outs
    res = pl.pallas_call(
        kernel,
        out_shape=[jax.ShapeDtypeStruct(s, f32) for s in shapes],
        in_specs=[SMEM] * smem + [VMEM] * (len(ins) - smem),
        out_specs=[VMEM] * len(shapes),
        scratch_shapes=list(scratch),
        name=name,
        compiler_params=pltpu.CompilerParams(vmem_limit_bytes=24 * 1024 * 1024),
        cost_estimate=pl.CostEstimate(
            flops=int(us * 4e6), bytes_accessed=int(us * 1e6), transcendentals=0
        ),
    )(*ins)
    return res[0] if single else res


def shift(x, axis, by):
    n = lax.axis_size(axis)
    return lax.ppermute(x, axis, [(i, (i + by) % n) for i in range(n)])


def swap_sides(slabs):
    xhi, xlo, yhi, ylo = slabs
    return shift(xhi, "gx", 1), shift(xlo, "gx", -1), shift(yhi, "gy", 1), shift(ylo, "gy", -1)


def swap_corners(xlo, xhi, widths, name):
    shape = (corner_rows(widths), 128)
    yhi, ylo = call(functools.partial(corner_kernel, widths), name, [shape] * 2, [xlo, xhi], us=0.3)
    return shift(yhi, "gy", 1), shift(ylo, "gy", -1)


def on_device(load_index, load_table, toughness, clamp_mask, load_mask, crack_mask):
    home = lax.axis_index("section").astype(jnp.int32)
    nx, ny = lax.axis_size("gx"), lax.axis_size("gy")
    place = jnp.stack(
        [
            lax.axis_index("gx").astype(jnp.int32),
            lax.axis_index("gy").astype(jnp.int32),
            jnp.int32(nx),
            jnp.int32(ny),
            load_index[0],
            home,
        ]
    )
    raw = [clamp_mask, load_mask, crack_mask, toughness]
    widths = mask_widths()
    slabs = call(first_pack_kernel, "first_pack", [(slab_rows(widths), 128)] * 4, raw, us=0.5)
    received = swap_sides(slabs)
    corners = swap_corners(received[0], received[1], widths, "first_corners")
    sides = tuple(sorted({h for h in T_HALO if h}, reverse=True))
    ext = (ROWS, 128)
    made = call(
        functools.partial(first_kernel, sides), "first",
        [(4,) + ext, ext, ext, ext, ext] + [(rows_of(h), 128) for h in sides],
        [place, load_table, *raw, *received, *corners], smem=2, us=1.0,
    )
    state, kinds = made[0], made[1:5]
    by_halo = dict(zip(sides, made[5:]))
    by_halo[0] = toughness.reshape(B * B, 128)
    tough = [
        by_halo[h] if r == 0 else shift(by_halo[h], "section", -r) for r, h in enumerate(T_HALO)
    ]
    sums = None
    for g, k in enumerate(GROUPS):
        start = sum(GROUPS[:g])
        ins = [place, load_table, *kinds, *tough[start : start + k]]
        if g == 0:
            ins.append(state)
        else:
            received = swap_sides(slabs)
            corners = swap_corners(received[0], received[1], state_widths(k), f"corners_{g}")
            ins += [state, *received, *corners, sums]
        final = g == len(GROUPS) - 1
        if final:
            outs = [(1, 3, B, B, 128), (1, B, B, 128), (nx * ny, 128)]
        else:
            n = slab_rows(state_widths(GROUPS[g + 1]))
            outs = [(4, B, B, 128)] + [(n, 128)] * 4 + [(1, 128)]
        scratch = [pltpu.VMEM(ext, f32)] * 2 + [pltpu.VMEM((4,) + ext, f32)] * (2 + (g > 0))
        res = call(
            functools.partial(group_kernel, g), f"group_{g}", outs, ins, scratch, smem=2, us=13.0
        )
        if final:
            moved, damage, parts = res
        else:
            state, slabs, sums = res[0], res[1:5], res[5]
    parts = lax.all_to_all(parts, ("gx", "gy"), 0, 0, tiled=True)
    scale = 1.0 / (3.0 * B * B * 128 * nx * ny)
    table = call(
        functools.partial(table_kernel, scale), "table", (1, ROUNDS), [place, parts], smem=1, us=0.1
    )
    return moved, damage, table


def solution(mesh):
    in_specs = (
        P("section"),
        P(),
        P("section", "gx", "gy", None),
        P("gx", "gy", None),
        P("gx", "gy", None),
        P("gx", "gy", None),
    )
    out_specs = (
        P("section", None, "gx", "gy", None),
        P("section", "gx", "gy", None),
        P("section", None),
    )
    return jax.shard_map(
        on_device, mesh=mesh, in_specs=in_specs, out_specs=out_specs, check_vma=False
    )
```

time: 274 us -> 162 us (0.59)
  starting transfers between devices: 112 us -> 25.8 us
  Pallas kernels: 0 us -> 71.2 us
  other arithmetic: 57.8 us -> 0 us
  waiting for transfers between devices: 86 us -> 38.2 us
  blocking collectives: 0 us -> 17.3 us
  local copies, waits for them, and re-layouts: 13.9 us -> 8.08 us
    ppermute x36 -> x19, starting transfers between devices: 99 us -> 25.8 us  [shift(): return lax.ppermute(x, axis, [(i, (i + by) % n) for i in range(n)])]
    pallas_call x0 -> x7, Pallas kernels: none -> 71.2 us  [call(): pl.pallas_call(kernel, out_shape=[jax.ShapeDtypeStruct(s, f32) for s in s...]
    ppermute x36 -> x19, waiting for transfers between devices: 73.8 us -> 38.2 us  [shift(): return lax.ppermute(x, axis, [(i, (i + by) % n) for i in range(n)])]
    all_to_all x0 -> x1, blocking collectives: none -> 17.3 us  [on_device(): parts = lax.all_to_all(parts, ('gx', 'gy'), 0, 0, tiled=True)]
    broadcast_in_dim x8 -> x0, other arithmetic: 16.5 us -> none  [sweep(): return (jnp.concatenate([new_moved, new_damage[:, None]], axis=1), squares)]
    all_to_all x2 -> x0, starting transfers between devices: 12.6 us -> none  [copy_for_each(): lax.all_to_all(jnp.broadcast_to(x[None], (length, *x.shape)), axis, 0, 0,...]
    all_to_all x2 -> x0, waiting for transfers between devices: 12.2 us -> none  [copy_for_each(): lax.all_to_all(jnp.broadcast_to(x[None], (length, *x.shape)), axis, 0, 0,...]
    mul x17 -> x0, other arithmetic: 8.98 us -> none  [the longest x16 8.87 us: elastic_parts(): jnp.expand_dims(face, -4) * (shifted(moved_pad, offset) - current)]
  transfers between devices with their start and end apart: 38 -> 19, of which waited for: 36 -> 9; matrix products, arithmetic and copies ran while one was open for 1% -> 1% of each run, Pallas kernels for 0% -> 0%
where the time goes in v1:
time: 162 us
  Pallas kernels  71.2 us (44%)
  waiting for transfers between devices  38.2 us (24%)
  starting transfers between devices  25.8 us (16%)
  blocking collectives  17.3 us (11%)
  local copies, waits for them, and re-layouts  8.08 us (5%)
    pallas_call x7, Pallas kernels, call(): pl.pallas_call(kernel, out_shape=[jax.ShapeDtypeStruct(s, f32) for s in s...  71.2 us
    ppermute x19, waiting for transfers between devices, shift(): return lax.ppermute(x, axis, [(i, (i + by) % n) for i in range(n)])  38.2 us
    ppermute x19, starting transfers between devices, shift(): return lax.ppermute(x, axis, [(i, (i + by) % n) for i in range(n)])  25.8 us
    all_to_all x1, blocking collectives, on_device(): parts = lax.all_to_all(parts, ('gx', 'gy'), 0, 0, tiled=True)  17.3 us
    unnamed x17, local copies, waits for them, and re-layouts  8 us
  transfers between devices with their start and end apart: 19, of which 9 were waited for; matrix products, arithmetic and copies ran while one was open for 1% of the time, Pallas kernels for 0%

profile of v1, /device:TPU:2, one launch (start us, length us, event | category | flops | bytes accessed | tf_op | source)
XLA Modules:
  0.0 161.9 jit_solution(8013377012195525623)
XLA Ops:
  0.6 0.0 copy-start
  0.6 0.9 copy-done
  1.5 0.9 copy-done.2
  2.4 0.9 copy-done.4
  3.3 0.9 copy-done.6
  4.3 0.1 first_pack.1
  4.3 2.0 %collective-permute-start = (f32[480,128]{1,0:T(8,128)S(1)}, f32[480,128]{1,0:T(8,128)S(1)}, u32[]{:S(2)}, u32[]{:S(2)}) collective-permute-start(f32[480,128]{1,0:T(8,128)S(1)} %get-tuple-element.28), channel_id=1, source_target_pairs={{0,4},{4,8},{8,12},{12,16},{16,20},{20,24},{24,28},{28,0},{1,5},{5... | collective-permute-start | bytes 737288 | tf_op jit(solution)/shard_map/ppermute | solution.py:413
  6.3 4.0 %collective-permute-start.1 = (f32[480,128]{1,0:T(8,128)S(1)}, f32[480,128]{1,0:T(8,128)S(1)}, u32[]{:S(2)}, u32[]{:S(2)}) collective-permute-start(f32[480,128]{1,0:T(8,128)S(1)} %get-tuple-element.29), channel_id=1, source_target_pairs={{0,28},{4,0},{8,4},{12,8},{16,12},{20,16},{24,20},{28,24},{1,29},{... | collective-permute-start | bytes 737288 | tf_op jit(solution)/shard_map/ppermute | solution.py:413
  10.4 1.5 collective-permute-start.2
  11.9 0.5 collective-permute-start.3
  12.4 3.8 %collective-permute-done.xlo = f32[480,128]{1,0:T(8,128)S(1)} collective-permute-done((f32[480,128]{1,0:T(8,128)S(1)}, f32[480,128]{1,0:T(8,128)S(1)}, u32[]{:S(2)}, u32[]{:S(2)}) %collective-permute-start) | collective-permute-done | bytes 245792 | tf_op jit(solution)/shard_map/ppermute | solution.py:413
  16.2 0.0 collective-permute-done.1.xhi
  16.3 1.6 collective-permute-start.4
  17.8 0.5 collective-permute-start.5
  19.0 0.8 copy.14.table.refs_1_
  19.8 0.1 stack.15.place.refs_0_
  19.9 0.0 collective-permute-done.3.yhi
  19.9 1.1 collective-permute-done.4.clo
  21.0 1.5 collective-permute-done.5.chi
  22.5 0.9 copy-done.1
  23.4 0.9 copy-done.3
  24.3 0.9 copy-done.5
  25.2 0.9 copy-done.7
  26.1 1.5 first.1
  27.6 0.8 collective-permute-start.10
  28.4 2.4 %collective-permute-start.11 = (f32[408,128]{1,0:T(8,128)S(1)}, f32[408,128]{1,0:T(8,128)S(1)}, u32[]{:S(2)}, u32[]{:S(2)}) collective-permute-start(f32[408,128]{1,0:T(8,128)S(1)} %get-tuple-element.40), channel_id=1, source_target_pairs={{0,192},{32,224},{64,0},{96,32},{128,64},{160,96},{192,128},{224,1... | collective-permute-start | bytes 626696 | tf_op jit(solution)/shard_map/ppermute | solution.py:413
  30.7 0.4 collective-permute-start.12
  31.1 6.9 %collective-permute-done.12.refs_9_ = f32[256,128]{1,0:T(8,128)S(1)} collective-permute-done((f32[256,128]{1,0:T(8,128)S(1)}, f32[256,128]{1,0:T(8,128)S(1)}, u32[]{:S(2)}, u32[]{:S(2)}) %collective-permute-start.12) | collective-permute-done | bytes 131104 | tf_op jit(solution)/shard_map/ppermute | solution.py:413
  38.0 1.8 %collective-permute-done.11.refs_8_ = f32[408,128]{1,0:T(8,128)S(1)} collective-permute-done((f32[408,128]{1,0:T(8,128)S(1)}, f32[408,128]{1,0:T(8,128)S(1)}, u32[]{:S(2)}, u32[]{:S(2)}) %collective-permute-start.11) | collective-permute-done | bytes 208928 | tf_op jit(solution)/shard_map/ppermute | solution.py:413
  39.8 0.0 collective-permute-done.10.refs_7_
  39.8 33.7 %group_0.1 = (f32[4,16,16,128]{3,2,1,0:T(8,128)S(1)}, f32[560,128]{1,0:T(8,128)S(1)}, f32[560,128]{1,0:T(8,128)S(1)}, f32[560,128]{1,0:T(8,128)S(1)}, f32[560,128]{1,0:T(8,128)S(1)}, /*index=5*/f32[1,128]{1,0:T(1,128)S(1)}) custom-call(s32[6]{0:T(128)S(1)} %stack.15.place.refs_0_, f32[64,3]{1,0:T(8,128)S(1)} %copy.14.table.refs_1_, ...), custom_call_target="tpu_custom_call" | custom-call | flops 52000000 | bytes 13000000 | tf_op jit(solution)/shard_map/group_0/pallas_call | solution.py:396
  73.6 0.1 collective-permute-start.13
  73.6 3.2 %collective-permute-start.14 = (f32[560,128]{1,0:T(8,128)S(1)}, f32[560,128]{1,0:T(8,128)S(1)}, u32[]{:S(2)}, u32[]{:S(2)}) collective-permute-start(f32[560,128]{1,0:T(8,128)S(1)} %get-tuple-element.44), channel_id=1, source_target_pairs={{0,28},{4,0},{8,4},{12,8},{16,12},{20,16},{24,20},{28,24},{1,29},{... | collective-permute-start | bytes 860168 | tf_op jit(solution)/shard_map/ppermute | solution.py:413
  76.9 0.0 collective-permute-start.9
  76.9 2.8 %collective-permute-start.7 = (f32[584,128]{1,0:T(8,128)S(1)}, f32[584,128]{1,0:T(8,128)S(1)}, u32[]{:S(2)}, u32[]{:S(2)}) collective-permute-start(f32[584,128]{1,0:T(8,128)S(1)} %get-tuple-element.39), channel_id=1, source_target_pairs={{0,96},{32,128},{64,160},{96,192},{128,224},{160,0},{192,32},{224,... | collective-permute-start | bytes 897032 | tf_op jit(solution)/shard_map/ppermute | solution.py:413
  79.6 1.8 %collective-permute-start.6 = (f32[792,128]{1,0:T(8,128)S(1)}, f32[792,128]{1,0:T(8,128)S(1)}, u32[]{:S(2)}, u32[]{:S(2)}) collective-permute-start(f32[792,128]{1,0:T(8,128)S(1)} %get-tuple-element.38.refs_6_), channel_id=1, source_target_pairs={{0,128},{32,160},{64,192},{96,224},{128,0},{160,32},{192,64},{224,... | collective-permute-start | bytes 1216520 | tf_op jit(solution)/shard_map/ppermute | solution.py:413
  81.5 1.2 collective-permute-done.9.refs_9_
  82.6 0.2 collective-permute-start.8
  82.8 1.2 collective-permute-start.15
  84.0 0.8 collective-permute-start.16
  84.9 17.6 %collective-permute-done.8.refs_8_ = f32[408,128]{1,0:T(8,128)S(1)} collective-permute-done((f32[408,128]{1,0:T(8,128)S(1)}, f32[408,128]{1,0:T(8,128)S(1)}, u32[]{:S(2)}, u32[]{:S(2)}) %collective-permute-start.8) | collective-permute-done | bytes 208928 | tf_op jit(solution)/shard_map/ppermute | solution.py:413
  102.5 1.2 collective-permute-start.17
  103.7 0.8 collective-permute-start.18
  104.6 3.0 %collective-permute-done.17.refs_15_ = f32[272,128]{1,0:T(8,128)S(1)} collective-permute-done((f32[272,128]{1,0:T(8,128)S(1)}, f32[272,128]{1,0:T(8,128)S(1)}, u32[]{:S(2)}, u32[]{:S(2)}) %collective-permute-start.17) | collective-permute-done | bytes 139296 | tf_op jit(solution)/shard_map/ppermute | solution.py:413
  107.6 1.2 collective-permute-done.18.refs_16_
  108.8 34.7 %group_1.1 = (f32[1,3,16,16,128]{4,3,2,1,0:T(8,128)}, f32[1,16,16,128]{3,2,1,0:T(8,128)}, f32[32,128]{1,0:T(8,128)S(1)}) custom-call(s32[6]{0:T(128)S(1)} %stack.15.place.refs_0_, f32[64,3]{1,0:T(8,128)S(1)} %copy.14.table.refs_1_, f32[1176,128]{1,0:T(8,128)S(1)} %get-tuple-element.34.refs_2_, f32[1176,128]{1,0:T(8,128)S(1)} %get-tuple-element.35.refs_3_, ...), custom_call_target="tpu_custom_call" | custom-call | flops 52000000 | bytes 13000000 | tf_op jit(solution)/shard_map/group_1/pallas_call | solution.py:396
  143.5 17.3 %all_to_all.11 = f32[32,1,128]{2,1,0:T(1,128)S(1)} all-to-all(f32[32,1,128]{2,1,0:T(1,128)S(1)} %bitcast.11), channel_id=1, replica_groups=mesh['section'=8,'gx'=8,'gy'=4] {'gx','gy'}, dimensions={0} | all-to-all | bytes 32768 | tf_op jit(solution)/shard_map/all_to_all | solution.py:482
  160.7 1.1 table.2
  (16 shorter events, 0.1 us)
Async XLA Ops:
  0.6 0.9 copy-start
  1.5 0.9 copy-start.2
  2.4 0.9 copy-start.4
  3.3 0.9 copy-start.6
  4.3 11.9 %collective-permute-start = (f32[480,128]{1,0:T(8,128)S(1)}, f32[480,128]{1,0:T(8,128)S(1)}, u32[]{:S(2)}, u32[]{:S(2)}) collective-permute-start(f32[480,128]{1,0:T(8,128)S(1)} %get-tuple-element.28), channel_id=1, source_target_pairs={{0,4},{4,8},{8,12},{12,16},{16,20},{20,24},{24,28},{28,0},{1,5},{5... | collective-permute-start | bytes 737288 | tf_op jit(solution)/shard_map/ppermute | solution.py:413
  6.3 9.9 %collective-permute-start.1 = (f32[480,128]{1,0:T(8,128)S(1)}, f32[480,128]{1,0:T(8,128)S(1)}, u32[]{:S(2)}, u32[]{:S(2)}) collective-permute-start(f32[480,128]{1,0:T(8,128)S(1)} %get-tuple-element.29), channel_id=1, source_target_pairs={{0,28},{4,0},{8,4},{12,8},{16,12},{20,16},{24,20},{28,24},{1,29},{... | collective-permute-start | bytes 737288 | tf_op jit(solution)/shard_map/ppermute | solution.py:413
  10.4 9.5 %collective-permute-start.2 = (f32[480,128]{1,0:T(8,128)S(1)}, f32[480,128]{1,0:T(8,128)S(1)}, u32[]{:S(2)}, u32[]{:S(2)}) collective-permute-start(f32[480,128]{1,0:T(8,128)S(1)} %get-tuple-element.30), channel_id=1, source_target_pairs={{0,1},{1,2},{2,3},{3,0},{4,5},{5,6},{6,7},{7,4},{8,9},{9,10},{10,1... | collective-permute-start | bytes 737288 | tf_op jit(solution)/shard_map/ppermute | solution.py:413
  11.9 8.0 %collective-permute-start.3 = (f32[480,128]{1,0:T(8,128)S(1)}, f32[480,128]{1,0:T(8,128)S(1)}, u32[]{:S(2)}, u32[]{:S(2)}) collective-permute-start(f32[480,128]{1,0:T(8,128)S(1)} %get-tuple-element.31), channel_id=1, source_target_pairs={{0,3},{1,0},{2,1},{3,2},{4,7},{5,4},{6,5},{7,6},{8,11},{9,8},{10,9... | collective-permute-start | bytes 737288 | tf_op jit(solution)/shard_map/ppermute | solution.py:413
  16.3 4.7 %collective-permute-start.4 = (f32[200,128]{1,0:T(8,128)S(1)}, f32[200,128]{1,0:T(8,128)S(1)}, u32[]{:S(2)}, u32[]{:S(2)}) collective-permute-start(f32[200,128]{1,0:T(8,128)S(1)} %get-tuple-element.32), channel_id=1, source_target_pairs={{0,1},{1,2},{2,3},{3,0},{4,5},{5,6},{6,7},{7,4},{8,9},{9,10},{10,1... | collective-permute-start | bytes 307208 | tf_op jit(solution)/shard_map/ppermute | solution.py:413
  17.8 4.7 %collective-permute-start.5 = (f32[200,128]{1,0:T(8,128)S(1)}, f32[200,128]{1,0:T(8,128)S(1)}, u32[]{:S(2)}, u32[]{:S(2)}) collective-permute-start(f32[200,128]{1,0:T(8,128)S(1)} %get-tuple-element.33), channel_id=1, source_target_pairs={{0,3},{1,0},{2,1},{3,2},{4,7},{5,4},{6,5},{7,6},{8,11},{9,8},{10,9... | collective-permute-start | bytes 307208 | tf_op jit(solution)/shard_map/ppermute | solution.py:413
  22.5 0.9 copy-start.1
  23.4 0.9 copy-start.3
  24.3 0.9 copy-start.5
  25.2 0.9 copy-start.7
  27.6 12.2 %collective-permute-start.10 = (f32[584,128]{1,0:T(8,128)S(1)}, f32[584,128]{1,0:T(8,128)S(1)}, u32[]{:S(2)}, u32[]{:S(2)}) collective-permute-start(f32[584,128]{1,0:T(8,128)S(1)} %get-tuple-element.39), channel_id=1, source_target_pairs={{0,224},{32,0},{64,32},{96,64},{128,96},{160,128},{192,160},{224,1... | collective-permute-start | bytes 897032 | tf_op jit(solution)/shard_map/ppermute | solution.py:413
  28.4 11.4 %collective-permute-start.11 = (f32[408,128]{1,0:T(8,128)S(1)}, f32[408,128]{1,0:T(8,128)S(1)}, u32[]{:S(2)}, u32[]{:S(2)}) collective-permute-start(f32[408,128]{1,0:T(8,128)S(1)} %get-tuple-element.40), channel_id=1, source_target_pairs={{0,192},{32,224},{64,0},{96,32},{128,64},{160,96},{192,128},{224,1... | collective-permute-start | bytes 626696 | tf_op jit(solution)/shard_map/ppermute | solution.py:413
  30.7 7.3 %collective-permute-start.12 = (f32[256,128]{1,0:T(8,128)S(1)}, f32[256,128]{1,0:T(8,128)S(1)}, u32[]{:S(2)}, u32[]{:S(2)}) collective-permute-start(f32[256,128]{1,0:T(8,128)S(1)} %bitcast.8), channel_id=1, source_target_pairs={{0,160},{32,192},{64,224},{96,0},{128,32},{160,64},{192,96},{224,1... | collective-permute-start | bytes 393224 | tf_op jit(solution)/shard_map/ppermute | solution.py:413
  73.6 9.3 %collective-permute-start.13 = (f32[560,128]{1,0:T(8,128)S(1)}, f32[560,128]{1,0:T(8,128)S(1)}, u32[]{:S(2)}, u32[]{:S(2)}) collective-permute-start(f32[560,128]{1,0:T(8,128)S(1)} %get-tuple-element.43), channel_id=1, source_target_pairs={{0,4},{4,8},{8,12},{12,16},{16,20},{20,24},{24,28},{28,0},{1,5},{5... | collective-permute-start | bytes 860168 | tf_op jit(solution)/shard_map/ppermute | solution.py:413
  73.6 10.4 %collective-permute-start.14 = (f32[560,128]{1,0:T(8,128)S(1)}, f32[560,128]{1,0:T(8,128)S(1)}, u32[]{:S(2)}, u32[]{:S(2)}) collective-permute-start(f32[560,128]{1,0:T(8,128)S(1)} %get-tuple-element.44), channel_id=1, source_target_pairs={{0,28},{4,0},{8,4},{12,8},{16,12},{20,16},{24,20},{28,24},{1,29},{... | collective-permute-start | bytes 860168 | tf_op jit(solution)/shard_map/ppermute | solution.py:413
  76.9 5.8 %collective-permute-start.9 = (f32[256,128]{1,0:T(8,128)S(1)}, f32[256,128]{1,0:T(8,128)S(1)}, u32[]{:S(2)}, u32[]{:S(2)}) collective-permute-start(f32[256,128]{1,0:T(8,128)S(1)} %bitcast.9), channel_id=1, source_target_pairs={{0,32},{32,64},{64,96},{96,128},{128,160},{160,192},{192,224},{224... | collective-permute-start | bytes 393224 | tf_op jit(solution)/shard_map/ppermute | solution.py:413
  76.9 26.8 %collective-permute-start.7 = (f32[584,128]{1,0:T(8,128)S(1)}, f32[584,128]{1,0:T(8,128)S(1)}, u32[]{:S(2)}, u32[]{:S(2)}) collective-permute-start(f32[584,128]{1,0:T(8,128)S(1)} %get-tuple-element.39), channel_id=1, source_target_pairs={{0,96},{32,128},{64,160},{96,192},{128,224},{160,0},{192,32},{224,... | collective-permute-start | bytes 897032 | tf_op jit(solution)/shard_map/ppermute | solution.py:413
  79.6 24.9 %collective-permute-start.6 = (f32[792,128]{1,0:T(8,128)S(1)}, f32[792,128]{1,0:T(8,128)S(1)}, u32[]{:S(2)}, u32[]{:S(2)}) collective-permute-start(f32[792,128]{1,0:T(8,128)S(1)} %get-tuple-element.38.refs_6_), channel_id=1, source_target_pairs={{0,128},{32,160},{64,192},{96,224},{128,0},{160,32},{192,64},{224,... | collective-permute-start | bytes 1216520 | tf_op jit(solution)/shard_map/ppermute | solution.py:413
  82.6 19.9 %collective-permute-start.8 = (f32[408,128]{1,0:T(8,128)S(1)}, f32[408,128]{1,0:T(8,128)S(1)}, u32[]{:S(2)}, u32[]{:S(2)}) collective-permute-start(f32[408,128]{1,0:T(8,128)S(1)} %get-tuple-element.40), channel_id=1, source_target_pairs={{0,64},{32,96},{64,128},{96,160},{128,192},{160,224},{192,0},{224,... | collective-permute-start | bytes 626696 | tf_op jit(solution)/shard_map/ppermute | solution.py:413
  82.8 21.7 %collective-permute-start.15 = (f32[560,128]{1,0:T(8,128)S(1)}, f32[560,128]{1,0:T(8,128)S(1)}, u32[]{:S(2)}, u32[]{:S(2)}) collective-permute-start(f32[560,128]{1,0:T(8,128)S(1)} %get-tuple-element.45), channel_id=1, source_target_pairs={{0,1},{1,2},{2,3},{3,0},{4,5},{5,6},{6,7},{7,4},{8,9},{9,10},{10,1... | collective-permute-start | bytes 860168 | tf_op jit(solution)/shard_map/ppermute | solution.py:413
  84.0 20.5 %collective-permute-start.16 = (f32[560,128]{1,0:T(8,128)S(1)}, f32[560,128]{1,0:T(8,128)S(1)}, u32[]{:S(2)}, u32[]{:S(2)}) collective-permute-start(f32[560,128]{1,0:T(8,128)S(1)} %get-tuple-element.46), channel_id=1, source_target_pairs={{0,3},{1,0},{2,1},{3,2},{4,7},{5,4},{6,5},{7,6},{8,11},{9,8},{10,9... | collective-permute-start | bytes 860168 | tf_op jit(solution)/shard_map/ppermute | solution.py:413
  102.5 5.1 %collective-permute-start.17 = (f32[272,128]{1,0:T(8,128)S(1)}, f32[272,128]{1,0:T(8,128)S(1)}, u32[]{:S(2)}, u32[]{:S(2)}) collective-permute-start(f32[272,128]{1,0:T(8,128)S(1)} %get-tuple-element.47), channel_id=1, source_target_pairs={{0,1},{1,2},{2,3},{3,0},{4,5},{5,6},{6,7},{7,4},{8,9},{9,10},{10,1... | collective-permute-start | bytes 417800 | tf_op jit(solution)/shard_map/ppermute | solution.py:413
  103.7 5.1 %collective-permute-start.18 = (f32[272,128]{1,0:T(8,128)S(1)}, f32[272,128]{1,0:T(8,128)S(1)}, u32[]{:S(2)}, u32[]{:S(2)}) collective-permute-start(f32[272,128]{1,0:T(8,128)S(1)} %get-tuple-element.48), channel_id=1, source_target_pairs={{0,3},{1,0},{2,1},{3,2},{4,7},{5,4},{6,5},{7,6},{8,11},{9,8},{10,9... | collective-permute-start | bytes 417800 | tf_op jit(solution)/shard_map/ppermute | solution.py:413

commit v2 on v1

--- a/solution.py
+++ b/solution.py
@@ -167,13 +167,16 @@
         v = choose(outside, v, 0.0)
         at = pl.ds(row(x, y), v.shape[0])
         ld[at, :] = v
+        above, below = up(v), down(v)
         for i in range(3):
             state[i, at, :] = v * w[i]
+            state[4 + i, at, :] = above * w[i]
+            state[7 + i, at, :] = below * w[i]
 
     def put_crack(x, y, v, outside):
         at = pl.ds(row(x, y), v.shape[0])
         cr[at, :] = choose(outside, v, -1.0)
-        state[3, at, :] = choose(outside, v, 0.0)
+        put_state(state, 3, at, choose(outside, v, 0.0))
 
     def put_tough(x, y, v, outside):
         n = v.shape[0]
@@ -198,115 +201,167 @@
     return acc
 
 
-def sweep(src, dst, half, flow, fix, ld, cr, own_free, tough, w, left):
-    lane = lax.broadcasted_iota(jnp.int32, (8, 128), 1)
-    first, last = lane == 0, lane == 127
-
-    def up(v, outside=0.0):
-        return jnp.where(last, outside, pltpu.roll(v, 127, 1))
-
-    def down(v, outside=0.0):
-        return jnp.where(first, outside, pltpu.roll(v, 1, 1))
-
-    def over(h, body, carry=0):
-        def one(i, c):
-            for t in range(-(-(B + 2 * h) // 8)):
-                c = body(i, (i - h + HALO) * YP + HALO - h + 8 * t, t, c)
-            return c
-
-        return lax.fori_loop(0, B + 2 * h, one, carry)
-
-    def pass_flow(i, r, t, c):
-        at = pl.ds(r, 8)
-        keep = 1.0 - src[3, at, :]
-        h = keep * keep * 0.5 + 0.0005
-        z = src[2, at, :]
-        div = (
-            (src[0, pl.ds(r + YP, 8), :] - src[0, pl.ds(r - YP, 8), :])
-            + (src[1, pl.ds(r + 1, 8), :] - src[1, pl.ds(r - 1, 8), :])
-            + (up(z) - down(z))
-        )
-        half[at, :] = h
-        flow[at, :] = jnp.where(cr[at, :] < -0.5, 0.0, h * div)
-        return c
-
-    def pass_moved(i, r, t, acc):
-        at = pl.ds(r, 8)
-        around = [pl.ds(r + d, 8) for d in (YP, -YP, 1, -1)]
-        h0 = half[at, :]
-        hn = [half[a, :] for a in around] + [up(h0, H_OUT), down(h0, H_OUT)]
-        pairs = [hn[0] + hn[1], hn[2] + hn[3], hn[4] + hn[5]]
-        weight = 6.0 * h0 + (pairs[0] + pairs[1] + pairs[2])
-        faces = [h0 + n for n in hn]
-        f0 = flow[at, :]
-        slope = [
-            flow[around[0], :] - flow[around[1], :],
-            flow[around[2], :] - flow[around[3], :],
-            up(f0) - down(f0),
-        ]
-        is_fixed = fix[at, :] > 0.5
-        load = ld[at, :]
-        squares = None
-        for c in range(3):
-            u0 = src[c, at, :]
-            un = [src[c, a, :] for a in around] + [up(u0), down(u0)]
-            res = slope[c] - weight * u0
-            for f, n in zip(faces, un):
-                res = res + f * n
-            relaxed = u0 + (res * 0.6) / (weight + pairs[c])
-            dst[c, at, :] = jnp.where(is_fixed, load * w[c], relaxed)
-            squares = res * res if squares is None else squares + res * res
-        return acc + jnp.where(own_free[at, :] > 0.5, squares, 0.0)
-
-    def pass_damage(i, r, t, c):
-        at = pl.ds(r, 8)
-        g = []
-        for k in range(3):
-            v = dst[k, at, :]
-            g.append(
+def up(v, outside=0.0):
+    lane = lax.broadcasted_iota(jnp.int32, v.shape, 1)
+    return jnp.where(lane == 127, outside, pltpu.roll(v, 127, 1))
+
+
+def down(v, outside=0.0):
+    lane = lax.broadcasted_iota(jnp.int32, v.shape, 1)
+    return jnp.where(lane == 0, outside, pltpu.roll(v, 1, 1))
+
+
+def put_state(ref, f, at, v):
+    ref[f, at, :] = v
+    plus, minus = ((4 + f, 7 + f) if f < 3 else (10, 11))
+    ref[plus, at, :] = up(v)
+    ref[minus, at, :] = down(v)
+
+
+def sweep(src, dst, half, flow, flow_z, fix, ld, cr, own_free, tough, w, left):
+    def chunks(h, i):
+        base = i * YP + HALO - h
+        return [base + 8 * t for t in range(-(-(B + 2 * h) // 8))]
+
+    def flow_row(i):
+        done = []
+        for r in chunks(hd + 2, i):
+            at = pl.ds(r, 8)
+            keep = 1.0 - src[3, at, :]
+            h = keep * keep * 0.5 + 0.0005
+            div = (
+                (src[0, pl.ds(r + YP, 8), :] - src[0, pl.ds(r - YP, 8), :])
+                + (src[1, pl.ds(r + 1, 8), :] - src[1, pl.ds(r - 1, 8), :])
+                + (src[6, at, :] - src[9, at, :])
+            )
+            f = jnp.where(cr[at, :] < -0.5, 0.0, h * div)
+            half[at, :] = h
+            flow[at, :] = f
+            done.append((at, up(f) - down(f)))
+        return done
+
+    def put_flow_z(done):
+        for at, v in done:
+            flow_z[at, :] = v
+
+    def turned(ref, fields, h, i):
+        out = []
+        for r in chunks(h, i):
+            at = pl.ds(r, 8)
+            for f in fields:
+                v = ref[f, at, :]
+                plus, minus = ((4 + f, 7 + f) if f < 3 else (10, 11))
+                out.append((plus, at, up(v)))
+                out.append((minus, at, down(v)))
+        return out
+
+    def put_turned(ref, done):
+        for f, at, v in done:
+            ref[f, at, :] = v
+
+    def half_of(d):
+        keep = 1.0 - d
+        return keep * keep * 0.5 + 0.0005
+
+    def moved_row(i, acc):
+        for r in chunks(hd + 1, i):
+            at = pl.ds(r, 8)
+            around = [pl.ds(r + d, 8) for d in (YP, -YP, 1, -1)]
+            h0 = half[at, :]
+            hn = [half[a, :] for a in around] + [half_of(src[10, at, :]), half_of(src[11, at, :])]
+            pairs = [hn[0] + hn[1], hn[2] + hn[3], hn[4] + hn[5]]
+            weight = 6.0 * h0 + (pairs[0] + pairs[1] + pairs[2])
+            faces = [h0 + n for n in hn]
+            slope = [
+                flow[around[0], :] - flow[around[1], :],
+                flow[around[2], :] - flow[around[3], :],
+                flow_z[at, :],
+            ]
+            is_fixed = fix[at, :] > 0.5
+            load = ld[at, :]
+            squares = None
+            for c in range(3):
+                u0 = src[c, at, :]
+                un = [src[c, a, :] for a in around] + [src[4 + c, at, :], src[7 + c, at, :]]
+                res = slope[c] - weight * u0
+                for f, n in zip(faces, un):
+                    res = res + f * n
+                relaxed = u0 + (res * 0.6) / (weight + pairs[c])
+                dst[c, at, :] = jnp.where(is_fixed, load * w[c], relaxed)
+                squares = res * res if squares is None else squares + res * res
+            acc = acc + jnp.where(own_free[at, :] > 0.5, squares, 0.0)
+        return acc
+
+    def damage_row(i):
+        for t, r in enumerate(chunks(hd, i)):
+            at = pl.ds(r, 8)
+            g = [
                 (
                     dst[k, pl.ds(r + YP, 8), :] - dst[k, pl.ds(r - YP, 8), :],
                     dst[k, pl.ds(r + 1, 8), :] - dst[k, pl.ds(r - 1, 8), :],
-                    up(v) - down(v),
+                    dst[4 + k, at, :] - dst[7 + k, at, :],
                 )
+                for k in range(3)
+            ]
+            total = g[0][0] + g[1][1] + g[2][2]
+            third = total * (1.0 / 3.0)
+            dx, dy, dz = g[0][0] - third, g[1][1] - third, g[2][2] - third
+            xy, xz, yz = g[0][1] + g[1][0], g[0][2] + g[2][0], g[1][2] + g[2][1]
+            xy2, xz2, yz2 = xy * xy, xz * xz, yz * yz
+            spread = (dx * dx + dy * dy + dz * dz) + 0.5 * (xy2 + xz2 + yz2)
+            det = dx * dy * dz + 0.25 * (xy * xz * yz - (dx * yz2 + dy * xz2 + dz * xy2))
+            s6 = spread * (1.0 / 24.0)
+            inv = lax.rsqrt(s6 + 1e-08)
+            ratio = (det * 0.0625) * (inv * inv * inv)
+            radius = s6 * lax.rsqrt(jnp.maximum(s6, 1e-37))
+            wq = jnp.maximum(0.5 - 0.5 * jnp.abs(ratio), 0.0)
+            cos = horner(COS_THIRD, wq)
+            sin = (wq * lax.rsqrt(jnp.maximum(wq, 1e-37))) * horner(SIN_THIRD, wq)
+            signed = jnp.where(ratio < 0.0, -radius, radius)
+            a, b = signed * cos, signed * sin
+            mean = total * (1.0 / 6.0)
+            l1, rest = mean + 2.0 * a, mean - a
+            p1 = jnp.maximum(l1, 0.0)
+            p2 = jnp.maximum(rest + b, 0.0)
+            p3 = jnp.maximum(rest - b, 0.0)
+            trace = jnp.maximum(total, 0.0)
+            psi2 = 0.25 * (trace * trace) + 2.0 * (p1 * p1 + p2 * p2 + p3 * p3)
+            beside = (
+                (src[3, pl.ds(r + YP, 8), :] + src[3, pl.ds(r - YP, 8), :])
+                + (src[3, pl.ds(r + 1, 8), :] + src[3, pl.ds(r - 1, 8), :])
+                + (src[10, at, :] + src[11, at, :])
             )
-        total = g[0][0] + g[1][1] + g[2][2]
-        third = total * (1.0 / 3.0)
-        dx, dy, dz = g[0][0] - third, g[1][1] - third, g[2][2] - third
-        xy, xz, yz = g[0][1] + g[1][0], g[0][2] + g[2][0], g[1][2] + g[2][1]
-        xy2, xz2, yz2 = xy * xy, xz * xz, yz * yz
-        spread = (dx * dx + dy * dy + dz * dz) + 0.5 * (xy2 + xz2 + yz2)
-        det = dx * dy * dz + 0.25 * (xy * xz * yz - (dx * yz2 + dy * xz2 + dz * xy2))
-        s6 = spread * (1.0 / 24.0)
-        inv = lax.rsqrt(s6 + 1e-08)
-        ratio = (det * 0.0625) * (inv * inv * inv)
-        radius = s6 * lax.rsqrt(jnp.maximum(s6, 1e-37))
-        wq = jnp.maximum(0.5 - 0.5 * jnp.abs(ratio), 0.0)
-        cos = horner(COS_THIRD, wq)
-        sin = (wq * lax.rsqrt(jnp.maximum(wq, 1e-37))) * horner(SIN_THIRD, wq)
-        signed = jnp.where(ratio < 0.0, -radius, radius)
-        a, b = signed * cos, signed * sin
-        mean = total * (1.0 / 6.0)
-        l1, rest = mean + 2.0 * a, mean - a
-        p1, p2, p3 = jnp.maximum(l1, 0.0), jnp.maximum(rest + b, 0.0), jnp.maximum(rest - b, 0.0)
-        trace = jnp.maximum(total, 0.0)
-        psi2 = 0.25 * (trace * trace) + 2.0 * (p1 * p1 + p2 * p2 + p3 * p3)
-        d0 = src[3, at, :]
-        beside = (
-            (src[3, pl.ds(r + YP, 8), :] + src[3, pl.ds(r - YP, 8), :])
-            + (src[3, pl.ds(r + 1, 8), :] + src[3, pl.ds(r - 1, 8), :])
-            + (up(d0) + down(d0))
-        )
-        gc = tough[pl.ds(i * (B + 2 * hd) + 8 * t, 8), :]
-        new = (psi2 + gc * beside) / (psi2 + 7.0 * gc)
-        kind = cr[at, :]
-        dst[3, at, :] = jnp.where(kind > 0.5, 1.0, jnp.where(kind < -0.5, 0.0, new))
+            gc = tough[pl.ds((i - (HALO - hd)) * (B + 2 * hd) + 8 * t, 8), :]
+            new = (psi2 + gc * beside) / (psi2 + 7.0 * gc)
+            kind = cr[at, :]
+            dst[3, at, :] = jnp.where(kind > 0.5, 1.0, jnp.where(kind < -0.5, 0.0, new))
+
+    hd = 2 * left
+    hm = hd + 1
+
+    def first_loop(i, acc):
+        later = turned(dst, range(3), hm, i - 1)
+        flow_later = flow_row(i + 1)
+        acc = moved_row(i, acc)
+        put_turned(dst, later)
+        put_flow_z(flow_later)
+        return acc
+
+    def second_loop(i, c):
+        later = turned(dst, (3,), hd, i - 1) if left else ()
+        damage_row(i)
+        put_turned(dst, later)
         return c
 
-    hd = 2 * left
-    over(hd + 2, pass_flow)
-    acc = over(hd + 1, pass_moved, jnp.zeros((8, 128), f32))
-    over(hd, pass_damage)
+    low, high = HALO - hm, HALO + B + hm
+    put_flow_z(flow_row(low - 1))
+    put_flow_z(flow_row(low))
+    acc = lax.fori_loop(low, high, first_loop, jnp.zeros((8, 128), f32))
+    put_turned(dst, turned(dst, range(3), hm, high - 1))
+    low, high = HALO - hd, HALO + B + hd
+    lax.fori_loop(low, high, second_loop, 0)
+    if left:
+        put_turned(dst, turned(dst, (3,), hd, high - 1))
     return acc
 
 
@@ -340,7 +395,7 @@
         (state_out,) = take(1)
         slab_outs = take(4)
         (sums_out,) = take(1)
-    half, flow, *bufs = refs
+    half, flow, flow_z, *bufs = refs
     if group > 0:
         src = bufs[2]
 
@@ -350,7 +405,7 @@
         def put(f):
             def one(x, y, v, outside):
                 v = v if outside is None else jnp.where(outside, 0.0, v)
-                src[f, pl.ds(row(x, y), v.shape[0]), :] = v
+                put_state(src, f, pl.ds(row(x, y), v.shape[0]), v)
 
             return one
 
@@ -361,7 +416,7 @@
     start = sum(GROUPS[:group])
     for j in range(k):
         dst = bufs[j % 2]
-        acc = sweep(src, dst, half, flow, fix, ld, cr, own_free, tough[j], w, k - 1 - j)
+        acc = sweep(src, dst, half, flow, flow_z, fix, ld, cr, own_free, tough[j], w, k - 1 - j)
         sums = add_sum(sums, acc, start + j)
         src = dst
     if final:
@@ -400,7 +455,7 @@
         out_specs=[VMEM] * len(shapes),
         scratch_shapes=list(scratch),
         name=name,
-        compiler_params=pltpu.CompilerParams(vmem_limit_bytes=24 * 1024 * 1024),
+        compiler_params=pltpu.CompilerParams(vmem_limit_bytes=32 * 1024 * 1024),
         cost_estimate=pl.CostEstimate(
             flops=int(us * 4e6), bytes_accessed=int(us * 1e6), transcendentals=0
         ),
@@ -446,7 +501,7 @@
     ext = (ROWS, 128)
     made = call(
         functools.partial(first_kernel, sides), "first",
-        [(4,) + ext, ext, ext, ext, ext] + [(rows_of(h), 128) for h in sides],
+        [(12,) + ext, ext, ext, ext, ext] + [(rows_of(h), 128) for h in sides],
         [place, load_table, *raw, *received, *corners], smem=2, us=1.0,
     )
     state, kinds = made[0], made[1:5]
@@ -471,7 +526,7 @@
         else:
             n = slab_rows(state_widths(GROUPS[g + 1]))
             outs = [(4, B, B, 128)] + [(n, 128)] * 4 + [(1, 128)]
-        scratch = [pltpu.VMEM(ext, f32)] * 2 + [pltpu.VMEM((4,) + ext, f32)] * (2 + (g > 0))
+        scratch = [pltpu.VMEM(ext, f32)] * 3 + [pltpu.VMEM((12,) + ext, f32)] * (2 + (g > 0))
         res = call(
             functools.partial(group_kernel, g), f"group_{g}", outs, ins, scratch, smem=2, us=13.0
         )

time: 162 us -> 138 us (0.85)
  Pallas kernels: 71.2 us -> 47.1 us
    pallas_call x7, Pallas kernels: 71.2 us -> 47.1 us  [call(): pl.pallas_call(kernel, out_shape=[jax.ShapeDtypeStruct(s, f32) for s in s...]
where the time goes in v2:
time: 138 us
  Pallas kernels  47.1 us (34%)
  waiting for transfers between devices  38.2 us (28%)
  starting transfers between devices  25.8 us (19%)
  blocking collectives  17.3 us (13%)
  local copies, waits for them, and re-layouts  8.08 us (6%)
    pallas_call x7, Pallas kernels, call(): pl.pallas_call(kernel, out_shape=[jax.ShapeDtypeStruct(s, f32) for s in s...  47.1 us
    ppermute x19, waiting for transfers between devices, shift(): return lax.ppermute(x, axis, [(i, (i + by) % n) for i in range(n)])  38.2 us
    ppermute x19, starting transfers between devices, shift(): return lax.ppermute(x, axis, [(i, (i + by) % n) for i in range(n)])  25.8 us
    all_to_all x1, blocking collectives, on_device(): parts = lax.all_to_all(parts, ('gx', 'gy'), 0, 0, tiled=True)  17.3 us
    unnamed x17, local copies, waits for them, and re-layouts  8 us
  transfers between devices with their start and end apart: 19, of which 9 were waited for; matrix products, arithmetic and copies ran while one was open for 1% of the time, Pallas kernels for 0%

profile of v2, /device:TPU:2, one launch (start us, length us, event | category | flops | bytes accessed | tf_op | source)
XLA Modules:
  0.0 137.8 jit_solution(15371022269207947846)
XLA Ops:
  0.6 0.0 copy-start
  0.6 0.9 copy-done
  1.5 0.9 copy-done.2
  2.4 0.9 copy-done.4
  3.3 0.9 copy-done.6
  4.3 0.1 first_pack.1
  4.3 2.0 %collective-permute-start = (f32[480,128]{1,0:T(8,128)S(1)}, f32[480,128]{1,0:T(8,128)S(1)}, u32[]{:S(2)}, u32[]{:S(2)}) collective-permute-start(f32[480,128]{1,0:T(8,128)S(1)} %get-tuple-element.28), channel_id=1, source_target_pairs={{0,4},{4,8},{8,12},{12,16},{16,20},{20,24},{24,28},{28,0},{1,5},{5... | collective-permute-start | bytes 737288 | tf_op jit(solution)/shard_map/ppermute | solution.py:468
  6.3 4.0 %collective-permute-start.1 = (f32[480,128]{1,0:T(8,128)S(1)}, f32[480,128]{1,0:T(8,128)S(1)}, u32[]{:S(2)}, u32[]{:S(2)}) collective-permute-start(f32[480,128]{1,0:T(8,128)S(1)} %get-tuple-element.29), channel_id=1, source_target_pairs={{0,28},{4,0},{8,4},{12,8},{16,12},{20,16},{24,20},{28,24},{1,29},{... | collective-permute-start | bytes 737288 | tf_op jit(solution)/shard_map/ppermute | solution.py:468
  10.4 1.5 %collective-permute-start.2 = (f32[480,128]{1,0:T(8,128)S(1)}, f32[480,128]{1,0:T(8,128)S(1)}, u32[]{:S(2)}, u32[]{:S(2)}) collective-permute-start(f32[480,128]{1,0:T(8,128)S(1)} %get-tuple-element.30), channel_id=1, source_target_pairs={{0,1},{1,2},{2,3},{3,0},{4,5},{5,6},{6,7},{7,4},{8,9},{9,10},{10,1... | collective-permute-start | bytes 737288 | tf_op jit(solution)/shard_map/ppermute | solution.py:468
  11.9 0.5 collective-permute-start.3
  12.4 3.8 %collective-permute-done.xlo = f32[480,128]{1,0:T(8,128)S(1)} collective-permute-done((f32[480,128]{1,0:T(8,128)S(1)}, f32[480,128]{1,0:T(8,128)S(1)}, u32[]{:S(2)}, u32[]{:S(2)}) %collective-permute-start) | collective-permute-done | bytes 245792 | tf_op jit(solution)/shard_map/ppermute | solution.py:468
  16.2 0.0 collective-permute-done.1.xhi
  16.3 1.6 %collective-permute-start.4 = (f32[200,128]{1,0:T(8,128)S(1)}, f32[200,128]{1,0:T(8,128)S(1)}, u32[]{:S(2)}, u32[]{:S(2)}) collective-permute-start(f32[200,128]{1,0:T(8,128)S(1)} %get-tuple-element.32), channel_id=1, source_target_pairs={{0,1},{1,2},{2,3},{3,0},{4,5},{5,6},{6,7},{7,4},{8,9},{9,10},{10,1... | collective-permute-start | bytes 307208 | tf_op jit(solution)/shard_map/ppermute | solution.py:468
  17.8 0.5 collective-permute-start.5
  19.0 0.8 copy.14.table.refs_1_
  19.8 0.1 stack.15.place.refs_0_
  19.9 0.0 collective-permute-done.3.yhi
  19.9 1.1 collective-permute-done.4.clo
  21.0 1.5 %collective-permute-done.5.chi = f32[200,128]{1,0:T(8,128)S(1)} collective-permute-done((f32[200,128]{1,0:T(8,128)S(1)}, f32[200,128]{1,0:T(8,128)S(1)}, u32[]{:S(2)}, u32[]{:S(2)}) %collective-permute-start.5) | collective-permute-done | bytes 102432 | tf_op jit(solution)/shard_map/ppermute | solution.py:468
  22.5 0.9 copy-done.1
  23.4 0.9 copy-done.3
  24.3 0.9 copy-done.5
  25.2 0.9 copy-done.7
  26.1 1.9 %first.1 = (f32[12,1176,128]{2,1,0:T(8,128)S(1)}, f32[1176,128]{1,0:T(8,128)S(1)}, f32[1176,128]{1,0:T(8,128)S(1)}, f32[1176,128]{1,0:T(8,128)S(1)}, f32[1176,12...) custom-call(s32[6]{0:T(128)S(1)} %stack.15.place.refs_0_, ...), custom_call_target="tpu_custom_call" | custom-call | flops 4000000 | bytes 1000000 | tf_op jit(solution)/shard_map/first/pallas_call | solution.py:451
  28.0 0.8 collective-permute-start.10
  28.8 2.4 %collective-permute-start.11 = (f32[408,128]{1,0:T(8,128)S(1)}, f32[408,128]{1,0:T(8,128)S(1)}, u32[]{:S(2)}, u32[]{:S(2)}) collective-permute-start(f32[408,128]{1,0:T(8,128)S(1)} %get-tuple-element.40), channel_id=1, source_target_pairs={{0,192},{32,224},{64,0},{96,32},{128,64},{160,96},{192,128},{224,1... | collective-permute-start | bytes 626696 | tf_op jit(solution)/shard_map/ppermute | solution.py:468
  31.1 0.4 collective-permute-start.12
  31.5 6.9 %collective-permute-done.12.refs_9_ = f32[256,128]{1,0:T(8,128)S(1)} collective-permute-done((f32[256,128]{1,0:T(8,128)S(1)}, f32[256,128]{1,0:T(8,128)S(1)}, u32[]{:S(2)}, u32[]{:S(2)}) %collective-permute-start.12) | collective-permute-done | bytes 131104 | tf_op jit(solution)/shard_map/ppermute | solution.py:468
  38.4 1.8 %collective-permute-done.11.refs_8_ = f32[408,128]{1,0:T(8,128)S(1)} collective-permute-done((f32[408,128]{1,0:T(8,128)S(1)}, f32[408,128]{1,0:T(8,128)S(1)}, u32[]{:S(2)}, u32[]{:S(2)}) %collective-permute-start.11) | collective-permute-done | bytes 208928 | tf_op jit(solution)/shard_map/ppermute | solution.py:468
  40.2 20.9 %group_0.1 = (f32[4,16,16,128]{3,2,1,0:T(8,128)S(1)}, f32[560,128]{1,0:T(8,128)S(1)}, f32[560,128]{1,0:T(8,128)S(1)}, f32[560,128]{1,0:T(8,128)S(1)}, f32[560,128]{1,0:T(8,128)S(1)}, /*index=5*/f32[1,128]{1,0:T(1,128)S(1)}) custom-call(s32[6]{0:T(128)S(1)} %stack.15.place.refs_0_, f32[64,3]{1,0:T(8,128)S(1)} %copy.14.table.refs_1_, ...), custom_call_target="tpu_custom_call" | custom-call | flops 52000000 | bytes 13000000 | tf_op jit(solution)/shard_map/group_0/pallas_call | solution.py:451
  61.2 0.1 collective-permute-start.13
  61.3 3.2 %collective-permute-start.14 = (f32[560,128]{1,0:T(8,128)S(1)}, f32[560,128]{1,0:T(8,128)S(1)}, u32[]{:S(2)}, u32[]{:S(2)}) collective-permute-start(f32[560,128]{1,0:T(8,128)S(1)} %get-tuple-element.44), channel_id=1, source_target_pairs={{0,28},{4,0},{8,4},{12,8},{16,12},{20,16},{24,20},{28,24},{1,29},{... | collective-permute-start | bytes 860168 | tf_op jit(solution)/shard_map/ppermute | solution.py:468
  64.5 2.8 %collective-permute-start.7 = (f32[584,128]{1,0:T(8,128)S(1)}, f32[584,128]{1,0:T(8,128)S(1)}, u32[]{:S(2)}, u32[]{:S(2)}) collective-permute-start(f32[584,128]{1,0:T(8,128)S(1)} %get-tuple-element.39), channel_id=1, source_target_pairs={{0,96},{32,128},{64,160},{96,192},{128,224},{160,0},{192,32},{224,... | collective-permute-start | bytes 897032 | tf_op jit(solution)/shard_map/ppermute | solution.py:468
  67.2 1.8 %collective-permute-start.6 = (f32[792,128]{1,0:T(8,128)S(1)}, f32[792,128]{1,0:T(8,128)S(1)}, u32[]{:S(2)}, u32[]{:S(2)}) collective-permute-start(f32[792,128]{1,0:T(8,128)S(1)} %get-tuple-element.38.refs_6_), channel_id=1, source_target_pairs={{0,128},{32,160},{64,192},{96,224},{128,0},{160,32},{192,64},{224,... | collective-permute-start | bytes 1216520 | tf_op jit(solution)/shard_map/ppermute | solution.py:468
  69.1 1.2 collective-permute-done.9.refs_9_
  70.2 0.2 collective-permute-start.8
  70.4 0.0 collective-permute-done.13.xlo.refs_11_
  70.5 1.2 collective-permute-start.15
  71.6 0.0 collective-permute-done.14.xhi.refs_12_
  71.7 0.8 collective-permute-start.16
  72.5 17.6 %collective-permute-done.8.refs_8_ = f32[408,128]{1,0:T(8,128)S(1)} collective-permute-done((f32[408,128]{1,0:T(8,128)S(1)}, f32[408,128]{1,0:T(8,128)S(1)}, u32[]{:S(2)}, u32[]{:S(2)}) %collective-permute-start.8) | collective-permute-done | bytes 208928 | tf_op jit(solution)/shard_map/ppermute | solution.py:468
  90.1 1.2 collective-permute-start.17
  91.3 0.8 collective-permute-start.18
  92.2 3.0 %collective-permute-done.17.refs_15_ = f32[272,128]{1,0:T(8,128)S(1)} collective-permute-done((f32[272,128]{1,0:T(8,128)S(1)}, f32[272,128]{1,0:T(8,128)S(1)}, u32[]{:S(2)}, u32[]{:S(2)}) %collective-permute-start.17) | collective-permute-done | bytes 139296 | tf_op jit(solution)/shard_map/ppermute | solution.py:468
  95.2 1.2 collective-permute-done.18.refs_16_
  96.4 23.0 %group_1.1 = (f32[1,3,16,16,128]{4,3,2,1,0:T(8,128)}, f32[1,16,16,128]{3,2,1,0:T(8,128)}, f32[32,128]{1,0:T(8,128)S(1)}) custom-call(s32[6]{0:T(128)S(1)} %stack.15.place.refs_0_, f32[64,3]{1,0:T(8,128)S(1)} %copy.14.table.refs_1_, f32[1176,128]{1,0:T(8,128)S(1)} %get-tuple-element.34.refs_2_, f32[1176,128]{1,0:T(8,128)S(1)} %get-tuple-element.35.refs_3_, ...), custom_call_target="tpu_custom_call" | custom-call | flops 52000000 | bytes 13000000 | tf_op jit(solution)/shard_map/group_1/pallas_call | solution.py:451
  119.4 17.3 %all_to_all.11 = f32[32,1,128]{2,1,0:T(1,128)S(1)} all-to-all(f32[32,1,128]{2,1,0:T(1,128)S(1)} %bitcast.11), channel_id=1, replica_groups=mesh['section'=8,'gx'=8,'gy'=4] {'gx','gy'}, dimensions={0} | all-to-all | bytes 32768 | tf_op jit(solution)/shard_map/all_to_all | solution.py:537
  136.7 1.1 table.2
  (16 shorter events, 0.1 us)
Async XLA Ops:
  0.6 0.9 copy-start
  1.5 0.9 copy-start.2
  2.4 0.9 copy-start.4
  3.3 0.9 copy-start.6
  4.3 11.9 %collective-permute-start = (f32[480,128]{1,0:T(8,128)S(1)}, f32[480,128]{1,0:T(8,128)S(1)}, u32[]{:S(2)}, u32[]{:S(2)}) collective-permute-start(f32[480,128]{1,0:T(8,128)S(1)} %get-tuple-element.28), channel_id=1, source_target_pairs={{0,4},{4,8},{8,12},{12,16},{16,20},{20,24},{24,28},{28,0},{1,5},{5... | collective-permute-start | bytes 737288 | tf_op jit(solution)/shard_map/ppermute | solution.py:468
  6.3 9.9 %collective-permute-start.1 = (f32[480,128]{1,0:T(8,128)S(1)}, f32[480,128]{1,0:T(8,128)S(1)}, u32[]{:S(2)}, u32[]{:S(2)}) collective-permute-start(f32[480,128]{1,0:T(8,128)S(1)} %get-tuple-element.29), channel_id=1, source_target_pairs={{0,28},{4,0},{8,4},{12,8},{16,12},{20,16},{24,20},{28,24},{1,29},{... | collective-permute-start | bytes 737288 | tf_op jit(solution)/shard_map/ppermute | solution.py:468
  10.4 9.5 %collective-permute-start.2 = (f32[480,128]{1,0:T(8,128)S(1)}, f32[480,128]{1,0:T(8,128)S(1)}, u32[]{:S(2)}, u32[]{:S(2)}) collective-permute-start(f32[480,128]{1,0:T(8,128)S(1)} %get-tuple-element.30), channel_id=1, source_target_pairs={{0,1},{1,2},{2,3},{3,0},{4,5},{5,6},{6,7},{7,4},{8,9},{9,10},{10,1... | collective-permute-start | bytes 737288 | tf_op jit(solution)/shard_map/ppermute | solution.py:468
  11.9 8.0 %collective-permute-start.3 = (f32[480,128]{1,0:T(8,128)S(1)}, f32[480,128]{1,0:T(8,128)S(1)}, u32[]{:S(2)}, u32[]{:S(2)}) collective-permute-start(f32[480,128]{1,0:T(8,128)S(1)} %get-tuple-element.31), channel_id=1, source_target_pairs={{0,3},{1,0},{2,1},{3,2},{4,7},{5,4},{6,5},{7,6},{8,11},{9,8},{10,9... | collective-permute-start | bytes 737288 | tf_op jit(solution)/shard_map/ppermute | solution.py:468
  16.3 4.7 %collective-permute-start.4 = (f32[200,128]{1,0:T(8,128)S(1)}, f32[200,128]{1,0:T(8,128)S(1)}, u32[]{:S(2)}, u32[]{:S(2)}) collective-permute-start(f32[200,128]{1,0:T(8,128)S(1)} %get-tuple-element.32), channel_id=1, source_target_pairs={{0,1},{1,2},{2,3},{3,0},{4,5},{5,6},{6,7},{7,4},{8,9},{9,10},{10,1... | collective-permute-start | bytes 307208 | tf_op jit(solution)/shard_map/ppermute | solution.py:468
  17.8 4.7 %collective-permute-start.5 = (f32[200,128]{1,0:T(8,128)S(1)}, f32[200,128]{1,0:T(8,128)S(1)}, u32[]{:S(2)}, u32[]{:S(2)}) collective-permute-start(f32[200,128]{1,0:T(8,128)S(1)} %get-tuple-element.33), channel_id=1, source_target_pairs={{0,3},{1,0},{2,1},{3,2},{4,7},{5,4},{6,5},{7,6},{8,11},{9,8},{10,9... | collective-permute-start | bytes 307208 | tf_op jit(solution)/shard_map/ppermute | solution.py:468
  22.5 0.9 copy-start.1
  23.4 0.9 copy-start.3
  24.3 0.9 copy-start.5
  25.2 0.9 copy-start.7
  28.0 12.2 %collective-permute-start.10 = (f32[584,128]{1,0:T(8,128)S(1)}, f32[584,128]{1,0:T(8,128)S(1)}, u32[]{:S(2)}, u32[]{:S(2)}) collective-permute-start(f32[584,128]{1,0:T(8,128)S(1)} %get-tuple-element.39), channel_id=1, source_target_pairs={{0,224},{32,0},{64,32},{96,64},{128,96},{160,128},{192,160},{224,1... | collective-permute-start | bytes 897032 | tf_op jit(solution)/shard_map/ppermute | solution.py:468
  28.8 11.4 %collective-permute-start.11 = (f32[408,128]{1,0:T(8,128)S(1)}, f32[408,128]{1,0:T(8,128)S(1)}, u32[]{:S(2)}, u32[]{:S(2)}) collective-permute-start(f32[408,128]{1,0:T(8,128)S(1)} %get-tuple-element.40), channel_id=1, source_target_pairs={{0,192},{32,224},{64,0},{96,32},{128,64},{160,96},{192,128},{224,1... | collective-permute-start | bytes 626696 | tf_op jit(solution)/shard_map/ppermute | solution.py:468
  31.1 7.3 %collective-permute-start.12 = (f32[256,128]{1,0:T(8,128)S(1)}, f32[256,128]{1,0:T(8,128)S(1)}, u32[]{:S(2)}, u32[]{:S(2)}) collective-permute-start(f32[256,128]{1,0:T(8,128)S(1)} %bitcast.8), channel_id=1, source_target_pairs={{0,160},{32,192},{64,224},{96,0},{128,32},{160,64},{192,96},{224,1... | collective-permute-start | bytes 393224 | tf_op jit(solution)/shard_map/ppermute | solution.py:468
  61.2 9.3 %collective-permute-start.13 = (f32[560,128]{1,0:T(8,128)S(1)}, f32[560,128]{1,0:T(8,128)S(1)}, u32[]{:S(2)}, u32[]{:S(2)}) collective-permute-start(f32[560,128]{1,0:T(8,128)S(1)} %get-tuple-element.43), channel_id=1, source_target_pairs={{0,4},{4,8},{8,12},{12,16},{16,20},{20,24},{24,28},{28,0},{1,5},{5... | collective-permute-start | bytes 860168 | tf_op jit(solution)/shard_map/ppermute | solution.py:468
  61.3 10.4 %collective-permute-start.14 = (f32[560,128]{1,0:T(8,128)S(1)}, f32[560,128]{1,0:T(8,128)S(1)}, u32[]{:S(2)}, u32[]{:S(2)}) collective-permute-start(f32[560,128]{1,0:T(8,128)S(1)} %get-tuple-element.44), channel_id=1, source_target_pairs={{0,28},{4,0},{8,4},{12,8},{16,12},{20,16},{24,20},{28,24},{1,29},{... | collective-permute-start | bytes 860168 | tf_op jit(solution)/shard_map/ppermute | solution.py:468
  64.5 5.8 %collective-permute-start.9 = (f32[256,128]{1,0:T(8,128)S(1)}, f32[256,128]{1,0:T(8,128)S(1)}, u32[]{:S(2)}, u32[]{:S(2)}) collective-permute-start(f32[256,128]{1,0:T(8,128)S(1)} %bitcast.9), channel_id=1, source_target_pairs={{0,32},{32,64},{64,96},{96,128},{128,160},{160,192},{192,224},{224... | collective-permute-start | bytes 393224 | tf_op jit(solution)/shard_map/ppermute | solution.py:468
  64.5 26.8 %collective-permute-start.7 = (f32[584,128]{1,0:T(8,128)S(1)}, f32[584,128]{1,0:T(8,128)S(1)}, u32[]{:S(2)}, u32[]{:S(2)}) collective-permute-start(f32[584,128]{1,0:T(8,128)S(1)} %get-tuple-element.39), channel_id=1, source_target_pairs={{0,96},{32,128},{64,160},{96,192},{128,224},{160,0},{192,32},{224,... | collective-permute-start | bytes 897032 | tf_op jit(solution)/shard_map/ppermute | solution.py:468
  67.2 24.9 %collective-permute-start.6 = (f32[792,128]{1,0:T(8,128)S(1)}, f32[792,128]{1,0:T(8,128)S(1)}, u32[]{:S(2)}, u32[]{:S(2)}) collective-permute-start(f32[792,128]{1,0:T(8,128)S(1)} %get-tuple-element.38.refs_6_), channel_id=1, source_target_pairs={{0,128},{32,160},{64,192},{96,224},{128,0},{160,32},{192,64},{224,... | collective-permute-start | bytes 1216520 | tf_op jit(solution)/shard_map/ppermute | solution.py:468
  70.2 19.9 %collective-permute-start.8 = (f32[408,128]{1,0:T(8,128)S(1)}, f32[408,128]{1,0:T(8,128)S(1)}, u32[]{:S(2)}, u32[]{:S(2)}) collective-permute-start(f32[408,128]{1,0:T(8,128)S(1)} %get-tuple-element.40), channel_id=1, source_target_pairs={{0,64},{32,96},{64,128},{96,160},{128,192},{160,224},{192,0},{224,... | collective-permute-start | bytes 626696 | tf_op jit(solution)/shard_map/ppermute | solution.py:468
  70.5 21.7 %collective-permute-start.15 = (f32[560,128]{1,0:T(8,128)S(1)}, f32[560,128]{1,0:T(8,128)S(1)}, u32[]{:S(2)}, u32[]{:S(2)}) collective-permute-start(f32[560,128]{1,0:T(8,128)S(1)} %get-tuple-element.45), channel_id=1, source_target_pairs={{0,1},{1,2},{2,3},{3,0},{4,5},{5,6},{6,7},{7,4},{8,9},{9,10},{10,1... | collective-permute-start | bytes 860168 | tf_op jit(solution)/shard_map/ppermute | solution.py:468
  71.7 20.5 %collective-permute-start.16 = (f32[560,128]{1,0:T(8,128)S(1)}, f32[560,128]{1,0:T(8,128)S(1)}, u32[]{:S(2)}, u32[]{:S(2)}) collective-permute-start(f32[560,128]{1,0:T(8,128)S(1)} %get-tuple-element.46), channel_id=1, source_target_pairs={{0,3},{1,0},{2,1},{3,2},{4,7},{5,4},{6,5},{7,6},{8,11},{9,8},{10,9... | collective-permute-start | bytes 860168 | tf_op jit(solution)/shard_map/ppermute | solution.py:468
  90.1 5.1 %collective-permute-start.17 = (f32[272,128]{1,0:T(8,128)S(1)}, f32[272,128]{1,0:T(8,128)S(1)}, u32[]{:S(2)}, u32[]{:S(2)}) collective-permute-start(f32[272,128]{1,0:T(8,128)S(1)} %get-tuple-element.47), channel_id=1, source_target_pairs={{0,1},{1,2},{2,3},{3,0},{4,5},{5,6},{6,7},{7,4},{8,9},{9,10},{10,1... | collective-permute-start | bytes 417800 | tf_op jit(solution)/shard_map/ppermute | solution.py:468
  91.3 5.1 %collective-permute-start.18 = (f32[272,128]{1,0:T(8,128)S(1)}, f32[272,128]{1,0:T(8,128)S(1)}, u32[]{:S(2)}, u32[]{:S(2)}) collective-permute-start(f32[272,128]{1,0:T(8,128)S(1)} %get-tuple-element.48), channel_id=1, source_target_pairs={{0,3},{1,0},{2,1},{3,2},{4,7},{5,4},{6,5},{7,6},{8,11},{9,8},{10,9... | collective-permute-start | bytes 417800 | tf_op jit(solution)/shard_map/ppermute | solution.py:468

commit v3 on v2

--- a/solution.py
+++ b/solution.py
@@ -11,8 +11,7 @@
 B = 16
 HALO = 2 * max(GROUPS) + 1
 YP = B + 2 * HALO
-ROWS = -(-(YP * YP + 16) // 8) * 8
-H_OUT = 0.5 * (1.0 + 0.001)
+ROWS = -(-(YP * (YP + 1) + 32) // 8) * 8
 
 COS_THIRD = (
     1.000000008260009, -0.22222426779181312, -0.06576120509434145, -0.035390736331322045,
@@ -24,6 +23,7 @@
 )
 
 ROUNDS = sum(GROUPS)
+SEGMENTS = ((0, 0, 1), (0, 1, 4), (1, 0, 4))
 PLACES = [(g, j) for g, k in enumerate(GROUPS) for j in range(k)]
 T_HALO = [2 * (GROUPS[g] - 1 - j) for g, j in PLACES]
 T_MAX = max(T_HALO)
@@ -90,7 +90,7 @@
         off += B * h
 
 
-def unpack(own, slabs, corners, widths, edges, stores, reach=None):
+def unpack(own, slabs, corners, widths, edges, stores):
     xlo, xhi, ylo, yhi = slabs
     clo, chi = corners
     exlo, exhi, eylo, eyhi = edges
@@ -123,37 +123,24 @@
     return gx == 0, gx == place[2] - 1, gy == 0, gy == place[3] - 1
 
 
-def first_pack_kernel(clamp, load, crack, tough, *outs):
-    def own(ref):
-        return lambda x, y, n: ref[x, pl.ds(y, n), :].astype(f32)
-
-    def fixed(x, y, n):
-        return jnp.maximum(clamp[x, pl.ds(y, n), :], load[x, pl.ds(y, n), :]).astype(f32)
-
-    readers = (fixed, own(load), own(crack), lambda x, y, n: tough[0, x, pl.ds(y, n), :])
-    pack_slabs(readers, mask_widths(), outs)
+def first_pack_kernel(own, *outs):
+    pack_slabs(own_readers(own), mask_widths(), outs)
+
+
+def own_readers(own):
+    return [lambda x, y, n, f=f: own[f, x, pl.ds(y, n), :] for f in range(4)]
 
 
 def row(x, y):
     return (x + HALO) * YP + y + HALO
 
 
-def load_vector(place, table):
-    return [table[place[4], i] for i in range(3)]
-
-
 def first_kernel(
-    sides, place, table, clamp, load, crack, tough, xlo, xhi, ylo, yhi, clo, chi,
+    sides, place, vector, own, xlo, xhi, ylo, yhi, clo, chi,
     state, fix, ld, cr, own_free, *tough_outs,
 ):
-    w = load_vector(place, table)
+    w = [vector[i] for i in range(3)]
     edges = edges_of(place)
-
-    def own(ref):
-        return lambda x, y, n: ref[x, pl.ds(y, n), :].astype(f32)
-
-    def fixed(x, y, n):
-        return jnp.maximum(clamp[x, pl.ds(y, n), :], load[x, pl.ds(y, n), :]).astype(f32)
 
     def choose(outside, value, other):
         return value if outside is None else jnp.where(outside, other, value)
@@ -188,8 +175,7 @@
 
     own_free[...] = jnp.zeros_like(own_free)
     unpack(
-        (fixed, own(load), own(crack), lambda x, y, n: tough[0, x, pl.ds(y, n), :]),
-        (xlo, xhi, ylo, yhi), (clo, chi), mask_widths(), edges,
+        own_readers(own), (xlo, xhi, ylo, yhi), (clo, chi), mask_widths(), edges,
         (put_fixed, put_load, put_crack, put_tough),
     )
 
@@ -219,12 +205,14 @@
 
 
 def sweep(src, dst, half, flow, flow_z, fix, ld, cr, own_free, tough, w, left):
+    hd = 2 * left
+    hm = hd + 1
+
     def chunks(h, i):
         base = i * YP + HALO - h
         return [base + 8 * t for t in range(-(-(B + 2 * h) // 8))]
 
     def flow_row(i):
-        done = []
         for r in chunks(hd + 2, i):
             at = pl.ds(r, 8)
             keep = 1.0 - src[3, at, :]
@@ -234,11 +222,16 @@
                 + (src[1, pl.ds(r + 1, 8), :] - src[1, pl.ds(r - 1, 8), :])
                 + (src[6, at, :] - src[9, at, :])
             )
-            f = jnp.where(cr[at, :] < -0.5, 0.0, h * div)
             half[at, :] = h
-            flow[at, :] = f
-            done.append((at, up(f) - down(f)))
-        return done
+            flow[at, :] = jnp.where(cr[at, :] < -0.5, 0.0, h * div)
+
+    def turned_flow(i):
+        out = []
+        for r in chunks(hm, i):
+            at = pl.ds(r, 8)
+            v = flow[at, :]
+            out.append((at, up(v) - down(v)))
+        return out
 
     def put_flow_z(done):
         for at, v in done:
@@ -336,32 +329,30 @@
             kind = cr[at, :]
             dst[3, at, :] = jnp.where(kind > 0.5, 1.0, jnp.where(kind < -0.5, 0.0, new))
 
-    hd = 2 * left
-    hm = hd + 1
-
-    def first_loop(i, acc):
-        later = turned(dst, range(3), hm, i - 1)
-        flow_later = flow_row(i + 1)
+    def step(i, acc, damaged):
+        later = turned(dst, range(3), hd, i - 1)
+        if damaged and left:
+            later += turned(dst, (3,), hd - 1, i - 3)
+        z_later = turned_flow(i + 1)
+        flow_row(i + 2)
         acc = moved_row(i, acc)
+        if damaged:
+            damage_row(i - 2)
         put_turned(dst, later)
-        put_flow_z(flow_later)
+        put_flow_z(z_later)
         return acc
 
-    def second_loop(i, c):
-        later = turned(dst, (3,), hd, i - 1) if left else ()
-        damage_row(i)
-        put_turned(dst, later)
-        return c
-
     low, high = HALO - hm, HALO + B + hm
-    put_flow_z(flow_row(low - 1))
-    put_flow_z(flow_row(low))
-    acc = lax.fori_loop(low, high, first_loop, jnp.zeros((8, 128), f32))
-    put_turned(dst, turned(dst, range(3), hm, high - 1))
-    low, high = HALO - hd, HALO + B + hd
-    lax.fori_loop(low, high, second_loop, 0)
-    if left:
-        put_turned(dst, turned(dst, (3,), hd, high - 1))
+    for i in (low - 1, low, low + 1):
+        flow_row(i)
+    put_flow_z(turned_flow(low))
+    acc = lax.fori_loop(
+        low, low + 3, lambda i, c: step(i, c, False), jnp.zeros((8, 128), f32)
+    )
+    acc = lax.fori_loop(low + 3, high, lambda i, c: step(i, c, True), acc)
+    later = turned(dst, (3,), hd - 1, high - 3) if left else ()
+    damage_row(high - 2)
+    put_turned(dst, later)
     return acc
 
 
@@ -370,9 +361,10 @@
     return jnp.where(lane % ROUNDS == r, jnp.sum(acc), sums)
 
 
-def group_kernel(group, *refs):
+def sweep_kernel(segment, *refs):
+    group, begin, end = segment
     k = GROUPS[group]
-    final = group == len(GROUPS) - 1
+    final = group == len(GROUPS) - 1 and end == k
     refs = list(refs)
 
     def take(n):
@@ -380,24 +372,25 @@
         del refs[:n]
         return out
 
-    place, table, fix, ld, cr, own_free = take(6)
-    tough = take(k)
-    w = load_vector(place, table)
-    if group == 0:
+    place, vector, fix, ld, cr, own_free, sums_in = take(7)
+    tough = take(end - begin)
+    w = [vector[i] for i in range(3)]
+    unpacks = group > 0 and begin == 0
+    if unpacks:
+        state, xlo, xhi, ylo, yhi, clo, chi = take(7)
+    else:
         (src,) = take(1)
-        sums = jnp.zeros((1, 128), f32)
-    else:
-        state, xlo, xhi, ylo, yhi, clo, chi, sums_in = take(8)
-        sums = sums_in[...]
     if final:
-        moved_out, damage_out, sums_out = take(3)
-    else:
+        moved_out, damage_out = take(2)
+    elif end == k:
         (state_out,) = take(1)
         slab_outs = take(4)
-        (sums_out,) = take(1)
+    else:
+        (wide_out,) = take(1)
+    (sums_out,) = take(1)
     half, flow, flow_z, *bufs = refs
-    if group > 0:
-        src = bufs[2]
+    if unpacks:
+        src = bufs[1]
 
         def own(f):
             return lambda x, y, n: state[f, x, pl.ds(y, n), :]
@@ -413,10 +406,13 @@
             [own(f) for f in range(4)], (xlo, xhi, ylo, yhi), (clo, chi), state_widths(k),
             edges_of(place), [put(f) for f in range(4)],
         )
+    sums = sums_in[...]
     start = sum(GROUPS[:group])
-    for j in range(k):
-        dst = bufs[j % 2]
-        acc = sweep(src, dst, half, flow, flow_z, fix, ld, cr, own_free, tough[j], w, k - 1 - j)
+    for j in range(begin, end):
+        dst = wide_out if j == end - 1 and end < k else bufs[j % 2]
+        acc = sweep(
+            src, dst, half, flow, flow_z, fix, ld, cr, own_free, tough[j - begin], w, k - 1 - j
+        )
         sums = add_sum(sums, acc, start + j)
         src = dst
     if final:
@@ -426,38 +422,35 @@
                 for c in range(3):
                     moved_out[0, c, x, pl.ds(s, n), :] = src[c, at, :]
                 damage_out[0, x, pl.ds(s, n), :] = src[3, at, :]
-        sums_out[...] = jnp.broadcast_to(sums, sums_out.shape)
-    else:
+    elif end == k:
         for f in range(4):
             for x in range(B):
                 for s, n in pieces(B):
                     state_out[f, x, pl.ds(s, n), :] = src[f, pl.ds(row(x, s), n), :]
-        readers = [
-            (lambda x, y, n, f=f: src[f, pl.ds(row(x, y), n), :]) for f in range(4)
-        ]
+        readers = [(lambda x, y, n, f=f: src[f, pl.ds(row(x, y), n), :]) for f in range(4)]
         pack_slabs(readers, state_widths(GROUPS[group + 1]), slab_outs)
-        sums_out[...] = sums
+    sums_out[...] = jnp.broadcast_to(sums, sums_out.shape)
 
 
 def table_kernel(scale, place, parts, out):
     total = jnp.sum(parts[...], axis=0, keepdims=True)
     root = jnp.sqrt(total * scale)
-    out[...] = pltpu.roll(jnp.broadcast_to(root, (8, 128)), place[5], 1)[:1, :ROUNDS]
-
-
-def call(kernel, name, outs, ins, scratch=(), smem=0, us=1.0):
+    out[...] = pltpu.roll(jnp.broadcast_to(root, (8, 128)), place[4], 1)[:1, :ROUNDS]
+
+
+def call(kernel, outs, ins, scratch=(), smem=0, us=1.0, limit=4):
     single = isinstance(outs, tuple)
     shapes = [outs] if single else outs
+    shapes = [s if isinstance(s, jax.ShapeDtypeStruct) else jax.ShapeDtypeStruct(s, f32) for s in shapes]
     res = pl.pallas_call(
         kernel,
-        out_shape=[jax.ShapeDtypeStruct(s, f32) for s in shapes],
+        out_shape=shapes,
         in_specs=[SMEM] * smem + [VMEM] * (len(ins) - smem),
         out_specs=[VMEM] * len(shapes),
         scratch_shapes=list(scratch),
-        name=name,
-        compiler_params=pltpu.CompilerParams(vmem_limit_bytes=32 * 1024 * 1024),
+        compiler_params=pltpu.CompilerParams(vmem_limit_bytes=limit * 1024 * 1024),
         cost_estimate=pl.CostEstimate(
-            flops=int(us * 4e6), bytes_accessed=int(us * 1e6), transcendentals=0
+            flops=int(us * 1e9), bytes_accessed=int(us * 1e6), transcendentals=0
         ),
     )(*ins)
     return res[0] if single else res
@@ -473,9 +466,9 @@
     return shift(xhi, "gx", 1), shift(xlo, "gx", -1), shift(yhi, "gy", 1), shift(ylo, "gy", -1)
 
 
-def swap_corners(xlo, xhi, widths, name):
+def swap_corners(xlo, xhi, widths):
     shape = (corner_rows(widths), 128)
-    yhi, ylo = call(functools.partial(corner_kernel, widths), name, [shape] * 2, [xlo, xhi], us=0.3)
+    yhi, ylo = call(functools.partial(corner_kernel, widths), [shape] * 2, [xlo, xhi], us=0.3)
     return shift(yhi, "gy", 1), shift(ylo, "gy", -1)
 
 
@@ -488,58 +481,76 @@
             lax.axis_index("gy").astype(jnp.int32),
             jnp.int32(nx),
             jnp.int32(ny),
-            load_index[0],
             home,
         ]
     )
-    raw = [clamp_mask, load_mask, crack_mask, toughness]
+    vector = lax.dynamic_slice(load_table, (load_index[0], 0), (1, 3)).reshape(3)
+    own = jnp.stack(
+        [
+            jnp.maximum(clamp_mask, load_mask).astype(f32),
+            load_mask.astype(f32),
+            crack_mask.astype(f32),
+            toughness[0],
+        ]
+    )
+    own = lax.optimization_barrier(own)
     widths = mask_widths()
-    slabs = call(first_pack_kernel, "first_pack", [(slab_rows(widths), 128)] * 4, raw, us=0.5)
+    slabs = call(first_pack_kernel, [(slab_rows(widths), 128)] * 4, [own], us=0.5)
     received = swap_sides(slabs)
-    corners = swap_corners(received[0], received[1], widths, "first_corners")
+    corners = swap_corners(received[0], received[1], widths)
     sides = tuple(sorted({h for h in T_HALO if h}, reverse=True))
     ext = (ROWS, 128)
     made = call(
-        functools.partial(first_kernel, sides), "first",
+        functools.partial(first_kernel, sides),
         [(12,) + ext, ext, ext, ext, ext] + [(rows_of(h), 128) for h in sides],
-        [place, load_table, *raw, *received, *corners], smem=2, us=1.0,
+        [place, vector, own, *received, *corners], smem=2, us=1.9,
     )
     state, kinds = made[0], made[1:5]
     by_halo = dict(zip(sides, made[5:]))
     by_halo[0] = toughness.reshape(B * B, 128)
-    tough = [
-        by_halo[h] if r == 0 else shift(by_halo[h], "section", -r) for r, h in enumerate(T_HALO)
-    ]
-    sums = None
-    for g, k in enumerate(GROUPS):
+    tough = []
+    for r, h in enumerate(T_HALO):
+        tough.append(by_halo[h] if r == 0 else shift(by_halo[h], "section", -r))
+    sums = jnp.zeros((1, 128), f32)
+    for segment in SEGMENTS:
+        g, begin, end = segment
+        k = GROUPS[g]
         start = sum(GROUPS[:g])
-        ins = [place, load_table, *kinds, *tough[start : start + k]]
-        if g == 0:
+        ins = [place, vector, *kinds, sums, *tough[start + begin : start + end]]
+        unpacks = g > 0 and begin == 0
+        if unpacks:
+            received = swap_sides(slabs)
+            corners = swap_corners(received[0], received[1], state_widths(k))
+            ins += [state, *received, *corners]
+        else:
             ins.append(state)
-        else:
-            received = swap_sides(slabs)
-            corners = swap_corners(received[0], received[1], state_widths(k), f"corners_{g}")
-            ins += [state, *received, *corners, sums]
-        final = g == len(GROUPS) - 1
+        final = g == len(GROUPS) - 1 and end == k
         if final:
             outs = [(1, 3, B, B, 128), (1, B, B, 128), (nx * ny, 128)]
-        else:
+        elif end == k:
             n = slab_rows(state_widths(GROUPS[g + 1]))
             outs = [(4, B, B, 128)] + [(n, 128)] * 4 + [(1, 128)]
-        scratch = [pltpu.VMEM(ext, f32)] * 3 + [pltpu.VMEM((12,) + ext, f32)] * (2 + (g > 0))
+        else:
+            outs = [(12,) + ext, (1, 128)]
+        bufs = 2 if end - begin > 1 else 0
+        scratch = [pltpu.VMEM(ext, f32)] * 3 + [pltpu.VMEM((12,) + ext, f32)] * bufs
+        cost = sum((B + 4 * (k - 1 - j)) ** 2 * 0.007 for j in range(begin, end))
         res = call(
-            functools.partial(group_kernel, g), f"group_{g}", outs, ins, scratch, smem=2, us=13.0
+            functools.partial(sweep_kernel, segment), outs, ins, scratch,
+            smem=2, us=cost, limit=4 + 8 * bufs,
         )
         if final:
             moved, damage, parts = res
+        elif end == k:
+            state, slabs, sums = res[0], res[1:5], res[5]
         else:
-            state, slabs, sums = res[0], res[1:5], res[5]
+            state, sums = res
     parts = lax.all_to_all(parts, ("gx", "gy"), 0, 0, tiled=True)
     scale = 1.0 / (3.0 * B * B * 128 * nx * ny)
-    table = call(
-        functools.partial(table_kernel, scale), "table", (1, ROUNDS), [place, parts], smem=1, us=0.1
-    )
-    return moved, damage, table
+    norms = call(
+        functools.partial(table_kernel, scale), (1, ROUNDS), [place, parts], smem=1, us=0.1
+    )
+    return moved, damage, norms
 
 
 def solution(mesh):

time: 138 us -> 116 us (0.84)
  Pallas kernels: 47.1 us -> 37 us
  waiting for transfers between devices: 38.2 us -> 30.3 us
  local copies, waits for them, and re-layouts: 8.08 us -> 0.28 us
  other arithmetic: 0 us -> 2.08 us
    pallas_call x7 -> x8, Pallas kernels: 47.1 us -> 37 us  [call(): pl.pallas_call(kernel, out_shape=shapes, in_specs=[SMEM] * smem + [VMEM]...]
    unnamed x17 -> x4, local copies, waits for them, and re-layouts: 8 us -> 0.01 us
    ppermute x19, waiting for transfers between devices: 38.2 us -> 30.3 us  [shift(): return lax.ppermute(x, axis, [(i, (i + by) % n) for i in range(n)])]
    another operation x0 -> x2, other arithmetic: none -> 2.08 us  [on_device(): jnp.stack([jnp.maximum(clamp_mask, load_mask).astype(f32), load_mask.asty...]
  transfers between devices with their start and end apart: 19 -> 19, of which waited for: 9 -> 8; matrix products, arithmetic and copies ran while one was open for 1% -> 0% of each run, Pallas kernels for 0% -> 6%
where the time goes in v3:
time: 116 us
  Pallas kernels  37 us (32%)
  waiting for transfers between devices  30.3 us (26%)
  starting transfers between devices  26.9 us (23%)
  blocking collectives  17.6 us (15%)
  other arithmetic  2.08 us (2%)
  between operations  1.39 us (1%)
    pallas_call x8, Pallas kernels, call(): pl.pallas_call(kernel, out_shape=shapes, in_specs=[SMEM] * smem + [VMEM]...  37 us
    ppermute x19, waiting for transfers between devices, shift(): return lax.ppermute(x, axis, [(i, (i + by) % n) for i in range(n)])  30.3 us
    ppermute x19, starting transfers between devices, shift(): return lax.ppermute(x, axis, [(i, (i + by) % n) for i in range(n)])  26.9 us
    all_to_all x1, blocking collectives, on_device(): parts = lax.all_to_all(parts, ('gx', 'gy'), 0, 0, tiled=True)  17.6 us
  transfers between devices with their start and end apart: 19, of which 8 were waited for; matrix products, arithmetic and copies ran while one was open for 0% of the time, Pallas kernels for 6%

profile of v3, /device:TPU:2, one launch (start us, length us, event | category | flops | bytes accessed | tf_op | source)
XLA Modules:
  0.0 115.6 jit_solution(3618089093585592195)
XLA Ops:
  0.6 0.0 copy-start
  0.6 1.1 convert_bitcast_fusion.2
  1.8 0.9 pad_maximum_fusion.own
  2.7 0.1 shard_map.85
  2.8 2.0 %collective-permute-start = (f32[480,128]{1,0:T(8,128)S(1)}, f32[480,128]{1,0:T(8,128)S(1)}, u32[]{:S(2)}, u32[]{:S(2)}) collective-permute-start(f32[480,128]{1,0:T(8,128)S(1)} %get-tuple-element.30), channel_id=1, source_target_pairs={{0,4},{4,8},{8,12},{12,16},{16,20},{20,24},{24,28},{28,0},{1,5},{5... | collective-permute-start | bytes 737288 | tf_op jit(solution)/shard_map/ppermute | solution.py:461
  4.8 4.0 %collective-permute-start.1 = (f32[480,128]{1,0:T(8,128)S(1)}, f32[480,128]{1,0:T(8,128)S(1)}, u32[]{:S(2)}, u32[]{:S(2)}) collective-permute-start(f32[480,128]{1,0:T(8,128)S(1)} %get-tuple-element.31), channel_id=1, source_target_pairs={{0,28},{4,0},{8,4},{12,8},{16,12},{20,16},{24,20},{28,24},{1,29},{... | collective-permute-start | bytes 737288 | tf_op jit(solution)/shard_map/ppermute | solution.py:461
  8.8 1.5 %collective-permute-start.2 = (f32[480,128]{1,0:T(8,128)S(1)}, f32[480,128]{1,0:T(8,128)S(1)}, u32[]{:S(2)}, u32[]{:S(2)}) collective-permute-start(f32[480,128]{1,0:T(8,128)S(1)} %get-tuple-element.32), channel_id=1, source_target_pairs={{0,1},{1,2},{2,3},{3,0},{4,5},{5,6},{6,7},{7,4},{8,9},{9,10},{10,1... | collective-permute-start | bytes 737288 | tf_op jit(solution)/shard_map/ppermute | solution.py:461
  10.3 0.5 collective-permute-start.3
  10.9 3.8 %collective-permute-done.xlo = f32[480,128]{1,0:T(8,128)S(1)} collective-permute-done((f32[480,128]{1,0:T(8,128)S(1)}, f32[480,128]{1,0:T(8,128)S(1)}, u32[]{:S(2)}, u32[]{:S(2)}) %collective-permute-start) | collective-permute-done | bytes 245792 | tf_op jit(solution)/shard_map/ppermute | solution.py:461
  14.7 0.0 collective-permute-done.1.xhi
  14.7 1.6 %collective-permute-start.4 = (f32[200,128]{1,0:T(8,128)S(1)}, f32[200,128]{1,0:T(8,128)S(1)}, u32[]{:S(2)}, u32[]{:S(2)}) collective-permute-start(f32[200,128]{1,0:T(8,128)S(1)} %get-tuple-element.34), channel_id=1, source_target_pairs={{0,1},{1,2},{2,3},{3,0},{4,5},{5,6},{6,7},{7,4},{8,9},{9,10},{10,1... | collective-permute-start | bytes 307208 | tf_op jit(solution)/shard_map/ppermute | solution.py:461
  16.3 0.5 collective-permute-start.5
  16.9 1.5 %collective-permute-start.8 = (f32[256,128]{1,0:T(8,128)}, f32[256,128]{1,0:T(8,128)S(1)}, u32[]{:S(2)}, u32[]{:S(2)}) collective-permute-start(f32[256,128]{1,0:T(8,128)} %bitcast.20), channel_id=1, source_target_pairs={{0,160},{32,192},{64,224},{96,0},{128,32},{160,64},{192,96},{224,1... | collective-permute-start | bytes 393224 | tf_op jit(solution)/shard_map/ppermute | solution.py:461
  19.0 0.2 dynamic-slice_reduce_fusion.vector.refs_1_
  19.2 0.1 stack.27.place.refs_0_
  19.3 0.0 collective-permute-done.2.ylo
  19.3 0.0 collective-permute-done.3.yhi
  19.3 0.2 collective-permute-done.4.clo
  19.5 1.5 %collective-permute-done.5.chi = f32[200,128]{1,0:T(8,128)S(1)} collective-permute-done((f32[200,128]{1,0:T(8,128)S(1)}, f32[200,128]{1,0:T(8,128)S(1)}, u32[]{:S(2)}, u32[]{:S(2)}) %collective-permute-start.5) | collective-permute-done | bytes 102432 | tf_op jit(solution)/shard_map/ppermute | solution.py:461
  21.0 1.4 %shard_map.87 = (f32[12,1224,128]{2,1,0:T(8,128)S(1)}, f32[1224,128]{1,0:T(8,128)S(1)}, f32[1224,128]{1,0:T(8,128)S(1)}, f32[1224,128]{1,0:T(8,128)S(1)}, f32[12...) custom-call(s32[5]{0:T(128)S(1)} %stack.27.place.refs_0_, ...), custom_call_target="tpu_custom_call" | custom-call | flops 1900000000 | bytes 1900000 | tf_op jit(solution)/shard_map/pallas_call | solution.py:445
  22.3 0.8 collective-permute-start.6
  23.1 2.4 %collective-permute-start.7 = (f32[408,128]{1,0:T(8,128)S(1)}, f32[408,128]{1,0:T(8,128)S(1)}, u32[]{:S(2)}, u32[]{:S(2)}) collective-permute-start(f32[408,128]{1,0:T(8,128)S(1)} %get-tuple-element.44), channel_id=1, source_target_pairs={{0,192},{32,224},{64,0},{96,32},{128,64},{160,96},{192,128},{224,1... | collective-permute-start | bytes 626696 | tf_op jit(solution)/shard_map/ppermute | solution.py:461
  25.5 5.9 %shard_map.88 = (f32[12,1224,128]{2,1,0:T(8,128)S(1)}, f32[1,128]{1,0:T(1,128)S(1)}) custom-call(s32[5]{0:T(128)S(1)} %stack.27.place.refs_0_, f32[3]{0:T(128)S(1)} %dynamic-slice_reduce_fusion.vector.refs_1_, f32[1224,128]{1,0:T(8,128)S(1)} %get-tuple-element.36.refs_2_, f32[1224,128]{1,0:T(8,128)S(1)} %get-tuple-element.37.refs_3_, ...), custom_call_target="tpu_custom_call" | custom-call | flops 5488000000 | bytes 5488000 | tf_op jit(solution)/shard_map/pallas_call | solution.py:445
  31.3 0.0 collective-permute-done.8.refs_9_
  31.3 1.8 %collective-permute-done.7.refs_8_ = f32[408,128]{1,0:T(8,128)S(1)} collective-permute-done((f32[408,128]{1,0:T(8,128)S(1)}, f32[408,128]{1,0:T(8,128)S(1)}, u32[]{:S(2)}, u32[]{:S(2)}) %collective-permute-start.7) | collective-permute-done | bytes 208928 | tf_op jit(solution)/shard_map/ppermute | solution.py:461
  33.1 0.0 collective-permute-done.6.refs_7_
  33.1 10.6 %shard_map.89 = (f32[4,16,16,128]{3,2,1,0:T(8,128)S(1)}, f32[560,128]{1,0:T(8,128)S(1)}, f32[560,128]{1,0:T(8,128)S(1)}, f32[560,128]{1,0:T(8,128)S(1)}, f32[560,128]{1,0:T(8,128)S(1)}, /*index=5*/f32[1,128]{1,0:T(1,128)S(1)}) custom-call(s32[5]{0:T(128)S(1)} %stack.27.place.refs_0_, f32[3]{0:T(128)S(1)} %dynamic-slice_reduce_fusion.vector.refs_1_, ...), custom_call_target="tpu_custom_call" | custom-call | flops 8624000000 | bytes 8624000 | tf_op jit(solution)/shard_map/pallas_call | solution.py:445
  43.7 0.1 collective-permute-start.13
  43.8 3.2 %collective-permute-start.14 = (f32[560,128]{1,0:T(8,128)S(1)}, f32[560,128]{1,0:T(8,128)S(1)}, u32[]{:S(2)}, u32[]{:S(2)}) collective-permute-start(f32[560,128]{1,0:T(8,128)S(1)} %get-tuple-element.49), channel_id=1, source_target_pairs={{0,28},{4,0},{8,4},{12,8},{16,12},{20,16},{24,20},{28,24},{1,29},{... | collective-permute-start | bytes 860168 | tf_op jit(solution)/shard_map/ppermute | solution.py:461
  47.0 0.0 collective-permute-start.12
  47.0 2.6 %collective-permute-start.10 = (f32[584,128]{1,0:T(8,128)S(1)}, f32[584,128]{1,0:T(8,128)S(1)}, u32[]{:S(2)}, u32[]{:S(2)}) collective-permute-start(f32[584,128]{1,0:T(8,128)S(1)} %get-tuple-element.43), channel_id=1, source_target_pairs={{0,96},{32,128},{64,160},{96,192},{128,224},{160,0},{192,32},{224,... | collective-permute-start | bytes 897032 | tf_op jit(solution)/shard_map/ppermute | solution.py:461
  49.6 1.8 %collective-permute-start.9 = (f32[792,128]{1,0:T(8,128)S(1)}, f32[792,128]{1,0:T(8,128)S(1)}, u32[]{:S(2)}, u32[]{:S(2)}) collective-permute-start(f32[792,128]{1,0:T(8,128)S(1)} %get-tuple-element.40.refs_7_), channel_id=1, source_target_pairs={{0,128},{32,160},{64,192},{96,224},{128,0},{160,32},{192,64},{224,... | collective-permute-start | bytes 1216520 | tf_op jit(solution)/shard_map/ppermute | solution.py:461
  51.5 1.2 %collective-permute-done.12.refs_10_ = f32[256,128]{1,0:T(8,128)S(1)} collective-permute-done((f32[256,128]{1,0:T(8,128)S(1)}, f32[256,128]{1,0:T(8,128)S(1)}, u32[]{:S(2)}, u32[]{:S(2)}) %collective-permute-start.12) | collective-permute-done | bytes 131104 | tf_op jit(solution)/shard_map/ppermute | solution.py:461
  52.6 0.4 collective-permute-start.11
  53.0 0.0 collective-permute-done.13.xlo.refs_12_
  53.0 1.2 %collective-permute-start.15 = (f32[560,128]{1,0:T(8,128)S(1)}, f32[560,128]{1,0:T(8,128)S(1)}, u32[]{:S(2)}, u32[]{:S(2)}) collective-permute-start(f32[560,128]{1,0:T(8,128)S(1)} %get-tuple-element.50), channel_id=1, source_target_pairs={{0,1},{1,2},{2,3},{3,0},{4,5},{5,6},{6,7},{7,4},{8,9},{9,10},{10,1... | collective-permute-start | bytes 860168 | tf_op jit(solution)/shard_map/ppermute | solution.py:461
  54.2 0.0 collective-permute-done.14.xhi.refs_13_
  54.2 0.8 collective-permute-start.16
  55.1 17.6 %collective-permute-done.11.refs_9_ = f32[408,128]{1,0:T(8,128)S(1)} collective-permute-done((f32[408,128]{1,0:T(8,128)S(1)}, f32[408,128]{1,0:T(8,128)S(1)}, u32[]{:S(2)}, u32[]{:S(2)}) %collective-permute-start.11) | collective-permute-done | bytes 208928 | tf_op jit(solution)/shard_map/ppermute | solution.py:461
  72.7 1.2 %collective-permute-start.17 = (f32[272,128]{1,0:T(8,128)S(1)}, f32[272,128]{1,0:T(8,128)S(1)}, u32[]{:S(2)}, u32[]{:S(2)}) collective-permute-start(f32[272,128]{1,0:T(8,128)S(1)} %get-tuple-element.52), channel_id=1, source_target_pairs={{0,1},{1,2},{2,3},{3,0},{4,5},{5,6},{6,7},{7,4},{8,9},{9,10},{10,1... | collective-permute-start | bytes 417800 | tf_op jit(solution)/shard_map/ppermute | solution.py:461
  73.9 0.0 collective-permute-done.10.refs_8_
  73.9 0.8 collective-permute-start.18
  74.7 0.0 collective-permute-done.9.refs_7_
  74.7 3.0 %collective-permute-done.17.refs_16_ = f32[272,128]{1,0:T(8,128)S(1)} collective-permute-done((f32[272,128]{1,0:T(8,128)S(1)}, f32[272,128]{1,0:T(8,128)S(1)}, u32[]{:S(2)}, u32[]{:S(2)}) %collective-permute-start.17) | collective-permute-done | bytes 139296 | tf_op jit(solution)/shard_map/ppermute | solution.py:461
  77.7 1.2 %collective-permute-done.18.refs_17_ = f32[272,128]{1,0:T(8,128)S(1)} collective-permute-done((f32[272,128]{1,0:T(8,128)S(1)}, f32[272,128]{1,0:T(8,128)S(1)}, u32[]{:S(2)}, u32[]{:S(2)}) %collective-permute-start.18) | collective-permute-done | bytes 139296 | tf_op jit(solution)/shard_map/ppermute | solution.py:461
  78.9 18.0 %shard_map.91 = (f32[1,3,16,16,128]{4,3,2,1,0:T(8,128)}, f32[1,16,16,128]{3,2,1,0:T(8,128)}, f32[32,128]{1,0:T(8,128)S(1)}) custom-call(s32[5]{0:T(128)S(1)} %stack.27.place.refs_0_, f32[3]{0:T(128)S(1)} %dynamic-slice_reduce_fusion.vector.refs_1_, f32[1224,128]{1,0:T(8,128)S(1)} %get-tuple-element.36.refs_2_, f32[1224,128]{1,0:T(8,128)S(1)} %get-tuple-element.37.refs_3_, ...), custom_call_target="tpu_custom_call" | custom-call | flops 14112000000 | bytes 14112000 | tf_op jit(solution)/shard_map/pallas_call | solution.py:445
  96.9 17.6 %all_to_all.11 = f32[32,1,128]{2,1,0:T(1,128)S(1)} all-to-all(f32[32,1,128]{2,1,0:T(1,128)S(1)} %bitcast.18), channel_id=1, replica_groups=mesh['section'=8,'gx'=8,'gy'=4] {'gx','gy'}, dimensions={0} | all-to-all | bytes 32768 | tf_op jit(solution)/shard_map/all_to_all | solution.py:548
  114.5 1.1 shard_map.92
  (8 shorter events, 0.1 us)
Async XLA Ops:
  0.6 18.4 %copy-start = (f32[64,3]{0,1:T(4,128)S(1)}, f32[64,3]{0,1:T(4,128)}, u32[]{:S(2)}) copy-start(f32[64,3]{0,1:T(4,128)} %param.7) | copy-start | bytes 2308
  2.8 11.9 %collective-permute-start = (f32[480,128]{1,0:T(8,128)S(1)}, f32[480,128]{1,0:T(8,128)S(1)}, u32[]{:S(2)}, u32[]{:S(2)}) collective-permute-start(f32[480,128]{1,0:T(8,128)S(1)} %get-tuple-element.30), channel_id=1, source_target_pairs={{0,4},{4,8},{8,12},{12,16},{16,20},{20,24},{24,28},{28,0},{1,5},{5... | collective-permute-start | bytes 737288 | tf_op jit(solution)/shard_map/ppermute | solution.py:461
  4.8 9.9 %collective-permute-start.1 = (f32[480,128]{1,0:T(8,128)S(1)}, f32[480,128]{1,0:T(8,128)S(1)}, u32[]{:S(2)}, u32[]{:S(2)}) collective-permute-start(f32[480,128]{1,0:T(8,128)S(1)} %get-tuple-element.31), channel_id=1, source_target_pairs={{0,28},{4,0},{8,4},{12,8},{16,12},{20,16},{24,20},{28,24},{1,29},{... | collective-permute-start | bytes 737288 | tf_op jit(solution)/shard_map/ppermute | solution.py:461
  8.8 10.4 %collective-permute-start.2 = (f32[480,128]{1,0:T(8,128)S(1)}, f32[480,128]{1,0:T(8,128)S(1)}, u32[]{:S(2)}, u32[]{:S(2)}) collective-permute-start(f32[480,128]{1,0:T(8,128)S(1)} %get-tuple-element.32), channel_id=1, source_target_pairs={{0,1},{1,2},{2,3},{3,0},{4,5},{5,6},{6,7},{7,4},{8,9},{9,10},{10,1... | collective-permute-start | bytes 737288 | tf_op jit(solution)/shard_map/ppermute | solution.py:461
  10.3 9.0 %collective-permute-start.3 = (f32[480,128]{1,0:T(8,128)S(1)}, f32[480,128]{1,0:T(8,128)S(1)}, u32[]{:S(2)}, u32[]{:S(2)}) collective-permute-start(f32[480,128]{1,0:T(8,128)S(1)} %get-tuple-element.33), channel_id=1, source_target_pairs={{0,3},{1,0},{2,1},{3,2},{4,7},{5,4},{6,5},{7,6},{8,11},{9,8},{10,9... | collective-permute-start | bytes 737288 | tf_op jit(solution)/shard_map/ppermute | solution.py:461
  14.7 4.7 %collective-permute-start.4 = (f32[200,128]{1,0:T(8,128)S(1)}, f32[200,128]{1,0:T(8,128)S(1)}, u32[]{:S(2)}, u32[]{:S(2)}) collective-permute-start(f32[200,128]{1,0:T(8,128)S(1)} %get-tuple-element.34), channel_id=1, source_target_pairs={{0,1},{1,2},{2,3},{3,0},{4,5},{5,6},{6,7},{7,4},{8,9},{9,10},{10,1... | collective-permute-start | bytes 307208 | tf_op jit(solution)/shard_map/ppermute | solution.py:461
  16.3 4.7 %collective-permute-start.5 = (f32[200,128]{1,0:T(8,128)S(1)}, f32[200,128]{1,0:T(8,128)S(1)}, u32[]{:S(2)}, u32[]{:S(2)}) collective-permute-start(f32[200,128]{1,0:T(8,128)S(1)} %get-tuple-element.35), channel_id=1, source_target_pairs={{0,3},{1,0},{2,1},{3,2},{4,7},{5,4},{6,5},{7,6},{8,11},{9,8},{10,9... | collective-permute-start | bytes 307208 | tf_op jit(solution)/shard_map/ppermute | solution.py:461
  16.9 14.5 %collective-permute-start.8 = (f32[256,128]{1,0:T(8,128)}, f32[256,128]{1,0:T(8,128)S(1)}, u32[]{:S(2)}, u32[]{:S(2)}) collective-permute-start(f32[256,128]{1,0:T(8,128)} %bitcast.20), channel_id=1, source_target_pairs={{0,160},{32,192},{64,224},{96,0},{128,32},{160,64},{192,96},{224,1... | collective-permute-start | bytes 393224 | tf_op jit(solution)/shard_map/ppermute | solution.py:461
  22.3 10.8 %collective-permute-start.6 = (f32[584,128]{1,0:T(8,128)S(1)}, f32[584,128]{1,0:T(8,128)S(1)}, u32[]{:S(2)}, u32[]{:S(2)}) collective-permute-start(f32[584,128]{1,0:T(8,128)S(1)} %get-tuple-element.43), channel_id=1, source_target_pairs={{0,224},{32,0},{64,32},{96,64},{128,96},{160,128},{192,160},{224,1... | collective-permute-start | bytes 897032 | tf_op jit(solution)/shard_map/ppermute | solution.py:461
  23.1 10.0 %collective-permute-start.7 = (f32[408,128]{1,0:T(8,128)S(1)}, f32[408,128]{1,0:T(8,128)S(1)}, u32[]{:S(2)}, u32[]{:S(2)}) collective-permute-start(f32[408,128]{1,0:T(8,128)S(1)} %get-tuple-element.44), channel_id=1, source_target_pairs={{0,192},{32,224},{64,0},{96,32},{128,64},{160,96},{192,128},{224,1... | collective-permute-start | bytes 626696 | tf_op jit(solution)/shard_map/ppermute | solution.py:461
  33.1 13.9 %copy-start.1 = (f32[1,16,16,128]{3,2,1,0:T(8,128)S(1)}, f32[1,16,16,128]{3,2,1,0:T(8,128)}, u32[]{:S(2)}) copy-start(f32[1,16,16,128]{3,2,1,0:T(8,128)} %param.8) | copy-start | bytes 393220
  43.7 9.3 %collective-permute-start.13 = (f32[560,128]{1,0:T(8,128)S(1)}, f32[560,128]{1,0:T(8,128)S(1)}, u32[]{:S(2)}, u32[]{:S(2)}) collective-permute-start(f32[560,128]{1,0:T(8,128)S(1)} %get-tuple-element.48), channel_id=1, source_target_pairs={{0,4},{4,8},{8,12},{12,16},{16,20},{20,24},{24,28},{28,0},{1,5},{5... | collective-permute-start | bytes 860168 | tf_op jit(solution)/shard_map/ppermute | solution.py:461
  43.8 10.4 %collective-permute-start.14 = (f32[560,128]{1,0:T(8,128)S(1)}, f32[560,128]{1,0:T(8,128)S(1)}, u32[]{:S(2)}, u32[]{:S(2)}) collective-permute-start(f32[560,128]{1,0:T(8,128)S(1)} %get-tuple-element.49), channel_id=1, source_target_pairs={{0,28},{4,0},{8,4},{12,8},{16,12},{20,16},{24,20},{28,24},{1,29},{... | collective-permute-start | bytes 860168 | tf_op jit(solution)/shard_map/ppermute | solution.py:461
  47.0 5.6 %collective-permute-start.12 = (f32[256,128]{1,0:T(8,128)S(1)}, f32[256,128]{1,0:T(8,128)S(1)}, u32[]{:S(2)}, u32[]{:S(2)}) collective-permute-start(f32[256,128]{1,0:T(8,128)S(1)} %bitcast.21), channel_id=1, source_target_pairs={{0,32},{32,64},{64,96},{96,128},{128,160},{160,192},{192,224},{224... | collective-permute-start | bytes 393224 | tf_op jit(solution)/shard_map/ppermute | solution.py:461
  47.0 26.8 %collective-permute-start.10 = (f32[584,128]{1,0:T(8,128)S(1)}, f32[584,128]{1,0:T(8,128)S(1)}, u32[]{:S(2)}, u32[]{:S(2)}) collective-permute-start(f32[584,128]{1,0:T(8,128)S(1)} %get-tuple-element.43), channel_id=1, source_target_pairs={{0,96},{32,128},{64,160},{96,192},{128,224},{160,0},{192,32},{224,... | collective-permute-start | bytes 897032 | tf_op jit(solution)/shard_map/ppermute | solution.py:461
  49.6 25.1 %collective-permute-start.9 = (f32[792,128]{1,0:T(8,128)S(1)}, f32[792,128]{1,0:T(8,128)S(1)}, u32[]{:S(2)}, u32[]{:S(2)}) collective-permute-start(f32[792,128]{1,0:T(8,128)S(1)} %get-tuple-element.40.refs_7_), channel_id=1, source_target_pairs={{0,128},{32,160},{64,192},{96,224},{128,0},{160,32},{192,64},{224,... | collective-permute-start | bytes 1216520 | tf_op jit(solution)/shard_map/ppermute | solution.py:461
  52.6 20.0 %collective-permute-start.11 = (f32[408,128]{1,0:T(8,128)S(1)}, f32[408,128]{1,0:T(8,128)S(1)}, u32[]{:S(2)}, u32[]{:S(2)}) collective-permute-start(f32[408,128]{1,0:T(8,128)S(1)} %get-tuple-element.44), channel_id=1, source_target_pairs={{0,64},{32,96},{64,128},{96,160},{128,192},{160,224},{192,0},{224,... | collective-permute-start | bytes 626696 | tf_op jit(solution)/shard_map/ppermute | solution.py:461
  53.0 21.7 %collective-permute-start.15 = (f32[560,128]{1,0:T(8,128)S(1)}, f32[560,128]{1,0:T(8,128)S(1)}, u32[]{:S(2)}, u32[]{:S(2)}) collective-permute-start(f32[560,128]{1,0:T(8,128)S(1)} %get-tuple-element.50), channel_id=1, source_target_pairs={{0,1},{1,2},{2,3},{3,0},{4,5},{5,6},{6,7},{7,4},{8,9},{9,10},{10,1... | collective-permute-start | bytes 860168 | tf_op jit(solution)/shard_map/ppermute | solution.py:461
  54.2 20.5 %collective-permute-start.16 = (f32[560,128]{1,0:T(8,128)S(1)}, f32[560,128]{1,0:T(8,128)S(1)}, u32[]{:S(2)}, u32[]{:S(2)}) collective-permute-start(f32[560,128]{1,0:T(8,128)S(1)} %get-tuple-element.51), channel_id=1, source_target_pairs={{0,3},{1,0},{2,1},{3,2},{4,7},{5,4},{6,5},{7,6},{8,11},{9,8},{10,9... | collective-permute-start | bytes 860168 | tf_op jit(solution)/shard_map/ppermute | solution.py:461
  72.7 5.1 %collective-permute-start.17 = (f32[272,128]{1,0:T(8,128)S(1)}, f32[272,128]{1,0:T(8,128)S(1)}, u32[]{:S(2)}, u32[]{:S(2)}) collective-permute-start(f32[272,128]{1,0:T(8,128)S(1)} %get-tuple-element.52), channel_id=1, source_target_pairs={{0,1},{1,2},{2,3},{3,0},{4,5},{5,6},{6,7},{7,4},{8,9},{9,10},{10,1... | collective-permute-start | bytes 417800 | tf_op jit(solution)/shard_map/ppermute | solution.py:461
  73.9 5.1 %collective-permute-start.18 = (f32[272,128]{1,0:T(8,128)S(1)}, f32[272,128]{1,0:T(8,128)S(1)}, u32[]{:S(2)}, u32[]{:S(2)}) collective-permute-start(f32[272,128]{1,0:T(8,128)S(1)} %get-tuple-element.53), channel_id=1, source_target_pairs={{0,3},{1,0},{2,1},{3,2},{4,7},{5,4},{6,5},{7,6},{8,11},{9,8},{10,9... | collective-permute-start | bytes 417800 | tf_op jit(solution)/shard_map/ppermute | solution.py:461

commit v4 on v3

--- a/solution.py
+++ b/solution.py
@@ -6,6 +6,7 @@
 from jax.experimental import pallas as pl
 from jax.experimental.pallas import tpu as pltpu
 from jax.sharding import PartitionSpec as P
+
 
 GROUPS = (4, 4)
 B = 16
@@ -23,7 +24,7 @@
 )
 
 ROUNDS = sum(GROUPS)
-SEGMENTS = ((0, 0, 1), (0, 1, 4), (1, 0, 4))
+SEGMENTS = ((0, 0, 1), (0, 1, 2), (0, 2, 4), (1, 0, 4))
 PLACES = [(g, j) for g, k in enumerate(GROUPS) for j in range(k)]
 T_HALO = [2 * (GROUPS[g] - 1 - j) for g, j in PLACES]
 T_MAX = max(T_HALO)
@@ -39,7 +40,7 @@
 
 def mask_widths():
     k = GROUPS[0]
-    return (2 * k - 1, 2 * k + 1, 2 * k, T_MAX)
+    return (2 * k + 1, 2 * k - 1, 2 * k, T_MAX)
 
 
 def state_widths(k):
@@ -123,12 +124,13 @@
     return gx == 0, gx == place[2] - 1, gy == 0, gy == place[3] - 1
 
 
-def first_pack_kernel(own, *outs):
-    pack_slabs(own_readers(own), mask_widths(), outs)
-
-
-def own_readers(own):
-    return [lambda x, y, n, f=f: own[f, x, pl.ds(y, n), :] for f in range(4)]
+def first_pack_kernel(masks, tough, *outs):
+    pack_slabs(own_readers(masks, tough), mask_widths(), outs)
+
+
+def own_readers(masks, tough):
+    readers = [lambda x, y, n, f=f: masks[f, x, pl.ds(y, n), :].astype(f32) for f in range(3)]
+    return readers + [lambda x, y, n: tough[0, x, pl.ds(y, n), :]]
 
 
 def row(x, y):
@@ -136,7 +138,7 @@
 
 
 def first_kernel(
-    sides, place, vector, own, xlo, xhi, ylo, yhi, clo, chi,
+    sides, place, vector, masks, own_tough, xlo, xhi, ylo, yhi, clo, chi,
     state, fix, ld, cr, own_free, *tough_outs,
 ):
     w = [vector[i] for i in range(3)]
@@ -145,10 +147,12 @@
     def choose(outside, value, other):
         return value if outside is None else jnp.where(outside, other, value)
 
-    def put_fixed(x, y, v, outside):
-        fix[pl.ds(row(x, y), v.shape[0]), :] = choose(outside, v, 1.0)
+    def put_clamp(x, y, v, outside):
+        at = pl.ds(row(x, y), v.shape[0])
+        v = jnp.maximum(choose(outside, v, 1.0), ld[at, :])
+        fix[at, :] = v
         if outside is None:
-            own_free[pl.ds(row(x, y), v.shape[0]), :] = 1.0 - v
+            own_free[at, :] = 1.0 - v
 
     def put_load(x, y, v, outside):
         v = choose(outside, v, 0.0)
@@ -175,8 +179,8 @@
 
     own_free[...] = jnp.zeros_like(own_free)
     unpack(
-        own_readers(own), (xlo, xhi, ylo, yhi), (clo, chi), mask_widths(), edges,
-        (put_fixed, put_load, put_crack, put_tough),
+        own_readers(masks, own_tough), (xlo, xhi, ylo, yhi), (clo, chi), mask_widths(), edges,
+        (put_load, put_clamp, put_crack, put_tough),
     )
 
 
@@ -432,12 +436,6 @@
     sums_out[...] = jnp.broadcast_to(sums, sums_out.shape)
 
 
-def table_kernel(scale, place, parts, out):
-    total = jnp.sum(parts[...], axis=0, keepdims=True)
-    root = jnp.sqrt(total * scale)
-    out[...] = pltpu.roll(jnp.broadcast_to(root, (8, 128)), place[4], 1)[:1, :ROUNDS]
-
-
 def call(kernel, outs, ins, scratch=(), smem=0, us=1.0, limit=4):
     single = isinstance(outs, tuple)
     shapes = [outs] if single else outs
@@ -481,21 +479,12 @@
             lax.axis_index("gy").astype(jnp.int32),
             jnp.int32(nx),
             jnp.int32(ny),
-            home,
         ]
     )
     vector = lax.dynamic_slice(load_table, (load_index[0], 0), (1, 3)).reshape(3)
-    own = jnp.stack(
-        [
-            jnp.maximum(clamp_mask, load_mask).astype(f32),
-            load_mask.astype(f32),
-            crack_mask.astype(f32),
-            toughness[0],
-        ]
-    )
-    own = lax.optimization_barrier(own)
+    masks = lax.optimization_barrier(jnp.stack([load_mask, clamp_mask, crack_mask]))
     widths = mask_widths()
-    slabs = call(first_pack_kernel, [(slab_rows(widths), 128)] * 4, [own], us=0.5)
+    slabs = call(first_pack_kernel, [(slab_rows(widths), 128)] * 4, [masks, toughness], us=0.5)
     received = swap_sides(slabs)
     corners = swap_corners(received[0], received[1], widths)
     sides = tuple(sorted({h for h in T_HALO if h}, reverse=True))
@@ -503,7 +492,7 @@
     made = call(
         functools.partial(first_kernel, sides),
         [(12,) + ext, ext, ext, ext, ext] + [(rows_of(h), 128) for h in sides],
-        [place, vector, own, *received, *corners], smem=2, us=1.9,
+        [place, vector, masks, toughness, *received, *corners], smem=2, us=1.9,
     )
     state, kinds = made[0], made[1:5]
     by_halo = dict(zip(sides, made[5:]))
@@ -547,9 +536,8 @@
             state, sums = res
     parts = lax.all_to_all(parts, ("gx", "gy"), 0, 0, tiled=True)
     scale = 1.0 / (3.0 * B * B * 128 * nx * ny)
-    norms = call(
-        functools.partial(table_kernel, scale), (1, ROUNDS), [place, parts], smem=1, us=0.1
-    )
+    parts = lax.dynamic_slice(parts, (0, ROUNDS - home), (nx * ny, ROUNDS))
+    norms = jnp.sqrt(jnp.sum(parts, axis=0, keepdims=True) * scale)
     return moved, damage, norms
 
 

time: 116 us -> 114 us (0.983)
  blocking collectives: 17.6 us -> 0 us
  starting transfers between devices: 26.9 us -> 36 us
  waiting for transfers between devices: 30.3 us -> 36.7 us
    all_to_all x1 -> x0, blocking collectives: 17.6 us -> none  [on_device(): parts = lax.all_to_all(parts, ('gx', 'gy'), 0, 0, tiled=True)]
    all_to_all x0 -> x1, starting transfers between devices: none -> 9.12 us  [on_device(): parts = lax.all_to_all(parts, ('gx', 'gy'), 0, 0, tiled=True)]
    all_to_all x0 -> x1, waiting for transfers between devices: none -> 8.54 us  [on_device(): parts = lax.all_to_all(parts, ('gx', 'gy'), 0, 0, tiled=True)]
    ppermute x19, waiting for transfers between devices: 30.3 us -> 28.1 us  [shift(): return lax.ppermute(x, axis, [(i, (i + by) % n) for i in range(n)])]
  transfers between devices with their start and end apart: 19 -> 20, of which waited for: 8 -> 9; matrix products, arithmetic and copies ran while one was open for 0% -> 0% of each run, Pallas kernels for 6% -> 11%
where the time goes in v4:
time: 114 us
  Pallas kernels  37.9 us (33%)
  waiting for transfers between devices  36.7 us (32%)
  starting transfers between devices  36 us (32%)
  other arithmetic  1.78 us (2%)
  between operations  1.42 us (1%)
    pallas_call x8, Pallas kernels, call(): pl.pallas_call(kernel, out_shape=shapes, in_specs=[SMEM] * smem + [VMEM]...  37.9 us
    ppermute x19, waiting for transfers between devices, shift(): return lax.ppermute(x, axis, [(i, (i + by) % n) for i in range(n)])  28.1 us
    ppermute x19, starting transfers between devices, shift(): return lax.ppermute(x, axis, [(i, (i + by) % n) for i in range(n)])  26.8 us
    all_to_all x1, starting transfers between devices, on_device(): parts = lax.all_to_all(parts, ('gx', 'gy'), 0, 0, tiled=True)  9.12 us
    all_to_all x1, waiting for transfers between devices, on_device(): parts = lax.all_to_all(parts, ('gx', 'gy'), 0, 0, tiled=True)  8.54 us
  transfers between devices with their start and end apart: 20, of which 9 were waited for; matrix products, arithmetic and copies ran while one was open for 0% of the time, Pallas kernels for 11%

profile of v4, /device:TPU:2, one launch (start us, length us, event | category | flops | bytes accessed | tf_op | source)
XLA Modules:
  0.0 113.9 jit_solution(11460737510194061827)
XLA Ops:
  0.6 0.0 copy-start
  0.6 1.1 pad_add_fusion.masks
  1.7 1.0 shard_map.85
  2.7 2.0 %collective-permute-start = (f32[480,128]{1,0:T(8,128)S(1)}, f32[480,128]{1,0:T(8,128)S(1)}, u32[]{:S(2)}, u32[]{:S(2)}) collective-permute-start(f32[480,128]{1,0:T(8,128)S(1)} %get-tuple-element.32), channel_id=1, source_target_pairs={{0,4},{4,8},{8,12},{12,16},{16,20},{20,24},{24,28},{28,0},{1,5},{5... | collective-permute-start | bytes 737288 | tf_op jit(solution)/shard_map/ppermute | solution.py:459
  4.7 4.0 %collective-permute-start.1 = (f32[480,128]{1,0:T(8,128)S(1)}, f32[480,128]{1,0:T(8,128)S(1)}, u32[]{:S(2)}, u32[]{:S(2)}) collective-permute-start(f32[480,128]{1,0:T(8,128)S(1)} %get-tuple-element.33), channel_id=1, source_target_pairs={{0,28},{4,0},{8,4},{12,8},{16,12},{20,16},{24,20},{28,24},{1,29},{... | collective-permute-start | bytes 737288 | tf_op jit(solution)/shard_map/ppermute | solution.py:459
  8.7 1.5 %collective-permute-start.2 = (f32[480,128]{1,0:T(8,128)S(1)}, f32[480,128]{1,0:T(8,128)S(1)}, u32[]{:S(2)}, u32[]{:S(2)}) collective-permute-start(f32[480,128]{1,0:T(8,128)S(1)} %get-tuple-element.34), channel_id=1, source_target_pairs={{0,1},{1,2},{2,3},{3,0},{4,5},{5,6},{6,7},{7,4},{8,9},{9,10},{10,1... | collective-permute-start | bytes 737288 | tf_op jit(solution)/shard_map/ppermute | solution.py:459
  10.2 0.5 collective-permute-start.3
  10.7 1.8 %collective-permute-start.8 = (f32[256,128]{1,0:T(8,128)}, f32[256,128]{1,0:T(8,128)S(1)}, u32[]{:S(2)}, u32[]{:S(2)}) collective-permute-start(f32[256,128]{1,0:T(8,128)} %bitcast.6), channel_id=1, source_target_pairs={{0,160},{32,192},{64,224},{96,0},{128,32},{160,64},{192,96},{224,1... | collective-permute-start | bytes 393224 | tf_op jit(solution)/shard_map/ppermute | solution.py:459
  13.2 0.2 dynamic-slice_reduce_fusion.1.vector.refs_1_
  13.4 1.2 %collective-permute-done.xlo = f32[480,128]{1,0:T(8,128)S(1)} collective-permute-done((f32[480,128]{1,0:T(8,128)S(1)}, f32[480,128]{1,0:T(8,128)S(1)}, u32[]{:S(2)}, u32[]{:S(2)}) %collective-permute-start) | collective-permute-done | bytes 245792 | tf_op jit(solution)/shard_map/ppermute | solution.py:459
  14.6 0.0 collective-permute-done.1.xhi
  14.6 1.6 %collective-permute-start.4 = (f32[200,128]{1,0:T(8,128)S(1)}, f32[200,128]{1,0:T(8,128)S(1)}, u32[]{:S(2)}, u32[]{:S(2)}) collective-permute-start(f32[200,128]{1,0:T(8,128)S(1)} %get-tuple-element.36), channel_id=1, source_target_pairs={{0,1},{1,2},{2,3},{3,0},{4,5},{5,6},{6,7},{7,4},{8,9},{9,10},{10,1... | collective-permute-start | bytes 307208 | tf_op jit(solution)/shard_map/ppermute | solution.py:459
  16.2 0.5 collective-permute-start.5
  16.7 0.1 pad_add_fusion.1.place.refs_0_
  16.8 0.0 collective-permute-done.2.ylo
  16.8 0.5 collective-permute-done.3.yhi
  17.3 2.3 %collective-permute-done.4.clo = f32[200,128]{1,0:T(8,128)S(1)} collective-permute-done((f32[200,128]{1,0:T(8,128)S(1)}, f32[200,128]{1,0:T(8,128)S(1)}, u32[]{:S(2)}, u32[]{:S(2)}) %collective-permute-start.4) | collective-permute-done | bytes 102432 | tf_op jit(solution)/shard_map/ppermute | solution.py:459
  19.7 1.2 %collective-permute-done.5.chi = f32[200,128]{1,0:T(8,128)S(1)} collective-permute-done((f32[200,128]{1,0:T(8,128)S(1)}, f32[200,128]{1,0:T(8,128)S(1)}, u32[]{:S(2)}, u32[]{:S(2)}) %collective-permute-start.5) | collective-permute-done | bytes 102432 | tf_op jit(solution)/shard_map/ppermute | solution.py:459
  20.9 1.8 %shard_map.87 = (f32[12,1224,128]{2,1,0:T(8,128)S(1)}, f32[1224,128]{1,0:T(8,128)S(1)}, f32[1224,128]{1,0:T(8,128)S(1)}, f32[1224,128]{1,0:T(8,128)S(1)}, f32[12...) custom-call(s32[4]{0:T(128)S(1)} %pad_add_fusion.1.place.refs_0_, ...), custom_call_target="tpu_custom_call" | custom-call | flops 1900000000 | bytes 1900000 | tf_op jit(solution)/shard_map/pallas_call | solution.py:443
  22.7 0.7 collective-permute-start.6
  23.4 2.4 %collective-permute-start.7 = (f32[408,128]{1,0:T(8,128)S(1)}, f32[408,128]{1,0:T(8,128)S(1)}, u32[]{:S(2)}, u32[]{:S(2)}) collective-permute-start(f32[408,128]{1,0:T(8,128)S(1)} %get-tuple-element.48), channel_id=1, source_target_pairs={{0,192},{32,224},{64,0},{96,32},{128,64},{160,96},{192,128},{224,1... | collective-permute-start | bytes 626696 | tf_op jit(solution)/shard_map/ppermute | solution.py:459
  25.8 5.9 %shard_map.88 = (f32[12,1224,128]{2,1,0:T(8,128)S(1)}, f32[1,128]{1,0:T(1,128)S(1)}) custom-call(s32[4]{0:T(128)S(1)} %pad_add_fusion.1.place.refs_0_, f32[3]{0:T(128)S(1)} %dynamic-slice_reduce_fusion.1.vector.refs_1_, f32[1224,128]{1,0:T(8,128)S(1)} %get-tuple-element.38.refs_2_, f32[1224,128]{1,0:T(8,128)S(1)} %get-tuple-element.39.refs_3_, ...), custom_call_target="tpu_custom_call" | custom-call | flops 5488000000 | bytes 5488000 | tf_op jit(solution)/shard_map/pallas_call | solution.py:443
  31.7 0.0 collective-permute-done.6.refs_7_
  31.7 4.8 %shard_map.89 = (f32[12,1224,128]{2,1,0:T(8,128)S(1)}, f32[1,128]{1,0:T(1,128)S(1)}) custom-call(s32[4]{0:T(128)S(1)} %pad_add_fusion.1.place.refs_0_, f32[3]{0:T(128)S(1)} %dynamic-slice_reduce_fusion.1.vector.refs_1_, f32[1224,128]{1,0:T(8,128)S(1)} %get-tuple-element.38.refs_2_, f32[1224,128]{1,0:T(8,128)S(1)} %get-tuple-element.39.refs_3_, ...), custom_call_target="tpu_custom_call" | custom-call | flops 4032000000 | bytes 4032000 | tf_op jit(solution)/shard_map/pallas_call | solution.py:443
  36.5 0.0 collective-permute-done.8.refs_8_
  36.5 0.0 collective-permute-done.7.refs_7_
  36.5 6.3 %shard_map.90 = (f32[4,16,16,128]{3,2,1,0:T(8,128)S(1)}, f32[560,128]{1,0:T(8,128)S(1)}, f32[560,128]{1,0:T(8,128)S(1)}, f32[560,128]{1,0:T(8,128)S(1)}, f32[560,128]{1,0:T(8,128)S(1)}, /*index=5*/f32[1,128]{1,0:T(1,128)S(1)}) custom-call(s32[4]{0:T(128)S(1)} %pad_add_fusion.1.place.refs_0_, f32[3]{0:T(128)S(1)} %dynamic-slice_reduce_fusion.1.vector.refs_1_, ...), custom_call_target="tpu_custom_call" | custom-call | flops 4592000000 | bytes 4592000 | tf_op jit(solution)/shard_map/pallas_call | solution.py:443
  42.8 0.1 collective-permute-start.13
  42.9 3.2 %collective-permute-start.14 = (f32[560,128]{1,0:T(8,128)S(1)}, f32[560,128]{1,0:T(8,128)S(1)}, u32[]{:S(2)}, u32[]{:S(2)}) collective-permute-start(f32[560,128]{1,0:T(8,128)S(1)} %get-tuple-element.53), channel_id=1, source_target_pairs={{0,28},{4,0},{8,4},{12,8},{16,12},{20,16},{24,20},{28,24},{1,29},{... | collective-permute-start | bytes 860168 | tf_op jit(solution)/shard_map/ppermute | solution.py:459
  46.1 0.0 collective-permute-start.12
  46.1 0.4 collective-permute-start.10
  46.5 4.0 %collective-permute-start.9 = (f32[792,128]{1,0:T(8,128)S(1)}, f32[792,128]{1,0:T(8,128)S(1)}, u32[]{:S(2)}, u32[]{:S(2)}) collective-permute-start(f32[792,128]{1,0:T(8,128)S(1)} %get-tuple-element.42.refs_7_), channel_id=1, source_target_pairs={{0,128},{32,160},{64,192},{96,224},{128,0},{160,32},{192,64},{224,... | collective-permute-start | bytes 1216520 | tf_op jit(solution)/shard_map/ppermute | solution.py:459
  50.5 6.3 %collective-permute-done.12.refs_10_ = f32[256,128]{1,0:T(8,128)S(1)} collective-permute-done((f32[256,128]{1,0:T(8,128)}, f32[256,128]{1,0:T(8,128)S(1)}, u32[]{:S(2)}, u32[]{:S(2)}) %collective-permute-start.12) | collective-permute-done | bytes 131104 | tf_op jit(solution)/shard_map/ppermute | solution.py:459
  56.8 0.0 collective-permute-start.11
  56.8 1.2 %collective-permute-start.15 = (f32[560,128]{1,0:T(8,128)S(1)}, f32[560,128]{1,0:T(8,128)S(1)}, u32[]{:S(2)}, u32[]{:S(2)}) collective-permute-start(f32[560,128]{1,0:T(8,128)S(1)} %get-tuple-element.54), channel_id=1, source_target_pairs={{0,1},{1,2},{2,3},{3,0},{4,5},{5,6},{6,7},{7,4},{8,9},{9,10},{10,1... | collective-permute-start | bytes 860168 | tf_op jit(solution)/shard_map/ppermute | solution.py:459
  58.0 0.0 collective-permute-done.14.xhi.refs_13_
  58.0 0.8 collective-permute-start.16
  58.9 12.3 %collective-permute-done.11.refs_9_ = f32[408,128]{1,0:T(8,128)S(1)} collective-permute-done((f32[408,128]{1,0:T(8,128)S(1)}, f32[408,128]{1,0:T(8,128)S(1)}, u32[]{:S(2)}, u32[]{:S(2)}) %collective-permute-start.11) | collective-permute-done | bytes 208928 | tf_op jit(solution)/shard_map/ppermute | solution.py:459
  71.2 1.2 %collective-permute-start.17 = (f32[272,128]{1,0:T(8,128)S(1)}, f32[272,128]{1,0:T(8,128)S(1)}, u32[]{:S(2)}, u32[]{:S(2)}) collective-permute-start(f32[272,128]{1,0:T(8,128)S(1)} %get-tuple-element.56), channel_id=1, source_target_pairs={{0,1},{1,2},{2,3},{3,0},{4,5},{5,6},{6,7},{7,4},{8,9},{9,10},{10,1... | collective-permute-start | bytes 417800 | tf_op jit(solution)/shard_map/ppermute | solution.py:459
  72.4 0.0 collective-permute-done.10.refs_8_
  72.4 0.8 collective-permute-start.18
  73.3 3.0 %collective-permute-done.17.refs_16_ = f32[272,128]{1,0:T(8,128)S(1)} collective-permute-done((f32[272,128]{1,0:T(8,128)S(1)}, f32[272,128]{1,0:T(8,128)S(1)}, u32[]{:S(2)}, u32[]{:S(2)}) %collective-permute-start.17) | collective-permute-done | bytes 139296 | tf_op jit(solution)/shard_map/ppermute | solution.py:459
  76.3 1.2 %collective-permute-done.18.refs_17_ = f32[272,128]{1,0:T(8,128)S(1)} collective-permute-done((f32[272,128]{1,0:T(8,128)S(1)}, f32[272,128]{1,0:T(8,128)S(1)}, u32[]{:S(2)}, u32[]{:S(2)}) %collective-permute-start.18) | collective-permute-done | bytes 139296 | tf_op jit(solution)/shard_map/ppermute | solution.py:459
  77.5 18.1 %shard_map.92 = (f32[1,3,16,16,128]{4,3,2,1,0:T(8,128)}, f32[1,16,16,128]{3,2,1,0:T(8,128)}, f32[32,128]{1,0:T(8,128)}) custom-call(s32[4]{0:T(128)S(1)} %pad_add_fusion.1.place.refs_0_, f32[3]{0:T(128)S(1)} %dynamic-slice_reduce_fusion.1.vector.refs_1_, f32[1224,128]{1,0:T(8,128)S(1)} %get-tuple-element.38.refs_2_, ...), custom_call_target="tpu_custom_call" | custom-call | flops 14112000000 | bytes 14112000 | tf_op jit(solution)/shard_map/pallas_call | solution.py:443
  95.6 9.1 %all-to-all-start = ((f32[32,1,128]{2,1,0:T(1,128)}), f32[32,1,128]{2,1,0:T(1,128)S(1)}, u32[]{:S(2)}, u32[]{:S(2)}) async-start(f32[32,1,128]{2,1,0:T(1,128)} %bitcast.8), calls=%async_computation | async-start | bytes 32768 | tf_op jit(solution)/shard_map/all_to_all | solution.py:537
  104.7 8.5 %all-to-all-done = f32[32,1,128]{2,1,0:T(1,128)S(1)} async-done(((f32[32,1,128]{2,1,0:T(1,128)}), f32[32,1,128]{2,1,0:T(1,128)S(1)}, u32[]{:S(2)}, u32[]{:S(2)}) %all-to-all-start) | async-done | bytes 16416 | tf_op jit(solution)/shard_map/all_to_all | solution.py:537
  113.2 0.1 dynamic-slice_reduce_fusion
  113.4 0.5 sqrt_bitcast_fusion
  (8 shorter events, 0.1 us)
Async XLA Ops:
  0.6 12.6 %copy-start = (f32[64,3]{0,1:T(4,128)S(1)}, f32[64,3]{0,1:T(4,128)}, u32[]{:S(2)}) copy-start(f32[64,3]{0,1:T(4,128)} %param.7) | copy-start | bytes 2308
  2.7 11.9 %collective-permute-start = (f32[480,128]{1,0:T(8,128)S(1)}, f32[480,128]{1,0:T(8,128)S(1)}, u32[]{:S(2)}, u32[]{:S(2)}) collective-permute-start(f32[480,128]{1,0:T(8,128)S(1)} %get-tuple-element.32), channel_id=1, source_target_pairs={{0,4},{4,8},{8,12},{12,16},{16,20},{20,24},{24,28},{28,0},{1,5},{5... | collective-permute-start | bytes 737288 | tf_op jit(solution)/shard_map/ppermute | solution.py:459
  4.7 9.9 %collective-permute-start.1 = (f32[480,128]{1,0:T(8,128)S(1)}, f32[480,128]{1,0:T(8,128)S(1)}, u32[]{:S(2)}, u32[]{:S(2)}) collective-permute-start(f32[480,128]{1,0:T(8,128)S(1)} %get-tuple-element.33), channel_id=1, source_target_pairs={{0,28},{4,0},{8,4},{12,8},{16,12},{20,16},{24,20},{28,24},{1,29},{... | collective-permute-start | bytes 737288 | tf_op jit(solution)/shard_map/ppermute | solution.py:459
  8.7 8.1 %collective-permute-start.2 = (f32[480,128]{1,0:T(8,128)S(1)}, f32[480,128]{1,0:T(8,128)S(1)}, u32[]{:S(2)}, u32[]{:S(2)}) collective-permute-start(f32[480,128]{1,0:T(8,128)S(1)} %get-tuple-element.34), channel_id=1, source_target_pairs={{0,1},{1,2},{2,3},{3,0},{4,5},{5,6},{6,7},{7,4},{8,9},{9,10},{10,1... | collective-permute-start | bytes 737288 | tf_op jit(solution)/shard_map/ppermute | solution.py:459
  10.2 7.1 %collective-permute-start.3 = (f32[480,128]{1,0:T(8,128)S(1)}, f32[480,128]{1,0:T(8,128)S(1)}, u32[]{:S(2)}, u32[]{:S(2)}) collective-permute-start(f32[480,128]{1,0:T(8,128)S(1)} %get-tuple-element.35), channel_id=1, source_target_pairs={{0,3},{1,0},{2,1},{3,2},{4,7},{5,4},{6,5},{7,6},{8,11},{9,8},{10,9... | collective-permute-start | bytes 737288 | tf_op jit(solution)/shard_map/ppermute | solution.py:459
  10.7 25.7 %collective-permute-start.8 = (f32[256,128]{1,0:T(8,128)}, f32[256,128]{1,0:T(8,128)S(1)}, u32[]{:S(2)}, u32[]{:S(2)}) collective-permute-start(f32[256,128]{1,0:T(8,128)} %bitcast.6), channel_id=1, source_target_pairs={{0,160},{32,192},{64,224},{96,0},{128,32},{160,64},{192,96},{224,1... | collective-permute-start | bytes 393224 | tf_op jit(solution)/shard_map/ppermute | solution.py:459
  14.6 5.0 %collective-permute-start.4 = (f32[200,128]{1,0:T(8,128)S(1)}, f32[200,128]{1,0:T(8,128)S(1)}, u32[]{:S(2)}, u32[]{:S(2)}) collective-permute-start(f32[200,128]{1,0:T(8,128)S(1)} %get-tuple-element.36), channel_id=1, source_target_pairs={{0,1},{1,2},{2,3},{3,0},{4,5},{5,6},{6,7},{7,4},{8,9},{9,10},{10,1... | collective-permute-start | bytes 307208 | tf_op jit(solution)/shard_map/ppermute | solution.py:459
  16.2 4.7 %collective-permute-start.5 = (f32[200,128]{1,0:T(8,128)S(1)}, f32[200,128]{1,0:T(8,128)S(1)}, u32[]{:S(2)}, u32[]{:S(2)}) collective-permute-start(f32[200,128]{1,0:T(8,128)S(1)} %get-tuple-element.37), channel_id=1, source_target_pairs={{0,3},{1,0},{2,1},{3,2},{4,7},{5,4},{6,5},{7,6},{8,11},{9,8},{10,9... | collective-permute-start | bytes 307208 | tf_op jit(solution)/shard_map/ppermute | solution.py:459
  22.7 9.0 %collective-permute-start.6 = (f32[584,128]{1,0:T(8,128)S(1)}, f32[584,128]{1,0:T(8,128)S(1)}, u32[]{:S(2)}, u32[]{:S(2)}) collective-permute-start(f32[584,128]{1,0:T(8,128)S(1)} %get-tuple-element.45), channel_id=1, source_target_pairs={{0,224},{32,0},{64,32},{96,64},{128,96},{160,128},{192,160},{224,1... | collective-permute-start | bytes 897032 | tf_op jit(solution)/shard_map/ppermute | solution.py:459
  23.4 13.1 %collective-permute-start.7 = (f32[408,128]{1,0:T(8,128)S(1)}, f32[408,128]{1,0:T(8,128)S(1)}, u32[]{:S(2)}, u32[]{:S(2)}) collective-permute-start(f32[408,128]{1,0:T(8,128)S(1)} %get-tuple-element.48), channel_id=1, source_target_pairs={{0,192},{32,224},{64,0},{96,32},{128,64},{160,96},{192,128},{224,1... | collective-permute-start | bytes 626696 | tf_op jit(solution)/shard_map/ppermute | solution.py:459
  42.8 14.0 %collective-permute-start.13 = (f32[560,128]{1,0:T(8,128)S(1)}, f32[560,128]{1,0:T(8,128)S(1)}, u32[]{:S(2)}, u32[]{:S(2)}) collective-permute-start(f32[560,128]{1,0:T(8,128)S(1)} %get-tuple-element.52), channel_id=1, source_target_pairs={{0,4},{4,8},{8,12},{12,16},{16,20},{20,24},{24,28},{28,0},{1,5},{5... | collective-permute-start | bytes 860168 | tf_op jit(solution)/shard_map/ppermute | solution.py:459
  42.9 15.2 %collective-permute-start.14 = (f32[560,128]{1,0:T(8,128)S(1)}, f32[560,128]{1,0:T(8,128)S(1)}, u32[]{:S(2)}, u32[]{:S(2)}) collective-permute-start(f32[560,128]{1,0:T(8,128)S(1)} %get-tuple-element.53), channel_id=1, source_target_pairs={{0,28},{4,0},{8,4},{12,8},{16,12},{20,16},{24,20},{28,24},{1,29},{... | collective-permute-start | bytes 860168 | tf_op jit(solution)/shard_map/ppermute | solution.py:459
  46.1 10.7 %collective-permute-start.12 = (f32[256,128]{1,0:T(8,128)}, f32[256,128]{1,0:T(8,128)S(1)}, u32[]{:S(2)}, u32[]{:S(2)}) collective-permute-start(f32[256,128]{1,0:T(8,128)} %bitcast.6), channel_id=1, source_target_pairs={{0,32},{32,64},{64,96},{96,128},{128,160},{160,192},{192,224},{224... | collective-permute-start | bytes 393224 | tf_op jit(solution)/shard_map/ppermute | solution.py:459
  46.1 26.3 %collective-permute-start.10 = (f32[584,128]{1,0:T(8,128)S(1)}, f32[584,128]{1,0:T(8,128)S(1)}, u32[]{:S(2)}, u32[]{:S(2)}) collective-permute-start(f32[584,128]{1,0:T(8,128)S(1)} %get-tuple-element.45), channel_id=1, source_target_pairs={{0,96},{32,128},{64,160},{96,192},{128,224},{160,0},{192,32},{224,... | collective-permute-start | bytes 897032 | tf_op jit(solution)/shard_map/ppermute | solution.py:459
  46.5 26.8 %collective-permute-start.9 = (f32[792,128]{1,0:T(8,128)S(1)}, f32[792,128]{1,0:T(8,128)S(1)}, u32[]{:S(2)}, u32[]{:S(2)}) collective-permute-start(f32[792,128]{1,0:T(8,128)S(1)} %get-tuple-element.42.refs_7_), channel_id=1, source_target_pairs={{0,128},{32,160},{64,192},{96,224},{128,0},{160,32},{192,64},{224,... | collective-permute-start | bytes 1216520 | tf_op jit(solution)/shard_map/ppermute | solution.py:459
  56.8 14.4 %collective-permute-start.11 = (f32[408,128]{1,0:T(8,128)S(1)}, f32[408,128]{1,0:T(8,128)S(1)}, u32[]{:S(2)}, u32[]{:S(2)}) collective-permute-start(f32[408,128]{1,0:T(8,128)S(1)} %get-tuple-element.48), channel_id=1, source_target_pairs={{0,64},{32,96},{64,128},{96,160},{128,192},{160,224},{192,0},{224,... | collective-permute-start | bytes 626696 | tf_op jit(solution)/shard_map/ppermute | solution.py:459
  56.8 16.4 %collective-permute-start.15 = (f32[560,128]{1,0:T(8,128)S(1)}, f32[560,128]{1,0:T(8,128)S(1)}, u32[]{:S(2)}, u32[]{:S(2)}) collective-permute-start(f32[560,128]{1,0:T(8,128)S(1)} %get-tuple-element.54), channel_id=1, source_target_pairs={{0,1},{1,2},{2,3},{3,0},{4,5},{5,6},{6,7},{7,4},{8,9},{9,10},{10,1... | collective-permute-start | bytes 860168 | tf_op jit(solution)/shard_map/ppermute | solution.py:459
  58.0 15.2 %collective-permute-start.16 = (f32[560,128]{1,0:T(8,128)S(1)}, f32[560,128]{1,0:T(8,128)S(1)}, u32[]{:S(2)}, u32[]{:S(2)}) collective-permute-start(f32[560,128]{1,0:T(8,128)S(1)} %get-tuple-element.55), channel_id=1, source_target_pairs={{0,3},{1,0},{2,1},{3,2},{4,7},{5,4},{6,5},{7,6},{8,11},{9,8},{10,9... | collective-permute-start | bytes 860168 | tf_op jit(solution)/shard_map/ppermute | solution.py:459
  71.2 5.1 %collective-permute-start.17 = (f32[272,128]{1,0:T(8,128)S(1)}, f32[272,128]{1,0:T(8,128)S(1)}, u32[]{:S(2)}, u32[]{:S(2)}) collective-permute-start(f32[272,128]{1,0:T(8,128)S(1)} %get-tuple-element.56), channel_id=1, source_target_pairs={{0,1},{1,2},{2,3},{3,0},{4,5},{5,6},{6,7},{7,4},{8,9},{9,10},{10,1... | collective-permute-start | bytes 417800 | tf_op jit(solution)/shard_map/ppermute | solution.py:459
  72.4 5.1 %collective-permute-start.18 = (f32[272,128]{1,0:T(8,128)S(1)}, f32[272,128]{1,0:T(8,128)S(1)}, u32[]{:S(2)}, u32[]{:S(2)}) collective-permute-start(f32[272,128]{1,0:T(8,128)S(1)} %get-tuple-element.57), channel_id=1, source_target_pairs={{0,3},{1,0},{2,1},{3,2},{4,7},{5,4},{6,5},{7,6},{8,11},{9,8},{10,9... | collective-permute-start | bytes 417800 | tf_op jit(solution)/shard_map/ppermute | solution.py:459
  95.6 17.7 %all-to-all-start = ((f32[32,1,128]{2,1,0:T(1,128)}), f32[32,1,128]{2,1,0:T(1,128)S(1)}, u32[]{:S(2)}, u32[]{:S(2)}) async-start(f32[32,1,128]{2,1,0:T(1,128)} %bitcast.8), calls=%async_computation | async-start | bytes 32768 | tf_op jit(solution)/shard_map/all_to_all | solution.py:537

commit v5 on v4

--- a/solution.py
+++ b/solution.py
@@ -23,6 +23,7 @@
     0.00953945386696008, 0.04580735112208377, -0.054824704413705544, 0.06541734748383539,
 )
 
+SCALE = 16.0 ** (2.0 / 3.0)
 ROUNDS = sum(GROUPS)
 SEGMENTS = ((0, 0, 1), (0, 1, 2), (0, 2, 4), (1, 0, 4))
 PLACES = [(g, j) for g, k in enumerate(GROUPS) for j in range(k)]
@@ -124,7 +125,8 @@
     return gx == 0, gx == place[2] - 1, gy == 0, gy == place[3] - 1
 
 
-def first_pack_kernel(masks, tough, *outs):
+def first_pack_kernel(masks, tough, kept, *outs):
+    kept[...] = tough[...]
     pack_slabs(own_readers(masks, tough), mask_widths(), outs)
 
 
@@ -139,8 +141,9 @@
 
 def first_kernel(
     sides, place, vector, masks, own_tough, xlo, xhi, ylo, yhi, clo, chi,
-    state, fix, ld, cr, own_free, *tough_outs,
+    state, fix, least, most, own_free, *rest,
 ):
+    *tough_outs, ld = rest
     w = [vector[i] for i in range(3)]
     edges = edges_of(place)
 
@@ -166,8 +169,10 @@
 
     def put_crack(x, y, v, outside):
         at = pl.ds(row(x, y), v.shape[0])
-        cr[at, :] = choose(outside, v, -1.0)
-        put_state(state, 3, at, choose(outside, v, 0.0))
+        v = choose(outside, v, 0.0)
+        least[at, :] = v
+        most[at, :] = choose(outside, jnp.ones_like(v), 0.0)
+        put_state(state, 3, at, v)
 
     def put_tough(x, y, v, outside):
         n = v.shape[0]
@@ -208,7 +213,7 @@
     ref[minus, at, :] = down(v)
 
 
-def sweep(src, dst, half, flow, flow_z, fix, ld, cr, own_free, tough, w, left):
+def sweep(src, dst, half, flow, flow_z, given, fix, least, most, own_free, tough, left):
     hd = 2 * left
     hm = hd + 1
 
@@ -227,7 +232,7 @@
                 + (src[6, at, :] - src[9, at, :])
             )
             half[at, :] = h
-            flow[at, :] = jnp.where(cr[at, :] < -0.5, 0.0, h * div)
+            flow[at, :] = h * div * most[at, :]
 
     def turned_flow(i):
         out = []
@@ -275,7 +280,6 @@
                 flow_z[at, :],
             ]
             is_fixed = fix[at, :] > 0.5
-            load = ld[at, :]
             squares = None
             for c in range(3):
                 u0 = src[c, at, :]
@@ -284,7 +288,7 @@
                 for f, n in zip(faces, un):
                     res = res + f * n
                 relaxed = u0 + (res * 0.6) / (weight + pairs[c])
-                dst[c, at, :] = jnp.where(is_fixed, load * w[c], relaxed)
+                dst[c, at, :] = jnp.where(is_fixed, given[c, at, :], relaxed)
                 squares = res * res if squares is None else squares + res * res
             acc = acc + jnp.where(own_free[at, :] > 0.5, squares, 0.0)
         return acc
@@ -308,8 +312,8 @@
             spread = (dx * dx + dy * dy + dz * dz) + 0.5 * (xy2 + xz2 + yz2)
             det = dx * dy * dz + 0.25 * (xy * xz * yz - (dx * yz2 + dy * xz2 + dz * xy2))
             s6 = spread * (1.0 / 24.0)
-            inv = lax.rsqrt(s6 + 1e-08)
-            ratio = (det * 0.0625) * (inv * inv * inv)
+            inv = lax.rsqrt(spread * (SCALE / 24.0) + 1e-08 * SCALE)
+            ratio = det * (inv * inv * inv)
             radius = s6 * lax.rsqrt(jnp.maximum(s6, 1e-37))
             wq = jnp.maximum(0.5 - 0.5 * jnp.abs(ratio), 0.0)
             cos = horner(COS_THIRD, wq)
@@ -330,8 +334,7 @@
             )
             gc = tough[pl.ds((i - (HALO - hd)) * (B + 2 * hd) + 8 * t, 8), :]
             new = (psi2 + gc * beside) / (psi2 + 7.0 * gc)
-            kind = cr[at, :]
-            dst[3, at, :] = jnp.where(kind > 0.5, 1.0, jnp.where(kind < -0.5, 0.0, new))
+            dst[3, at, :] = jnp.minimum(jnp.maximum(new, least[at, :]), most[at, :])
 
     def step(i, acc, damaged):
         later = turned(dst, range(3), hd, i - 1)
@@ -376,9 +379,8 @@
         del refs[:n]
         return out
 
-    place, vector, fix, ld, cr, own_free, sums_in = take(7)
+    place, given, fix, least, most, own_free, sums_in = take(7)
     tough = take(end - begin)
-    w = [vector[i] for i in range(3)]
     unpacks = group > 0 and begin == 0
     if unpacks:
         state, xlo, xhi, ylo, yhi, clo, chi = take(7)
@@ -415,7 +417,8 @@
     for j in range(begin, end):
         dst = wide_out if j == end - 1 and end < k else bufs[j % 2]
         acc = sweep(
-            src, dst, half, flow, flow_z, fix, ld, cr, own_free, tough[j - begin], w, k - 1 - j
+            src, dst, half, flow, flow_z, given, fix, least, most, own_free, tough[j - begin],
+            k - 1 - j,
         )
         sums = add_sum(sums, acc, start + j)
         src = dst
@@ -484,7 +487,10 @@
     vector = lax.dynamic_slice(load_table, (load_index[0], 0), (1, 3)).reshape(3)
     masks = lax.optimization_barrier(jnp.stack([load_mask, clamp_mask, crack_mask]))
     widths = mask_widths()
-    slabs = call(first_pack_kernel, [(slab_rows(widths), 128)] * 4, [masks, toughness], us=0.5)
+    kept, *slabs = call(
+        first_pack_kernel, [(1, B, B, 128)] + [(slab_rows(widths), 128)] * 4,
+        [masks, toughness], us=0.5,
+    )
     received = swap_sides(slabs)
     corners = swap_corners(received[0], received[1], widths)
     sides = tuple(sorted({h for h in T_HALO if h}, reverse=True))
@@ -492,9 +498,10 @@
     made = call(
         functools.partial(first_kernel, sides),
         [(12,) + ext, ext, ext, ext, ext] + [(rows_of(h), 128) for h in sides],
-        [place, vector, masks, toughness, *received, *corners], smem=2, us=1.9,
+        [place, vector, masks, kept, *received, *corners], [pltpu.VMEM(ext, f32)], smem=2, us=1.9,
     )
     state, kinds = made[0], made[1:5]
+    given = state
     by_halo = dict(zip(sides, made[5:]))
     by_halo[0] = toughness.reshape(B * B, 128)
     tough = []
@@ -505,7 +512,7 @@
         g, begin, end = segment
         k = GROUPS[g]
         start = sum(GROUPS[:g])
-        ins = [place, vector, *kinds, sums, *tough[start + begin : start + end]]
+        ins = [place, given, *kinds, sums, *tough[start + begin : start + end]]
         unpacks = g > 0 and begin == 0
         if unpacks:
             received = swap_sides(slabs)
@@ -526,7 +533,7 @@
         cost = sum((B + 4 * (k - 1 - j)) ** 2 * 0.007 for j in range(begin, end))
         res = call(
             functools.partial(sweep_kernel, segment), outs, ins, scratch,
-            smem=2, us=cost, limit=4 + 8 * bufs,
+            smem=1, us=cost, limit=4 + 8 * bufs,
         )
         if final:
             moved, damage, parts = res

time: 114 us -> 114 us (level)
  no operation moved by 1% of the time
where the time goes in v5:
time: 114 us
  Pallas kernels  37.6 us (33%)
  waiting for transfers between devices  36.7 us (32%)
  starting transfers between devices  35.9 us (31%)
  other arithmetic  1.78 us (2%)
  between operations  1.42 us (1%)
    pallas_call x8, Pallas kernels, call(): pl.pallas_call(kernel, out_shape=shapes, in_specs=[SMEM] * smem + [VMEM]...  37.6 us
    ppermute x19, waiting for transfers between devices, shift(): return lax.ppermute(x, axis, [(i, (i + by) % n) for i in range(n)])  28.1 us
    ppermute x19, starting transfers between devices, shift(): return lax.ppermute(x, axis, [(i, (i + by) % n) for i in range(n)])  26.8 us
    all_to_all x1, starting transfers between devices, on_device(): parts = lax.all_to_all(parts, ('gx', 'gy'), 0, 0, tiled=True)  9.03 us
    all_to_all x1, waiting for transfers between devices, on_device(): parts = lax.all_to_all(parts, ('gx', 'gy'), 0, 0, tiled=True)  8.54 us
  transfers between devices with their start and end apart: 20, of which 9 were waited for; matrix products, arithmetic and copies ran while one was open for 0% of the time, Pallas kernels for 11%

profile of v5, /device:TPU:2, one launch (start us, length us, event | category | flops | bytes accessed | tf_op | source)
XLA Modules:
  0.0 113.5 jit_solution(891519392674135619)
XLA Ops:
  0.6 0.0 copy-start
  0.6 1.1 pad_add_fusion.masks
  1.7 1.0 shard_map.85
  2.7 2.0 %collective-permute-start = (f32[480,128]{1,0:T(8,128)S(1)}, f32[480,128]{1,0:T(8,128)S(1)}, u32[]{:S(2)}, u32[]{:S(2)}) collective-permute-start(f32[480,128]{1,0:T(8,128)S(1)} %get-tuple-element.34), channel_id=1, source_target_pairs={{0,4},{4,8},{8,12},{12,16},{16,20},{20,24},{24,28},{28,0},{1,5},{5... | collective-permute-start | bytes 737288 | tf_op jit(solution)/shard_map/ppermute | solution.py:462
  4.7 4.0 %collective-permute-start.1 = (f32[480,128]{1,0:T(8,128)S(1)}, f32[480,128]{1,0:T(8,128)S(1)}, u32[]{:S(2)}, u32[]{:S(2)}) collective-permute-start(f32[480,128]{1,0:T(8,128)S(1)} %get-tuple-element.35), channel_id=1, source_target_pairs={{0,28},{4,0},{8,4},{12,8},{16,12},{20,16},{24,20},{28,24},{1,29},{... | collective-permute-start | bytes 737288 | tf_op jit(solution)/shard_map/ppermute | solution.py:462
  8.7 1.5 %collective-permute-start.2 = (f32[480,128]{1,0:T(8,128)S(1)}, f32[480,128]{1,0:T(8,128)S(1)}, u32[]{:S(2)}, u32[]{:S(2)}) collective-permute-start(f32[480,128]{1,0:T(8,128)S(1)} %get-tuple-element.36), channel_id=1, source_target_pairs={{0,1},{1,2},{2,3},{3,0},{4,5},{5,6},{6,7},{7,4},{8,9},{9,10},{10,1... | collective-permute-start | bytes 737288 | tf_op jit(solution)/shard_map/ppermute | solution.py:462
  10.2 0.5 collective-permute-start.3
  10.8 1.8 %collective-permute-start.8 = (f32[256,128]{1,0:T(8,128)}, f32[256,128]{1,0:T(8,128)S(1)}, u32[]{:S(2)}, u32[]{:S(2)}) collective-permute-start(f32[256,128]{1,0:T(8,128)} %bitcast.6), channel_id=1, source_target_pairs={{0,160},{32,192},{64,224},{96,0},{128,32},{160,64},{192,96},{224,1... | collective-permute-start | bytes 393224 | tf_op jit(solution)/shard_map/ppermute | solution.py:462
  13.2 0.2 dynamic-slice_reduce_fusion.1.vector
  13.4 1.2 %collective-permute-done.xlo = f32[480,128]{1,0:T(8,128)S(1)} collective-permute-done((f32[480,128]{1,0:T(8,128)S(1)}, f32[480,128]{1,0:T(8,128)S(1)}, u32[]{:S(2)}, u32[]{:S(2)}) %collective-permute-start) | collective-permute-done | bytes 245792 | tf_op jit(solution)/shard_map/ppermute | solution.py:462
  14.6 0.0 collective-permute-done.1.xhi
  14.6 1.6 %collective-permute-start.4 = (f32[200,128]{1,0:T(8,128)S(1)}, f32[200,128]{1,0:T(8,128)S(1)}, u32[]{:S(2)}, u32[]{:S(2)}) collective-permute-start(f32[200,128]{1,0:T(8,128)S(1)} %get-tuple-element.38), channel_id=1, source_target_pairs={{0,1},{1,2},{2,3},{3,0},{4,5},{5,6},{6,7},{7,4},{8,9},{9,10},{10,1... | collective-permute-start | bytes 307208 | tf_op jit(solution)/shard_map/ppermute | solution.py:462
  16.2 0.5 collective-permute-start.5
  16.7 0.1 pad_add_fusion.1.place.refs_0_
  16.8 0.0 collective-permute-done.2.ylo
  16.8 0.5 collective-permute-done.3.yhi
  17.4 2.3 %collective-permute-done.4.clo = f32[200,128]{1,0:T(8,128)S(1)} collective-permute-done((f32[200,128]{1,0:T(8,128)S(1)}, f32[200,128]{1,0:T(8,128)S(1)}, u32[]{:S(2)}, u32[]{:S(2)}) %collective-permute-start.4) | collective-permute-done | bytes 102432 | tf_op jit(solution)/shard_map/ppermute | solution.py:462
  19.7 1.2 %collective-permute-done.5.chi = f32[200,128]{1,0:T(8,128)S(1)} collective-permute-done((f32[200,128]{1,0:T(8,128)S(1)}, f32[200,128]{1,0:T(8,128)S(1)}, u32[]{:S(2)}, u32[]{:S(2)}) %collective-permute-start.5) | collective-permute-done | bytes 102432 | tf_op jit(solution)/shard_map/ppermute | solution.py:462
  20.9 1.4 %shard_map.87 = (f32[12,1224,128]{2,1,0:T(8,128)S(1)}, f32[1224,128]{1,0:T(8,128)S(1)}, f32[1224,128]{1,0:T(8,128)S(1)}, f32[1224,128]{1,0:T(8,128)S(1)}, f32[12...) custom-call(s32[4]{0:T(128)S(1)} %pad_add_fusion.1.place.refs_0_, ...), custom_call_target="tpu_custom_call" | custom-call | flops 1900000000 | bytes 1900000 | tf_op jit(solution)/shard_map/pallas_call | solution.py:446
  22.3 0.8 collective-permute-start.6
  23.1 2.4 %collective-permute-start.7 = (f32[408,128]{1,0:T(8,128)S(1)}, f32[408,128]{1,0:T(8,128)S(1)}, u32[]{:S(2)}, u32[]{:S(2)}) collective-permute-start(f32[408,128]{1,0:T(8,128)S(1)} %get-tuple-element.50), channel_id=1, source_target_pairs={{0,192},{32,224},{64,0},{96,32},{128,64},{160,96},{192,128},{224,1... | collective-permute-start | bytes 626696 | tf_op jit(solution)/shard_map/ppermute | solution.py:462
  25.4 5.9 %shard_map.88 = (f32[12,1224,128]{2,1,0:T(8,128)S(1)}, f32[1,128]{1,0:T(1,128)S(1)}) custom-call(s32[4]{0:T(128)S(1)} %pad_add_fusion.1.place.refs_0_, f32[12,1224,128]{2,1,0:T(8,128)S(1)} %get-tuple-element.40.refs_1_.refs_8_, f32[1224,128]{1,0:T(8,128)S(1)} %get-tuple-element.41.refs_2_, f32[1224,128]{1,0:T(8,128)S(1)} %get-tuple-element.42.refs_3_, ...), custom_call_target="tpu_custom_call" | custom-call | flops 5488000000 | bytes 5488000 | tf_op jit(solution)/shard_map/pallas_call | solution.py:446
  31.4 0.0 collective-permute-done.6.refs_7_
  31.4 4.8 %shard_map.89 = (f32[12,1224,128]{2,1,0:T(8,128)S(1)}, f32[1,128]{1,0:T(1,128)S(1)}) custom-call(s32[4]{0:T(128)S(1)} %pad_add_fusion.1.place.refs_0_, f32[12,1224,128]{2,1,0:T(8,128)S(1)} %get-tuple-element.40.refs_1_.refs_8_, f32[1224,128]{1,0:T(8,128)S(1)} %get-tuple-element.41.refs_2_, f32[1224,128]{1,0:T(8,128)S(1)} %get-tuple-element.42.refs_3_, ...), custom_call_target="tpu_custom_call" | custom-call | flops 4032000000 | bytes 4032000 | tf_op jit(solution)/shard_map/pallas_call | solution.py:446
  36.3 0.0 collective-permute-done.8.refs_8_
  36.3 6.3 %shard_map.90 = (f32[4,16,16,128]{3,2,1,0:T(8,128)S(1)}, f32[560,128]{1,0:T(8,128)S(1)}, f32[560,128]{1,0:T(8,128)S(1)}, f32[560,128]{1,0:T(8,128)S(1)}, f32[560,128]{1,0:T(8,128)S(1)}, /*index=5*/f32[1,128]{1,0:T(1,128)S(1)}) custom-call(s32[4]{0:T(128)S(1)} %pad_add_fusion.1.place.refs_0_, f32[12,1224,128]{2,1,0:T(8,128)S(1)} %get-tuple-element.40.refs_1_.refs_8_, ...), custom_call_target="tpu_custom_call" | custom-call | flops 4592000000 | bytes 4592000 | tf_op jit(solution)/shard_map/pallas_call | solution.py:446
  42.6 0.1 collective-permute-start.13
  42.7 3.2 %collective-permute-start.14 = (f32[560,128]{1,0:T(8,128)S(1)}, f32[560,128]{1,0:T(8,128)S(1)}, u32[]{:S(2)}, u32[]{:S(2)}) collective-permute-start(f32[560,128]{1,0:T(8,128)S(1)} %get-tuple-element.55), channel_id=1, source_target_pairs={{0,28},{4,0},{8,4},{12,8},{16,12},{20,16},{24,20},{28,24},{1,29},{... | collective-permute-start | bytes 860168 | tf_op jit(solution)/shard_map/ppermute | solution.py:462
  45.9 0.3 collective-permute-start.10
  46.2 4.1 %collective-permute-start.9 = (f32[792,128]{1,0:T(8,128)S(1)}, f32[792,128]{1,0:T(8,128)S(1)}, u32[]{:S(2)}, u32[]{:S(2)}) collective-permute-start(f32[792,128]{1,0:T(8,128)S(1)} %get-tuple-element.45.refs_7_), channel_id=1, source_target_pairs={{0,128},{32,160},{64,192},{96,224},{128,0},{160,32},{192,64},{224,... | collective-permute-start | bytes 1216520 | tf_op jit(solution)/shard_map/ppermute | solution.py:462
  50.3 6.3 %collective-permute-done.12.refs_10_ = f32[256,128]{1,0:T(8,128)S(1)} collective-permute-done((f32[256,128]{1,0:T(8,128)}, f32[256,128]{1,0:T(8,128)S(1)}, u32[]{:S(2)}, u32[]{:S(2)}) %collective-permute-start.12) | collective-permute-done | bytes 131104 | tf_op jit(solution)/shard_map/ppermute | solution.py:462
  56.7 0.0 collective-permute-start.11
  56.7 1.2 %collective-permute-start.15 = (f32[560,128]{1,0:T(8,128)S(1)}, f32[560,128]{1,0:T(8,128)S(1)}, u32[]{:S(2)}, u32[]{:S(2)}) collective-permute-start(f32[560,128]{1,0:T(8,128)S(1)} %get-tuple-element.56), channel_id=1, source_target_pairs={{0,1},{1,2},{2,3},{3,0},{4,5},{5,6},{6,7},{7,4},{8,9},{9,10},{10,1... | collective-permute-start | bytes 860168 | tf_op jit(solution)/shard_map/ppermute | solution.py:462
  57.9 0.0 collective-permute-done.14.xhi.refs_13_
  57.9 0.8 collective-permute-start.16
  58.7 12.3 %collective-permute-done.11.refs_9_ = f32[408,128]{1,0:T(8,128)S(1)} collective-permute-done((f32[408,128]{1,0:T(8,128)S(1)}, f32[408,128]{1,0:T(8,128)S(1)}, u32[]{:S(2)}, u32[]{:S(2)}) %collective-permute-start.11) | collective-permute-done | bytes 208928 | tf_op jit(solution)/shard_map/ppermute | solution.py:462
  71.1 1.2 %collective-permute-start.17 = (f32[272,128]{1,0:T(8,128)S(1)}, f32[272,128]{1,0:T(8,128)S(1)}, u32[]{:S(2)}, u32[]{:S(2)}) collective-permute-start(f32[272,128]{1,0:T(8,128)S(1)} %get-tuple-element.58), channel_id=1, source_target_pairs={{0,1},{1,2},{2,3},{3,0},{4,5},{5,6},{6,7},{7,4},{8,9},{9,10},{10,1... | collective-permute-start | bytes 417800 | tf_op jit(solution)/shard_map/ppermute | solution.py:462
  72.3 0.8 collective-permute-start.18
  73.1 0.0 collective-permute-done.9.refs_7_
  73.1 0.0 collective-permute-done.15.refs_14_
  73.1 0.0 collective-permute-done.16.refs_15_
  73.1 3.0 %collective-permute-done.17.refs_16_ = f32[272,128]{1,0:T(8,128)S(1)} collective-permute-done((f32[272,128]{1,0:T(8,128)S(1)}, f32[272,128]{1,0:T(8,128)S(1)}, u32[]{:S(2)}, u32[]{:S(2)}) %collective-permute-start.17) | collective-permute-done | bytes 139296 | tf_op jit(solution)/shard_map/ppermute | solution.py:462
  76.1 1.2 %collective-permute-done.18.refs_17_ = f32[272,128]{1,0:T(8,128)S(1)} collective-permute-done((f32[272,128]{1,0:T(8,128)S(1)}, f32[272,128]{1,0:T(8,128)S(1)}, u32[]{:S(2)}, u32[]{:S(2)}) %collective-permute-start.18) | collective-permute-done | bytes 139296 | tf_op jit(solution)/shard_map/ppermute | solution.py:462
  77.3 18.0 %shard_map.92 = (f32[1,3,16,16,128]{4,3,2,1,0:T(8,128)}, f32[1,16,16,128]{3,2,1,0:T(8,128)}, f32[32,128]{1,0:T(8,128)}) custom-call(s32[4]{0:T(128)S(1)} %pad_add_fusion.1.place.refs_0_, f32[12,1224,128]{2,1,0:T(8,128)S(1)} %get-tuple-element.40.refs_1_.refs_8_, f32[1224,128]{1,0:T(8,128)S(1)} %get-tuple-element.41.refs_2_, ...), custom_call_target="tpu_custom_call" | custom-call | flops 14112000000 | bytes 14112000 | tf_op jit(solution)/shard_map/pallas_call | solution.py:446
  95.3 9.0 %all-to-all-start = ((f32[32,1,128]{2,1,0:T(1,128)}), f32[32,1,128]{2,1,0:T(1,128)S(1)}, u32[]{:S(2)}, u32[]{:S(2)}) async-start(f32[32,1,128]{2,1,0:T(1,128)} %bitcast.8), calls=%async_computation | async-start | bytes 32768 | tf_op jit(solution)/shard_map/all_to_all | solution.py:544
  104.4 8.5 %all-to-all-done = f32[32,1,128]{2,1,0:T(1,128)S(1)} async-done(((f32[32,1,128]{2,1,0:T(1,128)}), f32[32,1,128]{2,1,0:T(1,128)S(1)}, u32[]{:S(2)}, u32[]{:S(2)}) %all-to-all-start) | async-done | bytes 16416 | tf_op jit(solution)/shard_map/all_to_all | solution.py:544
  112.9 0.1 dynamic-slice_reduce_fusion
  113.0 0.5 sqrt_bitcast_fusion
  (8 shorter events, 0.1 us)
Async XLA Ops:
  0.6 12.6 %copy-start = (f32[64,3]{0,1:T(4,128)S(1)}, f32[64,3]{0,1:T(4,128)}, u32[]{:S(2)}) copy-start(f32[64,3]{0,1:T(4,128)} %param.7) | copy-start | bytes 2308
  2.7 11.9 %collective-permute-start = (f32[480,128]{1,0:T(8,128)S(1)}, f32[480,128]{1,0:T(8,128)S(1)}, u32[]{:S(2)}, u32[]{:S(2)}) collective-permute-start(f32[480,128]{1,0:T(8,128)S(1)} %get-tuple-element.34), channel_id=1, source_target_pairs={{0,4},{4,8},{8,12},{12,16},{16,20},{20,24},{24,28},{28,0},{1,5},{5... | collective-permute-start | bytes 737288 | tf_op jit(solution)/shard_map/ppermute | solution.py:462
  4.7 9.9 %collective-permute-start.1 = (f32[480,128]{1,0:T(8,128)S(1)}, f32[480,128]{1,0:T(8,128)S(1)}, u32[]{:S(2)}, u32[]{:S(2)}) collective-permute-start(f32[480,128]{1,0:T(8,128)S(1)} %get-tuple-element.35), channel_id=1, source_target_pairs={{0,28},{4,0},{8,4},{12,8},{16,12},{20,16},{24,20},{28,24},{1,29},{... | collective-permute-start | bytes 737288 | tf_op jit(solution)/shard_map/ppermute | solution.py:462
  8.7 8.1 %collective-permute-start.2 = (f32[480,128]{1,0:T(8,128)S(1)}, f32[480,128]{1,0:T(8,128)S(1)}, u32[]{:S(2)}, u32[]{:S(2)}) collective-permute-start(f32[480,128]{1,0:T(8,128)S(1)} %get-tuple-element.36), channel_id=1, source_target_pairs={{0,1},{1,2},{2,3},{3,0},{4,5},{5,6},{6,7},{7,4},{8,9},{9,10},{10,1... | collective-permute-start | bytes 737288 | tf_op jit(solution)/shard_map/ppermute | solution.py:462
  10.2 7.1 %collective-permute-start.3 = (f32[480,128]{1,0:T(8,128)S(1)}, f32[480,128]{1,0:T(8,128)S(1)}, u32[]{:S(2)}, u32[]{:S(2)}) collective-permute-start(f32[480,128]{1,0:T(8,128)S(1)} %get-tuple-element.37), channel_id=1, source_target_pairs={{0,3},{1,0},{2,1},{3,2},{4,7},{5,4},{6,5},{7,6},{8,11},{9,8},{10,9... | collective-permute-start | bytes 737288 | tf_op jit(solution)/shard_map/ppermute | solution.py:462
  10.8 25.5 %collective-permute-start.8 = (f32[256,128]{1,0:T(8,128)}, f32[256,128]{1,0:T(8,128)S(1)}, u32[]{:S(2)}, u32[]{:S(2)}) collective-permute-start(f32[256,128]{1,0:T(8,128)} %bitcast.6), channel_id=1, source_target_pairs={{0,160},{32,192},{64,224},{96,0},{128,32},{160,64},{192,96},{224,1... | collective-permute-start | bytes 393224 | tf_op jit(solution)/shard_map/ppermute | solution.py:462
  14.6 5.0 %collective-permute-start.4 = (f32[200,128]{1,0:T(8,128)S(1)}, f32[200,128]{1,0:T(8,128)S(1)}, u32[]{:S(2)}, u32[]{:S(2)}) collective-permute-start(f32[200,128]{1,0:T(8,128)S(1)} %get-tuple-element.38), channel_id=1, source_target_pairs={{0,1},{1,2},{2,3},{3,0},{4,5},{5,6},{6,7},{7,4},{8,9},{9,10},{10,1... | collective-permute-start | bytes 307208 | tf_op jit(solution)/shard_map/ppermute | solution.py:462
  16.2 4.7 %collective-permute-start.5 = (f32[200,128]{1,0:T(8,128)S(1)}, f32[200,128]{1,0:T(8,128)S(1)}, u32[]{:S(2)}, u32[]{:S(2)}) collective-permute-start(f32[200,128]{1,0:T(8,128)S(1)} %get-tuple-element.39), channel_id=1, source_target_pairs={{0,3},{1,0},{2,1},{3,2},{4,7},{5,4},{6,5},{7,6},{8,11},{9,8},{10,9... | collective-permute-start | bytes 307208 | tf_op jit(solution)/shard_map/ppermute | solution.py:462
  22.3 9.1 %collective-permute-start.6 = (f32[584,128]{1,0:T(8,128)S(1)}, f32[584,128]{1,0:T(8,128)S(1)}, u32[]{:S(2)}, u32[]{:S(2)}) collective-permute-start(f32[584,128]{1,0:T(8,128)S(1)} %get-tuple-element.47), channel_id=1, source_target_pairs={{0,224},{32,0},{64,32},{96,64},{128,96},{160,128},{192,160},{224,1... | collective-permute-start | bytes 897032 | tf_op jit(solution)/shard_map/ppermute | solution.py:462
  23.1 13.2 %collective-permute-start.7 = (f32[408,128]{1,0:T(8,128)S(1)}, f32[408,128]{1,0:T(8,128)S(1)}, u32[]{:S(2)}, u32[]{:S(2)}) collective-permute-start(f32[408,128]{1,0:T(8,128)S(1)} %get-tuple-element.50), channel_id=1, source_target_pairs={{0,192},{32,224},{64,0},{96,32},{128,64},{160,96},{192,128},{224,1... | collective-permute-start | bytes 626696 | tf_op jit(solution)/shard_map/ppermute | solution.py:462
  42.6 14.0 %collective-permute-start.13 = (f32[560,128]{1,0:T(8,128)S(1)}, f32[560,128]{1,0:T(8,128)S(1)}, u32[]{:S(2)}, u32[]{:S(2)}) collective-permute-start(f32[560,128]{1,0:T(8,128)S(1)} %get-tuple-element.54), channel_id=1, source_target_pairs={{0,4},{4,8},{8,12},{12,16},{16,20},{20,24},{24,28},{28,0},{1,5},{5... | collective-permute-start | bytes 860168 | tf_op jit(solution)/shard_map/ppermute | solution.py:462
  42.7 15.2 %collective-permute-start.14 = (f32[560,128]{1,0:T(8,128)S(1)}, f32[560,128]{1,0:T(8,128)S(1)}, u32[]{:S(2)}, u32[]{:S(2)}) collective-permute-start(f32[560,128]{1,0:T(8,128)S(1)} %get-tuple-element.55), channel_id=1, source_target_pairs={{0,28},{4,0},{8,4},{12,8},{16,12},{20,16},{24,20},{28,24},{1,29},{... | collective-permute-start | bytes 860168 | tf_op jit(solution)/shard_map/ppermute | solution.py:462
  45.9 10.7 %collective-permute-start.12 = (f32[256,128]{1,0:T(8,128)}, f32[256,128]{1,0:T(8,128)S(1)}, u32[]{:S(2)}, u32[]{:S(2)}) collective-permute-start(f32[256,128]{1,0:T(8,128)} %bitcast.6), channel_id=1, source_target_pairs={{0,32},{32,64},{64,96},{96,128},{128,160},{160,192},{192,224},{224... | collective-permute-start | bytes 393224 | tf_op jit(solution)/shard_map/ppermute | solution.py:462
  45.9 26.3 %collective-permute-start.10 = (f32[584,128]{1,0:T(8,128)S(1)}, f32[584,128]{1,0:T(8,128)S(1)}, u32[]{:S(2)}, u32[]{:S(2)}) collective-permute-start(f32[584,128]{1,0:T(8,128)S(1)} %get-tuple-element.47), channel_id=1, source_target_pairs={{0,96},{32,128},{64,160},{96,192},{128,224},{160,0},{192,32},{224,... | collective-permute-start | bytes 897032 | tf_op jit(solution)/shard_map/ppermute | solution.py:462
  46.2 26.9 %collective-permute-start.9 = (f32[792,128]{1,0:T(8,128)S(1)}, f32[792,128]{1,0:T(8,128)S(1)}, u32[]{:S(2)}, u32[]{:S(2)}) collective-permute-start(f32[792,128]{1,0:T(8,128)S(1)} %get-tuple-element.45.refs_7_), channel_id=1, source_target_pairs={{0,128},{32,160},{64,192},{96,224},{128,0},{160,32},{192,64},{224,... | collective-permute-start | bytes 1216520 | tf_op jit(solution)/shard_map/ppermute | solution.py:462
  56.7 14.4 %collective-permute-start.11 = (f32[408,128]{1,0:T(8,128)S(1)}, f32[408,128]{1,0:T(8,128)S(1)}, u32[]{:S(2)}, u32[]{:S(2)}) collective-permute-start(f32[408,128]{1,0:T(8,128)S(1)} %get-tuple-element.50), channel_id=1, source_target_pairs={{0,64},{32,96},{64,128},{96,160},{128,192},{160,224},{192,0},{224,... | collective-permute-start | bytes 626696 | tf_op jit(solution)/shard_map/ppermute | solution.py:462
  56.7 16.4 %collective-permute-start.15 = (f32[560,128]{1,0:T(8,128)S(1)}, f32[560,128]{1,0:T(8,128)S(1)}, u32[]{:S(2)}, u32[]{:S(2)}) collective-permute-start(f32[560,128]{1,0:T(8,128)S(1)} %get-tuple-element.56), channel_id=1, source_target_pairs={{0,1},{1,2},{2,3},{3,0},{4,5},{5,6},{6,7},{7,4},{8,9},{9,10},{10,1... | collective-permute-start | bytes 860168 | tf_op jit(solution)/shard_map/ppermute | solution.py:462
  57.9 15.2 %collective-permute-start.16 = (f32[560,128]{1,0:T(8,128)S(1)}, f32[560,128]{1,0:T(8,128)S(1)}, u32[]{:S(2)}, u32[]{:S(2)}) collective-permute-start(f32[560,128]{1,0:T(8,128)S(1)} %get-tuple-element.57), channel_id=1, source_target_pairs={{0,3},{1,0},{2,1},{3,2},{4,7},{5,4},{6,5},{7,6},{8,11},{9,8},{10,9... | collective-permute-start | bytes 860168 | tf_op jit(solution)/shard_map/ppermute | solution.py:462
  71.1 5.1 %collective-permute-start.17 = (f32[272,128]{1,0:T(8,128)S(1)}, f32[272,128]{1,0:T(8,128)S(1)}, u32[]{:S(2)}, u32[]{:S(2)}) collective-permute-start(f32[272,128]{1,0:T(8,128)S(1)} %get-tuple-element.58), channel_id=1, source_target_pairs={{0,1},{1,2},{2,3},{3,0},{4,5},{5,6},{6,7},{7,4},{8,9},{9,10},{10,1... | collective-permute-start | bytes 417800 | tf_op jit(solution)/shard_map/ppermute | solution.py:462
  72.3 5.1 %collective-permute-start.18 = (f32[272,128]{1,0:T(8,128)S(1)}, f32[272,128]{1,0:T(8,128)S(1)}, u32[]{:S(2)}, u32[]{:S(2)}) collective-permute-start(f32[272,128]{1,0:T(8,128)S(1)} %get-tuple-element.59), channel_id=1, source_target_pairs={{0,3},{1,0},{2,1},{3,2},{4,7},{5,4},{6,5},{7,6},{8,11},{9,8},{10,9... | collective-permute-start | bytes 417800 | tf_op jit(solution)/shard_map/ppermute | solution.py:462
  95.3 17.6 %all-to-all-start = ((f32[32,1,128]{2,1,0:T(1,128)}), f32[32,1,128]{2,1,0:T(1,128)S(1)}, u32[]{:S(2)}, u32[]{:S(2)}) async-start(f32[32,1,128]{2,1,0:T(1,128)} %bitcast.8), calls=%async_computation | async-start | bytes 32768 | tf_op jit(solution)/shard_map/all_to_all | solution.py:544

commit v6 on v5

--- a/solution.py
+++ b/solution.py
@@ -463,8 +463,10 @@
 
 
 def swap_sides(slabs):
-    xhi, xlo, yhi, ylo = slabs
-    return shift(xhi, "gx", 1), shift(xlo, "gx", -1), shift(yhi, "gy", 1), shift(ylo, "gy", -1)
+    received = []
+    for slab, axis, by in zip(slabs, ("gx", "gx", "gy", "gy"), (1, -1, 1, -1)):
+        received.append(shift(slab, axis, by))
+    return received
 
 
 def swap_corners(xlo, xhi, widths):

time: 114 us -> 114 us (level)
  no operation moved by 1% of the time
where the time goes in v6:
time: 114 us
  Pallas kernels  37.6 us (33%)
  waiting for transfers between devices  36.7 us (32%)
  starting transfers between devices  35.9 us (31%)
  other arithmetic  1.78 us (2%)
  between operations  1.42 us (1%)
    pallas_call x8, Pallas kernels, call(): pl.pallas_call(kernel, out_shape=shapes, in_specs=[SMEM] * smem + [VMEM]...  37.6 us
    ppermute x19, waiting for transfers between devices, shift(): return lax.ppermute(x, axis, [(i, (i + by) % n) for i in range(n)])  28.1 us
    ppermute x19, starting transfers between devices, shift(): return lax.ppermute(x, axis, [(i, (i + by) % n) for i in range(n)])  26.8 us
    all_to_all x1, starting transfers between devices, on_device(): parts = lax.all_to_all(parts, ('gx', 'gy'), 0, 0, tiled=True)  9.03 us
    all_to_all x1, waiting for transfers between devices, on_device(): parts = lax.all_to_all(parts, ('gx', 'gy'), 0, 0, tiled=True)  8.54 us
  transfers between devices with their start and end apart: 20, of which 9 were waited for; matrix products, arithmetic and copies ran while one was open for 0% of the time, Pallas kernels for 11%

profile of v6, /device:TPU:2, one launch (start us, length us, event | category | flops | bytes accessed | tf_op | source)
XLA Modules:
  0.0 113.5 jit_solution(891519392674135619)
XLA Ops:
  0.6 0.0 copy-start
  0.6 1.1 pad_add_fusion.masks
  1.7 1.0 shard_map.85
  2.7 2.0 %collective-permute-start = (f32[480,128]{1,0:T(8,128)S(1)}, f32[480,128]{1,0:T(8,128)S(1)}, u32[]{:S(2)}, u32[]{:S(2)}) collective-permute-start(f32[480,128]{1,0:T(8,128)S(1)} %get-tuple-element.34), channel_id=1, source_target_pairs={{0,4},{4,8},{8,12},{12,16},{16,20},{20,24},{24,28},{28,0},{1,5},{5... | collective-permute-start | bytes 737288 | tf_op jit(solution)/shard_map/ppermute | solution.py:462
  4.7 4.0 %collective-permute-start.1 = (f32[480,128]{1,0:T(8,128)S(1)}, f32[480,128]{1,0:T(8,128)S(1)}, u32[]{:S(2)}, u32[]{:S(2)}) collective-permute-start(f32[480,128]{1,0:T(8,128)S(1)} %get-tuple-element.35), channel_id=1, source_target_pairs={{0,28},{4,0},{8,4},{12,8},{16,12},{20,16},{24,20},{28,24},{1,29},{... | collective-permute-start | bytes 737288 | tf_op jit(solution)/shard_map/ppermute | solution.py:462
  8.7 1.5 %collective-permute-start.2 = (f32[480,128]{1,0:T(8,128)S(1)}, f32[480,128]{1,0:T(8,128)S(1)}, u32[]{:S(2)}, u32[]{:S(2)}) collective-permute-start(f32[480,128]{1,0:T(8,128)S(1)} %get-tuple-element.36), channel_id=1, source_target_pairs={{0,1},{1,2},{2,3},{3,0},{4,5},{5,6},{6,7},{7,4},{8,9},{9,10},{10,1... | collective-permute-start | bytes 737288 | tf_op jit(solution)/shard_map/ppermute | solution.py:462
  10.2 0.5 collective-permute-start.3
  10.8 1.8 %collective-permute-start.8 = (f32[256,128]{1,0:T(8,128)}, f32[256,128]{1,0:T(8,128)S(1)}, u32[]{:S(2)}, u32[]{:S(2)}) collective-permute-start(f32[256,128]{1,0:T(8,128)} %bitcast.6), channel_id=1, source_target_pairs={{0,160},{32,192},{64,224},{96,0},{128,32},{160,64},{192,96},{224,1... | collective-permute-start | bytes 393224 | tf_op jit(solution)/shard_map/ppermute | solution.py:462
  13.2 0.2 dynamic-slice_reduce_fusion.1.vector
  13.4 1.2 %collective-permute-done.xlo = f32[480,128]{1,0:T(8,128)S(1)} collective-permute-done((f32[480,128]{1,0:T(8,128)S(1)}, f32[480,128]{1,0:T(8,128)S(1)}, u32[]{:S(2)}, u32[]{:S(2)}) %collective-permute-start) | collective-permute-done | bytes 245792 | tf_op jit(solution)/shard_map/ppermute | solution.py:462
  14.6 0.0 collective-permute-done.1.xhi
  14.6 1.6 %collective-permute-start.4 = (f32[200,128]{1,0:T(8,128)S(1)}, f32[200,128]{1,0:T(8,128)S(1)}, u32[]{:S(2)}, u32[]{:S(2)}) collective-permute-start(f32[200,128]{1,0:T(8,128)S(1)} %get-tuple-element.38), channel_id=1, source_target_pairs={{0,1},{1,2},{2,3},{3,0},{4,5},{5,6},{6,7},{7,4},{8,9},{9,10},{10,1... | collective-permute-start | bytes 307208 | tf_op jit(solution)/shard_map/ppermute | solution.py:462
  16.2 0.5 collective-permute-start.5
  16.7 0.1 pad_add_fusion.1.place.refs_0_
  16.8 0.0 collective-permute-done.2.ylo
  16.8 0.5 collective-permute-done.3.yhi
  17.4 2.3 %collective-permute-done.4.clo = f32[200,128]{1,0:T(8,128)S(1)} collective-permute-done((f32[200,128]{1,0:T(8,128)S(1)}, f32[200,128]{1,0:T(8,128)S(1)}, u32[]{:S(2)}, u32[]{:S(2)}) %collective-permute-start.4) | collective-permute-done | bytes 102432 | tf_op jit(solution)/shard_map/ppermute | solution.py:462
  19.7 1.2 %collective-permute-done.5.chi = f32[200,128]{1,0:T(8,128)S(1)} collective-permute-done((f32[200,128]{1,0:T(8,128)S(1)}, f32[200,128]{1,0:T(8,128)S(1)}, u32[]{:S(2)}, u32[]{:S(2)}) %collective-permute-start.5) | collective-permute-done | bytes 102432 | tf_op jit(solution)/shard_map/ppermute | solution.py:462
  20.9 1.4 %shard_map.87 = (f32[12,1224,128]{2,1,0:T(8,128)S(1)}, f32[1224,128]{1,0:T(8,128)S(1)}, f32[1224,128]{1,0:T(8,128)S(1)}, f32[1224,128]{1,0:T(8,128)S(1)}, f32[12...) custom-call(s32[4]{0:T(128)S(1)} %pad_add_fusion.1.place.refs_0_, ...), custom_call_target="tpu_custom_call" | custom-call | flops 1900000000 | bytes 1900000 | tf_op jit(solution)/shard_map/pallas_call | solution.py:446
  22.3 0.8 collective-permute-start.6
  23.1 2.4 %collective-permute-start.7 = (f32[408,128]{1,0:T(8,128)S(1)}, f32[408,128]{1,0:T(8,128)S(1)}, u32[]{:S(2)}, u32[]{:S(2)}) collective-permute-start(f32[408,128]{1,0:T(8,128)S(1)} %get-tuple-element.50), channel_id=1, source_target_pairs={{0,192},{32,224},{64,0},{96,32},{128,64},{160,96},{192,128},{224,1... | collective-permute-start | bytes 626696 | tf_op jit(solution)/shard_map/ppermute | solution.py:462
  25.4 5.9 %shard_map.88 = (f32[12,1224,128]{2,1,0:T(8,128)S(1)}, f32[1,128]{1,0:T(1,128)S(1)}) custom-call(s32[4]{0:T(128)S(1)} %pad_add_fusion.1.place.refs_0_, f32[12,1224,128]{2,1,0:T(8,128)S(1)} %get-tuple-element.40.refs_1_.refs_8_, f32[1224,128]{1,0:T(8,128)S(1)} %get-tuple-element.41.refs_2_, f32[1224,128]{1,0:T(8,128)S(1)} %get-tuple-element.42.refs_3_, ...), custom_call_target="tpu_custom_call" | custom-call | flops 5488000000 | bytes 5488000 | tf_op jit(solution)/shard_map/pallas_call | solution.py:446
  31.4 0.0 collective-permute-done.6.refs_7_
  31.4 4.8 %shard_map.89 = (f32[12,1224,128]{2,1,0:T(8,128)S(1)}, f32[1,128]{1,0:T(1,128)S(1)}) custom-call(s32[4]{0:T(128)S(1)} %pad_add_fusion.1.place.refs_0_, f32[12,1224,128]{2,1,0:T(8,128)S(1)} %get-tuple-element.40.refs_1_.refs_8_, f32[1224,128]{1,0:T(8,128)S(1)} %get-tuple-element.41.refs_2_, f32[1224,128]{1,0:T(8,128)S(1)} %get-tuple-element.42.refs_3_, ...), custom_call_target="tpu_custom_call" | custom-call | flops 4032000000 | bytes 4032000 | tf_op jit(solution)/shard_map/pallas_call | solution.py:446
  36.3 0.0 collective-permute-done.8.refs_8_
  36.3 6.3 %shard_map.90 = (f32[4,16,16,128]{3,2,1,0:T(8,128)S(1)}, f32[560,128]{1,0:T(8,128)S(1)}, f32[560,128]{1,0:T(8,128)S(1)}, f32[560,128]{1,0:T(8,128)S(1)}, f32[560,128]{1,0:T(8,128)S(1)}, /*index=5*/f32[1,128]{1,0:T(1,128)S(1)}) custom-call(s32[4]{0:T(128)S(1)} %pad_add_fusion.1.place.refs_0_, f32[12,1224,128]{2,1,0:T(8,128)S(1)} %get-tuple-element.40.refs_1_.refs_8_, ...), custom_call_target="tpu_custom_call" | custom-call | flops 4592000000 | bytes 4592000 | tf_op jit(solution)/shard_map/pallas_call | solution.py:446
  42.6 0.1 collective-permute-start.13
  42.7 3.2 %collective-permute-start.14 = (f32[560,128]{1,0:T(8,128)S(1)}, f32[560,128]{1,0:T(8,128)S(1)}, u32[]{:S(2)}, u32[]{:S(2)}) collective-permute-start(f32[560,128]{1,0:T(8,128)S(1)} %get-tuple-element.55), channel_id=1, source_target_pairs={{0,28},{4,0},{8,4},{12,8},{16,12},{20,16},{24,20},{28,24},{1,29},{... | collective-permute-start | bytes 860168 | tf_op jit(solution)/shard_map/ppermute | solution.py:462
  45.9 0.3 collective-permute-start.10
  46.2 4.1 %collective-permute-start.9 = (f32[792,128]{1,0:T(8,128)S(1)}, f32[792,128]{1,0:T(8,128)S(1)}, u32[]{:S(2)}, u32[]{:S(2)}) collective-permute-start(f32[792,128]{1,0:T(8,128)S(1)} %get-tuple-element.45.refs_7_), channel_id=1, source_target_pairs={{0,128},{32,160},{64,192},{96,224},{128,0},{160,32},{192,64},{224,... | collective-permute-start | bytes 1216520 | tf_op jit(solution)/shard_map/ppermute | solution.py:462
  50.3 6.3 %collective-permute-done.12.refs_10_ = f32[256,128]{1,0:T(8,128)S(1)} collective-permute-done((f32[256,128]{1,0:T(8,128)}, f32[256,128]{1,0:T(8,128)S(1)}, u32[]{:S(2)}, u32[]{:S(2)}) %collective-permute-start.12) | collective-permute-done | bytes 131104 | tf_op jit(solution)/shard_map/ppermute | solution.py:462
  56.7 0.0 collective-permute-start.11
  56.7 1.2 %collective-permute-start.15 = (f32[560,128]{1,0:T(8,128)S(1)}, f32[560,128]{1,0:T(8,128)S(1)}, u32[]{:S(2)}, u32[]{:S(2)}) collective-permute-start(f32[560,128]{1,0:T(8,128)S(1)} %get-tuple-element.56), channel_id=1, source_target_pairs={{0,1},{1,2},{2,3},{3,0},{4,5},{5,6},{6,7},{7,4},{8,9},{9,10},{10,1... | collective-permute-start | bytes 860168 | tf_op jit(solution)/shard_map/ppermute | solution.py:462
  57.9 0.0 collective-permute-done.14.xhi.refs_13_
  57.9 0.8 collective-permute-start.16
  58.7 12.3 %collective-permute-done.11.refs_9_ = f32[408,128]{1,0:T(8,128)S(1)} collective-permute-done((f32[408,128]{1,0:T(8,128)S(1)}, f32[408,128]{1,0:T(8,128)S(1)}, u32[]{:S(2)}, u32[]{:S(2)}) %collective-permute-start.11) | collective-permute-done | bytes 208928 | tf_op jit(solution)/shard_map/ppermute | solution.py:462
  71.1 1.2 %collective-permute-start.17 = (f32[272,128]{1,0:T(8,128)S(1)}, f32[272,128]{1,0:T(8,128)S(1)}, u32[]{:S(2)}, u32[]{:S(2)}) collective-permute-start(f32[272,128]{1,0:T(8,128)S(1)} %get-tuple-element.58), channel_id=1, source_target_pairs={{0,1},{1,2},{2,3},{3,0},{4,5},{5,6},{6,7},{7,4},{8,9},{9,10},{10,1... | collective-permute-start | bytes 417800 | tf_op jit(solution)/shard_map/ppermute | solution.py:462
  72.3 0.8 collective-permute-start.18
  73.1 0.0 collective-permute-done.9.refs_7_
  73.1 0.0 collective-permute-done.15.refs_14_
  73.1 0.0 collective-permute-done.16.refs_15_
  73.1 3.0 %collective-permute-done.17.refs_16_ = f32[272,128]{1,0:T(8,128)S(1)} collective-permute-done((f32[272,128]{1,0:T(8,128)S(1)}, f32[272,128]{1,0:T(8,128)S(1)}, u32[]{:S(2)}, u32[]{:S(2)}) %collective-permute-start.17) | collective-permute-done | bytes 139296 | tf_op jit(solution)/shard_map/ppermute | solution.py:462
  76.1 1.2 %collective-permute-done.18.refs_17_ = f32[272,128]{1,0:T(8,128)S(1)} collective-permute-done((f32[272,128]{1,0:T(8,128)S(1)}, f32[272,128]{1,0:T(8,128)S(1)}, u32[]{:S(2)}, u32[]{:S(2)}) %collective-permute-start.18) | collective-permute-done | bytes 139296 | tf_op jit(solution)/shard_map/ppermute | solution.py:462
  77.3 18.0 %shard_map.92 = (f32[1,3,16,16,128]{4,3,2,1,0:T(8,128)}, f32[1,16,16,128]{3,2,1,0:T(8,128)}, f32[32,128]{1,0:T(8,128)}) custom-call(s32[4]{0:T(128)S(1)} %pad_add_fusion.1.place.refs_0_, f32[12,1224,128]{2,1,0:T(8,128)S(1)} %get-tuple-element.40.refs_1_.refs_8_, f32[1224,128]{1,0:T(8,128)S(1)} %get-tuple-element.41.refs_2_, ...), custom_call_target="tpu_custom_call" | custom-call | flops 14112000000 | bytes 14112000 | tf_op jit(solution)/shard_map/pallas_call | solution.py:446
  95.3 9.0 %all-to-all-start = ((f32[32,1,128]{2,1,0:T(1,128)}), f32[32,1,128]{2,1,0:T(1,128)S(1)}, u32[]{:S(2)}, u32[]{:S(2)}) async-start(f32[32,1,128]{2,1,0:T(1,128)} %bitcast.8), calls=%async_computation | async-start | bytes 32768 | tf_op jit(solution)/shard_map/all_to_all | solution.py:546
  104.4 8.5 %all-to-all-done = f32[32,1,128]{2,1,0:T(1,128)S(1)} async-done(((f32[32,1,128]{2,1,0:T(1,128)}), f32[32,1,128]{2,1,0:T(1,128)S(1)}, u32[]{:S(2)}, u32[]{:S(2)}) %all-to-all-start) | async-done | bytes 16416 | tf_op jit(solution)/shard_map/all_to_all | solution.py:546
  112.9 0.1 dynamic-slice_reduce_fusion
  113.0 0.5 sqrt_bitcast_fusion
  (8 shorter events, 0.1 us)
Async XLA Ops:
  0.6 12.6 %copy-start = (f32[64,3]{0,1:T(4,128)S(1)}, f32[64,3]{0,1:T(4,128)}, u32[]{:S(2)}) copy-start(f32[64,3]{0,1:T(4,128)} %param.7) | copy-start | bytes 2308
  2.7 11.9 %collective-permute-start = (f32[480,128]{1,0:T(8,128)S(1)}, f32[480,128]{1,0:T(8,128)S(1)}, u32[]{:S(2)}, u32[]{:S(2)}) collective-permute-start(f32[480,128]{1,0:T(8,128)S(1)} %get-tuple-element.34), channel_id=1, source_target_pairs={{0,4},{4,8},{8,12},{12,16},{16,20},{20,24},{24,28},{28,0},{1,5},{5... | collective-permute-start | bytes 737288 | tf_op jit(solution)/shard_map/ppermute | solution.py:462
  4.7 9.9 %collective-permute-start.1 = (f32[480,128]{1,0:T(8,128)S(1)}, f32[480,128]{1,0:T(8,128)S(1)}, u32[]{:S(2)}, u32[]{:S(2)}) collective-permute-start(f32[480,128]{1,0:T(8,128)S(1)} %get-tuple-element.35), channel_id=1, source_target_pairs={{0,28},{4,0},{8,4},{12,8},{16,12},{20,16},{24,20},{28,24},{1,29},{... | collective-permute-start | bytes 737288 | tf_op jit(solution)/shard_map/ppermute | solution.py:462
  8.7 8.1 %collective-permute-start.2 = (f32[480,128]{1,0:T(8,128)S(1)}, f32[480,128]{1,0:T(8,128)S(1)}, u32[]{:S(2)}, u32[]{:S(2)}) collective-permute-start(f32[480,128]{1,0:T(8,128)S(1)} %get-tuple-element.36), channel_id=1, source_target_pairs={{0,1},{1,2},{2,3},{3,0},{4,5},{5,6},{6,7},{7,4},{8,9},{9,10},{10,1... | collective-permute-start | bytes 737288 | tf_op jit(solution)/shard_map/ppermute | solution.py:462
  10.2 7.1 %collective-permute-start.3 = (f32[480,128]{1,0:T(8,128)S(1)}, f32[480,128]{1,0:T(8,128)S(1)}, u32[]{:S(2)}, u32[]{:S(2)}) collective-permute-start(f32[480,128]{1,0:T(8,128)S(1)} %get-tuple-element.37), channel_id=1, source_target_pairs={{0,3},{1,0},{2,1},{3,2},{4,7},{5,4},{6,5},{7,6},{8,11},{9,8},{10,9... | collective-permute-start | bytes 737288 | tf_op jit(solution)/shard_map/ppermute | solution.py:462
  10.8 25.5 %collective-permute-start.8 = (f32[256,128]{1,0:T(8,128)}, f32[256,128]{1,0:T(8,128)S(1)}, u32[]{:S(2)}, u32[]{:S(2)}) collective-permute-start(f32[256,128]{1,0:T(8,128)} %bitcast.6), channel_id=1, source_target_pairs={{0,160},{32,192},{64,224},{96,0},{128,32},{160,64},{192,96},{224,1... | collective-permute-start | bytes 393224 | tf_op jit(solution)/shard_map/ppermute | solution.py:462
  14.6 5.0 %collective-permute-start.4 = (f32[200,128]{1,0:T(8,128)S(1)}, f32[200,128]{1,0:T(8,128)S(1)}, u32[]{:S(2)}, u32[]{:S(2)}) collective-permute-start(f32[200,128]{1,0:T(8,128)S(1)} %get-tuple-element.38), channel_id=1, source_target_pairs={{0,1},{1,2},{2,3},{3,0},{4,5},{5,6},{6,7},{7,4},{8,9},{9,10},{10,1... | collective-permute-start | bytes 307208 | tf_op jit(solution)/shard_map/ppermute | solution.py:462
  16.2 4.7 %collective-permute-start.5 = (f32[200,128]{1,0:T(8,128)S(1)}, f32[200,128]{1,0:T(8,128)S(1)}, u32[]{:S(2)}, u32[]{:S(2)}) collective-permute-start(f32[200,128]{1,0:T(8,128)S(1)} %get-tuple-element.39), channel_id=1, source_target_pairs={{0,3},{1,0},{2,1},{3,2},{4,7},{5,4},{6,5},{7,6},{8,11},{9,8},{10,9... | collective-permute-start | bytes 307208 | tf_op jit(solution)/shard_map/ppermute | solution.py:462
  22.3 9.1 %collective-permute-start.6 = (f32[584,128]{1,0:T(8,128)S(1)}, f32[584,128]{1,0:T(8,128)S(1)}, u32[]{:S(2)}, u32[]{:S(2)}) collective-permute-start(f32[584,128]{1,0:T(8,128)S(1)} %get-tuple-element.47), channel_id=1, source_target_pairs={{0,224},{32,0},{64,32},{96,64},{128,96},{160,128},{192,160},{224,1... | collective-permute-start | bytes 897032 | tf_op jit(solution)/shard_map/ppermute | solution.py:462
  23.1 13.2 %collective-permute-start.7 = (f32[408,128]{1,0:T(8,128)S(1)}, f32[408,128]{1,0:T(8,128)S(1)}, u32[]{:S(2)}, u32[]{:S(2)}) collective-permute-start(f32[408,128]{1,0:T(8,128)S(1)} %get-tuple-element.50), channel_id=1, source_target_pairs={{0,192},{32,224},{64,0},{96,32},{128,64},{160,96},{192,128},{224,1... | collective-permute-start | bytes 626696 | tf_op jit(solution)/shard_map/ppermute | solution.py:462
  42.6 14.0 %collective-permute-start.13 = (f32[560,128]{1,0:T(8,128)S(1)}, f32[560,128]{1,0:T(8,128)S(1)}, u32[]{:S(2)}, u32[]{:S(2)}) collective-permute-start(f32[560,128]{1,0:T(8,128)S(1)} %get-tuple-element.54), channel_id=1, source_target_pairs={{0,4},{4,8},{8,12},{12,16},{16,20},{20,24},{24,28},{28,0},{1,5},{5... | collective-permute-start | bytes 860168 | tf_op jit(solution)/shard_map/ppermute | solution.py:462
  42.7 15.2 %collective-permute-start.14 = (f32[560,128]{1,0:T(8,128)S(1)}, f32[560,128]{1,0:T(8,128)S(1)}, u32[]{:S(2)}, u32[]{:S(2)}) collective-permute-start(f32[560,128]{1,0:T(8,128)S(1)} %get-tuple-element.55), channel_id=1, source_target_pairs={{0,28},{4,0},{8,4},{12,8},{16,12},{20,16},{24,20},{28,24},{1,29},{... | collective-permute-start | bytes 860168 | tf_op jit(solution)/shard_map/ppermute | solution.py:462
  45.9 10.7 %collective-permute-start.12 = (f32[256,128]{1,0:T(8,128)}, f32[256,128]{1,0:T(8,128)S(1)}, u32[]{:S(2)}, u32[]{:S(2)}) collective-permute-start(f32[256,128]{1,0:T(8,128)} %bitcast.6), channel_id=1, source_target_pairs={{0,32},{32,64},{64,96},{96,128},{128,160},{160,192},{192,224},{224... | collective-permute-start | bytes 393224 | tf_op jit(solution)/shard_map/ppermute | solution.py:462
  45.9 26.3 %collective-permute-start.10 = (f32[584,128]{1,0:T(8,128)S(1)}, f32[584,128]{1,0:T(8,128)S(1)}, u32[]{:S(2)}, u32[]{:S(2)}) collective-permute-start(f32[584,128]{1,0:T(8,128)S(1)} %get-tuple-element.47), channel_id=1, source_target_pairs={{0,96},{32,128},{64,160},{96,192},{128,224},{160,0},{192,32},{224,... | collective-permute-start | bytes 897032 | tf_op jit(solution)/shard_map/ppermute | solution.py:462
  46.2 26.9 %collective-permute-start.9 = (f32[792,128]{1,0:T(8,128)S(1)}, f32[792,128]{1,0:T(8,128)S(1)}, u32[]{:S(2)}, u32[]{:S(2)}) collective-permute-start(f32[792,128]{1,0:T(8,128)S(1)} %get-tuple-element.45.refs_7_), channel_id=1, source_target_pairs={{0,128},{32,160},{64,192},{96,224},{128,0},{160,32},{192,64},{224,... | collective-permute-start | bytes 1216520 | tf_op jit(solution)/shard_map/ppermute | solution.py:462
  56.7 14.4 %collective-permute-start.11 = (f32[408,128]{1,0:T(8,128)S(1)}, f32[408,128]{1,0:T(8,128)S(1)}, u32[]{:S(2)}, u32[]{:S(2)}) collective-permute-start(f32[408,128]{1,0:T(8,128)S(1)} %get-tuple-element.50), channel_id=1, source_target_pairs={{0,64},{32,96},{64,128},{96,160},{128,192},{160,224},{192,0},{224,... | collective-permute-start | bytes 626696 | tf_op jit(solution)/shard_map/ppermute | solution.py:462
  56.7 16.4 %collective-permute-start.15 = (f32[560,128]{1,0:T(8,128)S(1)}, f32[560,128]{1,0:T(8,128)S(1)}, u32[]{:S(2)}, u32[]{:S(2)}) collective-permute-start(f32[560,128]{1,0:T(8,128)S(1)} %get-tuple-element.56), channel_id=1, source_target_pairs={{0,1},{1,2},{2,3},{3,0},{4,5},{5,6},{6,7},{7,4},{8,9},{9,10},{10,1... | collective-permute-start | bytes 860168 | tf_op jit(solution)/shard_map/ppermute | solution.py:462
  57.9 15.2 %collective-permute-start.16 = (f32[560,128]{1,0:T(8,128)S(1)}, f32[560,128]{1,0:T(8,128)S(1)}, u32[]{:S(2)}, u32[]{:S(2)}) collective-permute-start(f32[560,128]{1,0:T(8,128)S(1)} %get-tuple-element.57), channel_id=1, source_target_pairs={{0,3},{1,0},{2,1},{3,2},{4,7},{5,4},{6,5},{7,6},{8,11},{9,8},{10,9... | collective-permute-start | bytes 860168 | tf_op jit(solution)/shard_map/ppermute | solution.py:462
  71.1 5.1 %collective-permute-start.17 = (f32[272,128]{1,0:T(8,128)S(1)}, f32[272,128]{1,0:T(8,128)S(1)}, u32[]{:S(2)}, u32[]{:S(2)}) collective-permute-start(f32[272,128]{1,0:T(8,128)S(1)} %get-tuple-element.58), channel_id=1, source_target_pairs={{0,1},{1,2},{2,3},{3,0},{4,5},{5,6},{6,7},{7,4},{8,9},{9,10},{10,1... | collective-permute-start | bytes 417800 | tf_op jit(solution)/shard_map/ppermute | solution.py:462
  72.3 5.1 %collective-permute-start.18 = (f32[272,128]{1,0:T(8,128)S(1)}, f32[272,128]{1,0:T(8,128)S(1)}, u32[]{:S(2)}, u32[]{:S(2)}) collective-permute-start(f32[272,128]{1,0:T(8,128)S(1)} %get-tuple-element.59), channel_id=1, source_target_pairs={{0,3},{1,0},{2,1},{3,2},{4,7},{5,4},{6,5},{7,6},{8,11},{9,8},{10,9... | collective-permute-start | bytes 417800 | tf_op jit(solution)/shard_map/ppermute | solution.py:462
  95.3 17.6 %all-to-all-start = ((f32[32,1,128]{2,1,0:T(1,128)}), f32[32,1,128]{2,1,0:T(1,128)S(1)}, u32[]{:S(2)}, u32[]{:S(2)}) async-start(f32[32,1,128]{2,1,0:T(1,128)} %bitcast.8), calls=%async_computation | async-start | bytes 32768 | tf_op jit(solution)/shard_map/all_to_all | solution.py:546
